TPU v7x, 32 devices: a whole 2x2x4 slice. The times are simulated.
32 devices in a mesh: dp: 16 (over z, y, x), seq: 2 (over core).
Axes of the slice: x: 2, y: 2, z: 4, core: 2. Of those that a mesh axis runs over, the one named last changes fastest.
Arguments:
- content: bfloat16 [32, 512, 768], P('dp', 'seq'), may hold values from -6 to 6
- query_in: bfloat16 [32, 512, 768], P('dp', 'seq'), may hold values from -6 to 6
- content_cot: bfloat16 [32, 512, 768], P('dp', 'seq'), may hold values from -6 to 6
- query_cot: bfloat16 [32, 512, 768], P('dp', 'seq'), may hold values from -6 to 6
- lengths: int32 [32, 8], P('dp'), may hold values from 1 to 256, 512 in all within a row
- order: int32 [32, 512], P('dp'), may hold values from 0 to 511, each once within a row
- query_weight: bfloat16 [768, 768], P('dp'), may hold values from -0.21875 to 0.21875
- query_bias: bfloat16 [768], P('dp'), may hold values from -3 to 3
- key_weight: bfloat16 [768, 768], P('dp'), may hold values from -0.21875 to 0.21875
- value_weight: bfloat16 [768, 768], P('dp'), may hold values from -0.21875 to 0.21875
- value_bias: bfloat16 [768], P('dp'), may hold values from -3 to 3
- out_weight: bfloat16 [768, 768], P('dp'), may hold values from -0.875 to 0.875
- out_bias: bfloat16 [768], P('dp'), may hold values from -3 to 3
- mixer_gain: bfloat16 [768], P('dp'), may hold values from 0.5 to 1.5
- mixer_shift: bfloat16 [768], P('dp'), may hold values from -3 to 3
- up_weight: bfloat16 [768, 3072], P(None, 'dp'), may hold values from -0.21875 to 0.21875
- up_bias: bfloat16 [3072], P('dp'), may hold values from -3 to 3
- down_weight: bfloat16 [3072, 768], P('dp'), may hold values from -0.109375 to 0.109375
- down_bias: bfloat16 [768], P('dp'), may hold values from -3 to 3
- final_gain: bfloat16 [768], P('dp'), may hold values from 0.5 to 1.5
- final_shift: bfloat16 [768], P('dp'), may hold values from -3 to 3
- position_bias: bfloat16 [384], P('dp'), may hold values from -4 to 4
Outputs:
- content_out: bfloat16 [32, 512, 768], P('dp', 'seq')
- query_out: bfloat16 [32, 512, 768], P('dp', 'seq')
- content_grad: bfloat16 [32, 512, 768], P('dp', 'seq')
- query_grad: bfloat16 [32, 512, 768], P('dp', 'seq')
- query_weight_grad: float32 [768, 768], P('dp')
- query_bias_grad: float32 [768], P('dp')
- key_weight_grad: float32 [768, 768], P('dp')
- value_weight_grad: float32 [768, 768], P('dp')
- value_bias_grad: float32 [768], P('dp')
- out_weight_grad: float32 [768, 768], P('dp')
- out_bias_grad: float32 [768], P('dp')
- mixer_gain_grad: float32 [768], P('dp')
- mixer_shift_grad: float32 [768], P('dp')
- up_weight_grad: float32 [768, 3072], P(None, 'dp')
- up_bias_grad: float32 [3072], P('dp')
- down_weight_grad: float32 [3072, 768], P('dp')
- down_bias_grad: float32 [768], P('dp')
- final_gain_grad: float32 [768], P('dp')
- final_shift_grad: float32 [768], P('dp')
- position_bias_grad: float32 [384], P('dp')
Inputs may be any that keep to these rules, and one draw needn't show every extreme that they name: Each row of order holds every position 0 to 511 once. Each row of lengths sums to 512, and its largest entry is 256.
All inputs are finite; a program needn't handle non-finite values.
Results may differ from a plain program's by a relative error of at most 0.013.
Values may be sent and summed in bfloat16 or wider, within the bound.
No kernel may reach another device: no remote copies, remote signals or barrier semaphores. Data moves between devices by JAX's collectives and lax.ppermute only.
A program may use at most 256 MiB of HBM per device.

v0:
```python
import math

import jax
import jax.numpy as jnp
from jax import lax
from jax.sharding import PartitionSpec as P

HEADS = 12
HEAD_DIM = 64
BUCKETS = 32
MICRO = 2


limits = (1, 2, 3, 4, 5, 6, 7, 8, 12, 16, 23, 32, 46, 64, 91)


def layer_norm(values, gain, shift):
    center = values - jnp.mean(values, axis=-1, keepdims=True)
    spread = jnp.mean(center * center, axis=-1, keepdims=True)
    return center * lax.rsqrt(spread + 1e-05) * gain + shift


def gelu_exact(values):
    return jax.nn.gelu(values, approximate=False)


def bucket_table(query_places, key_places):
    distance = key_places[None, :] - query_places[:, None]
    magnitude = jnp.abs(distance)
    counted = jnp.zeros(distance.shape, jnp.int32)
    for limit in limits:
        counted = counted + (magnitude >= limit).astype(jnp.int32)
    return counted + 16 * (distance > 0).astype(jnp.int32)


def matmul(left, right):
    return jnp.dot(left, right, preferred_element_type=jnp.float32)


def left_product(left, right):
    return lax.dot_general(
        left, right, (((0,), (0,)), ((), ())), preferred_element_type=jnp.float32
    )


def right_product(left, right):
    return lax.dot_general(
        left, right, (((1,), (1,)), ((), ())), preferred_element_type=jnp.float32
    )


def add_trees(total, extra):
    return jax.tree.map(lambda left, right: left + right, total, extra)


def shards(
    content,
    query_in,
    content_cot,
    query_cot,
    lengths,
    order,
    query_weight,
    query_bias,
    key_weight,
    value_weight,
    value_bias,
    out_weight,
    out_bias,
    mixer_gain,
    mixer_shift,
    up_weight,
    up_bias,
    down_weight,
    down_bias,
    final_gain,
    final_shift,
    position_bias,
):
    rows_local, block, width = content.shape
    row_len = order.shape[1]
    micro_rows = rows_local // MICRO
    start = lax.axis_index("seq") * block
    scale = 1.0 / math.sqrt(HEAD_DIM)

    def row_context(order_row, lengths_row):
        bounds = jnp.cumsum(lengths_row)[:-1]
        segment = jnp.sum((order_row[:, None] >= bounds[None, :]).astype(jnp.int32), axis=1)
        query_places = lax.dynamic_slice_in_dim(order_row, start, block)
        query_segment = lax.dynamic_slice_in_dim(segment, start, block)
        index = start + jnp.arange(block)
        same = query_segment[:, None] == segment[None, :]
        places = jnp.arange(row_len)[None, :]
        allowed_content = same & (places <= index[:, None])
        allowed_query = same & (places < index[:, None])
        allowed = jnp.concatenate([allowed_content, allowed_query], axis=0)
        live = jnp.any(allowed, axis=-1).astype(jnp.float32)
        bucket = bucket_table(query_places, order_row)
        onehot = (bucket[None, :, :] == jnp.arange(BUCKETS)[:, None, None]).astype(jnp.bfloat16)
        return (allowed, live, onehot)

    def row_scores(order_row, lengths_row, row_queries, row_keys, table):
        allowed, live, onehot = row_context(order_row, lengths_row)
        bias = jnp.einsum("bcl,bh->hcl", onehot, table, preferred_element_type=jnp.float32)
        bias = jnp.concatenate([bias, bias], axis=1)
        scores = (
            jnp.einsum("qhd,khd->hqk", row_queries, row_keys, preferred_element_type=jnp.float32)
            * scale
            + bias
        )
        return (jnp.where(allowed[None], scores, -1e30), live, onehot)

    content_parts, query_parts, content_grads, query_grads = ([], [], [], [])
    totals = None
    for micro in range(MICRO):
        own = content[micro * micro_rows : (micro + 1) * micro_rows]
        other = query_in[micro * micro_rows : (micro + 1) * micro_rows]
        order_rows = order[micro * micro_rows : (micro + 1) * micro_rows]
        length_rows = lengths[micro * micro_rows : (micro + 1) * micro_rows]
        gathered = (
            lax.all_gather(query_weight, "dp", axis=0, tiled=True),
            lax.all_gather(query_bias, "dp", axis=0, tiled=True),
            lax.all_gather(key_weight, "dp", axis=0, tiled=True),
            lax.all_gather(value_weight, "dp", axis=0, tiled=True),
            lax.all_gather(value_bias, "dp", axis=0, tiled=True),
            lax.all_gather(out_weight, "dp", axis=0, tiled=True),
            lax.all_gather(out_bias, "dp", axis=0, tiled=True),
            lax.all_gather(mixer_gain, "dp", axis=0, tiled=True),
            lax.all_gather(mixer_shift, "dp", axis=0, tiled=True),
            lax.all_gather(up_weight, "dp", axis=1, tiled=True),
            lax.all_gather(up_bias, "dp", axis=0, tiled=True),
            lax.all_gather(down_weight, "dp", axis=0, tiled=True),
            lax.all_gather(down_bias, "dp", axis=0, tiled=True),
            lax.all_gather(final_gain, "dp", axis=0, tiled=True),
            lax.all_gather(final_shift, "dp", axis=0, tiled=True),
            lax.all_gather(position_bias, "dp", axis=0, tiled=True),
        )
        query_matrix, key_matrix, value_matrix = (gathered[0], gathered[2], gathered[3])
        output_matrix, up_matrix, down_matrix = (gathered[5], gathered[9], gathered[11])
        query_offset = gathered[1].astype(jnp.float32)
        value_offset = gathered[4].astype(jnp.float32)
        output_offset = gathered[6].astype(jnp.float32)
        mixer_scale = gathered[7].astype(jnp.float32)
        mixer_offset = gathered[8].astype(jnp.float32)
        up_offset = gathered[10].astype(jnp.float32)
        down_offset = gathered[12].astype(jnp.float32)
        final_scale = gathered[13].astype(jnp.float32)
        final_offset = gathered[14].astype(jnp.float32)
        table = gathered[15].reshape(BUCKETS, HEADS)
        stacked = jnp.concatenate([own, other], axis=1)
        flat = stacked.reshape(-1, width)
        own_flat = own.reshape(-1, width)
        queries = (matmul(flat, query_matrix) + query_offset).astype(jnp.bfloat16)
        keys_local = (
            matmul(own_flat, key_matrix).astype(jnp.bfloat16).reshape(micro_rows, block, width)
        )
        values_local = (
            (matmul(own_flat, value_matrix) + value_offset)
            .astype(jnp.bfloat16)
            .reshape(micro_rows, block, width)
        )
        keys_all, values_all = (
            lax.all_gather(keys_local, "seq", axis=1, tiled=True),
            lax.all_gather(values_local, "seq", axis=1, tiled=True),
        )
        queries_rows = queries.reshape(micro_rows, 2 * block, HEADS, HEAD_DIM)
        keys_rows = keys_all.reshape(micro_rows, row_len, HEADS, HEAD_DIM)
        values_rows = values_all.reshape(micro_rows, row_len, HEADS, HEAD_DIM)

        def attend_row(pieces):
            order_row, lengths_row, row_queries, row_keys, row_values = pieces
            scores, live, onehot = row_scores(order_row, lengths_row, row_queries, row_keys, table)
            peak = jnp.max(scores, axis=-1, keepdims=True)
            total = jnp.sum(jnp.exp(scores - peak), axis=-1, keepdims=True)
            logsum = peak + jnp.log(total)
            probs = (jnp.exp(scores - logsum) * live[None, :, None]).astype(jnp.bfloat16)
            mixed = jnp.einsum(
                "hqk,khd->qhd", probs, row_values, preferred_element_type=jnp.float32
            )
            return (mixed.reshape(2 * block, width).astype(jnp.bfloat16), logsum)

        mixed, logsums = lax.map(
            attend_row, (order_rows, length_rows, queries_rows, keys_rows, values_rows)
        )
        mixed_flat = mixed.reshape(-1, width)
        branch = matmul(mixed_flat, output_matrix) + output_offset
        first_in = flat.astype(jnp.float32) + branch
        first = layer_norm(first_in, mixer_scale, mixer_offset)
        first_low = first.astype(jnp.bfloat16)
        up = matmul(first_low, up_matrix) + up_offset
        act = gelu_exact(up).astype(jnp.bfloat16)
        down = matmul(act, down_matrix) + down_offset
        second_in = first + down
        result = layer_norm(second_in, final_scale, final_offset).reshape(
            micro_rows, 2 * block, width
        )
        content_parts.append(result[:, :block].astype(jnp.bfloat16))
        query_parts.append(result[:, block:].astype(jnp.bfloat16))
        cot = jnp.concatenate(
            [
                content_cot[micro * micro_rows : (micro + 1) * micro_rows],
                query_cot[micro * micro_rows : (micro + 1) * micro_rows],
            ],
            axis=1,
        )
        cot = cot.reshape(-1, width).astype(jnp.float32)
        _, final_back = jax.vjp(layer_norm, second_in, final_scale, final_offset)
        grad_second, grad_fscale, grad_foffset = final_back(cot)
        grad_down = grad_second.astype(jnp.bfloat16)
        grad_down_matrix = left_product(act, grad_down)
        grad_down_offset = jnp.sum(grad_down.astype(jnp.float32), axis=0)
        grad_act = right_product(grad_down, down_matrix)
        _, gelu_back = jax.vjp(gelu_exact, up)
        grad_up = gelu_back(grad_act)[0].astype(jnp.bfloat16)
        grad_up_matrix = left_product(first_low, grad_up)
        grad_up_offset = jnp.sum(grad_up.astype(jnp.float32), axis=0)
        grad_first = grad_second + right_product(grad_up, up_matrix)
        _, mixer_back = jax.vjp(layer_norm, first_in, mixer_scale, mixer_offset)
        grad_res, grad_mscale, grad_moffset = mixer_back(grad_first)
        grad_branch = grad_res.astype(jnp.bfloat16)
        grad_out_matrix = left_product(mixed_flat, grad_branch)
        grad_out_offset = jnp.sum(grad_branch.astype(jnp.float32), axis=0)
        grad_mixed = right_product(grad_branch, output_matrix).astype(jnp.bfloat16)
        grad_mixed_rows = grad_mixed.reshape(micro_rows, 2 * block, HEADS, HEAD_DIM)

        def attend_back(pieces):
            order_row, lengths_row, row_queries, row_keys, row_values, row_logsum, row_grad = pieces
            scores, live, onehot = row_scores(order_row, lengths_row, row_queries, row_keys, table)
            probs = jnp.exp(scores - row_logsum) * live[None, :, None]
            grad_probs = jnp.einsum(
                "qhd,khd->hqk", row_grad, row_values, preferred_element_type=jnp.float32
            )
            inner = jnp.sum(probs * grad_probs, axis=-1, keepdims=True)
            grad_scores = (probs * (grad_probs - inner)).astype(jnp.bfloat16)
            grad_queries = (
                jnp.einsum(
                    "hqk,khd->qhd", grad_scores, row_keys, preferred_element_type=jnp.float32
                )
                * scale
            )
            grad_keys = (
                jnp.einsum(
                    "hqk,qhd->khd", grad_scores, row_queries, preferred_element_type=jnp.float32
                )
                * scale
            )
            grad_values = jnp.einsum(
                "hqk,qhd->khd",
                probs.astype(jnp.bfloat16),
                row_grad,
                preferred_element_type=jnp.float32,
            )
            split_scores = grad_scores.reshape(HEADS, 2, block, row_len)
            grad_table = jnp.einsum(
                "bcl,hscl->bh", onehot, split_scores, preferred_element_type=jnp.float32
            )
            return (
                grad_queries.reshape(2 * block, width),
                grad_keys.reshape(row_len, width),
                grad_values.reshape(row_len, width),
                grad_table,
            )

        grad_queries, grad_keys_all, grad_values_all, grad_tables = lax.map(
            attend_back,
            (
                order_rows,
                length_rows,
                queries_rows,
                keys_rows,
                values_rows,
                logsums,
                grad_mixed_rows,
            ),
        )
        grad_keys, grad_values = (
            lax.psum_scatter(grad_keys_all, "seq", scatter_dimension=1, tiled=True),
            lax.psum_scatter(grad_values_all, "seq", scatter_dimension=1, tiled=True),
        )
        grad_q = grad_queries.reshape(-1, width).astype(jnp.bfloat16)
        grad_k = grad_keys.reshape(-1, width).astype(jnp.bfloat16)
        grad_v = grad_values.reshape(-1, width).astype(jnp.bfloat16)
        grad_query_matrix = left_product(flat, grad_q)
        grad_query_offset = jnp.sum(grad_q.astype(jnp.float32), axis=0)
        grad_key_matrix = left_product(own_flat, grad_k)
        grad_value_matrix = left_product(own_flat, grad_v)
        grad_value_offset = jnp.sum(grad_v.astype(jnp.float32), axis=0)
        grad_table_flat = jnp.sum(grad_tables, axis=0).reshape(-1)
        grad_inputs = (grad_res + right_product(grad_q, query_matrix)).reshape(
            micro_rows, 2 * block, width
        )
        from_keys = right_product(grad_k, key_matrix) + right_product(grad_v, value_matrix)
        content_grads.append(
            (grad_inputs[:, :block] + from_keys.reshape(micro_rows, block, width)).astype(
                jnp.bfloat16
            )
        )
        query_grads.append(grad_inputs[:, block:].astype(jnp.bfloat16))
        shard_sums = (
            lax.psum_scatter(grad_query_matrix, "dp", scatter_dimension=0, tiled=True),
            lax.psum_scatter(grad_query_offset, "dp", scatter_dimension=0, tiled=True),
            lax.psum_scatter(grad_key_matrix, "dp", scatter_dimension=0, tiled=True),
            lax.psum_scatter(grad_value_matrix, "dp", scatter_dimension=0, tiled=True),
            lax.psum_scatter(grad_value_offset, "dp", scatter_dimension=0, tiled=True),
            lax.psum_scatter(grad_out_matrix, "dp", scatter_dimension=0, tiled=True),
            lax.psum_scatter(grad_out_offset, "dp", scatter_dimension=0, tiled=True),
            lax.psum_scatter(grad_mscale, "dp", scatter_dimension=0, tiled=True),
            lax.psum_scatter(grad_moffset, "dp", scatter_dimension=0, tiled=True),
            lax.psum_scatter(grad_up_matrix, "dp", scatter_dimension=1, tiled=True),
            lax.psum_scatter(grad_up_offset, "dp", scatter_dimension=0, tiled=True),
            lax.psum_scatter(grad_down_matrix, "dp", scatter_dimension=0, tiled=True),
            lax.psum_scatter(grad_down_offset, "dp", scatter_dimension=0, tiled=True),
            lax.psum_scatter(grad_fscale, "dp", scatter_dimension=0, tiled=True),
            lax.psum_scatter(grad_foffset, "dp", scatter_dimension=0, tiled=True),
            lax.psum_scatter(grad_table_flat, "dp", scatter_dimension=0, tiled=True),
        )
        totals = shard_sums if totals is None else add_trees(totals, shard_sums)
    summed = lax.psum(
        (
            totals[0],
            totals[1],
            totals[2],
            totals[3],
            totals[4],
            totals[5],
            totals[6],
            totals[7],
            totals[8],
            totals[9],
            totals[10],
            totals[11],
            totals[12],
            totals[13],
            totals[14],
            totals[15],
        ),
        "seq",
    )
    return (
        jnp.concatenate(content_parts, axis=0),
        jnp.concatenate(query_parts, axis=0),
        jnp.concatenate(content_grads, axis=0),
        jnp.concatenate(query_grads, axis=0),
        summed[0],
        summed[1],
        summed[2],
        summed[3],
        summed[4],
        summed[5],
        summed[6],
        summed[7],
        summed[8],
        summed[9],
        summed[10],
        summed[11],
        summed[12],
        summed[13],
        summed[14],
        summed[15],
    )


def solution(mesh):
    in_specs = (
        P("dp", "seq", None),
        P("dp", "seq", None),
        P("dp", "seq", None),
        P("dp", "seq", None),
        P("dp", None),
        P("dp", None),
        P("dp", None),
        P("dp"),
        P("dp", None),
        P("dp", None),
        P("dp"),
        P("dp", None),
        P("dp"),
        P("dp"),
        P("dp"),
        P(None, "dp"),
        P("dp"),
        P("dp", None),
        P("dp"),
        P("dp"),
        P("dp"),
        P("dp"),
    )
    out_specs = (
        P("dp", "seq", None),
        P("dp", "seq", None),
        P("dp", "seq", None),
        P("dp", "seq", None),
        P("dp", None),
        P("dp"),
        P("dp", None),
        P("dp", None),
        P("dp"),
        P("dp", None),
        P("dp"),
        P("dp"),
        P("dp"),
        P(None, "dp"),
        P("dp"),
        P("dp", None),
        P("dp"),
        P("dp"),
        P("dp"),
        P("dp"),
    )
    return jax.shard_map(shards, mesh=mesh, in_specs=in_specs, out_specs=out_specs, check_vma=False)
```

profile of v0, /device:TPU:0, one launch (start us, length us, event | category | flops | bytes accessed | tf_op | source)
XLA Modules:
  0.0 1529.2 jit_solution(5929596899238769337)
XLA Ops:
  25.0 79.0 %all-reduce.23 = (bf16[768]{0:T(1024)(128)(2,1)S(1)}, bf16[384]{0:T(512)(128)(2,1)S(1)}, bf16[768]{0:T(1024)(128)(2,1)S(1)}, bf16[768]{0:T(1024)(128)(2,1)S(1)},...) all-reduce(bf16[768]{0:T(1024)(128)(2,1)S(1)} %dynamic-update-slice, ...), channel_id=1, replica_groups=mesh['dp'=16,'seq'=2] {'dp'}, use_global_device_ids=true, to_apply=%add | all-reduce | flops 9600 | bytes 38400
  119.1 6.3 copy.110
  128.6 6.2 copy.104
  154.1 31.6 %all-gather.13.cloned.1.call-done = bf16[768,768]{1,0:T(8,128)(2,1)} async-done(((bf16[48,768]{1,0:T(8,128)(2,1)}), bf16[768,768]{1,0:T(8,128)(2,1)}) %all-gather.13.cloned.1.call-update) | async-done | bytes 1179664 | tf_op jit(solution)/shard_map/all_gather | solution.py:121
  194.9 8.0 fusion.161
  215.1 28.2 %all-gather.17.cloned.1.call-done = bf16[768,768]{1,0:T(8,128)(2,1)} async-done(((bf16[48,768]{1,0:T(8,128)(2,1)}), bf16[768,768]{1,0:T(8,128)(2,1)}) %all-gather.17.cloned.1.call-update) | async-done | bytes 1179664 | tf_op jit(solution)/shard_map/all_gather | solution.py:126
  246.9 7.2 fusion.159
  265.1 60.3 %all-gather.19.cloned.1.call-done = bf16[768,3072]{0,1:T(8,128)(2,1)} async-done(((bf16[768,192]{0,1:T(8,128)(2,1)}), bf16[768,3072]{0,1:T(8,128)(2,1)}) %all-gather.19.cloned.1.call-update) | async-done | bytes 4718608 | tf_op jit(solution)/shard_map/all_gather | solution.py:130
  333.2 35.5 %multiply_convert_fusion.3 = (bf16[512,3072]{1,0:T(8,128)(2,1)}, f32[512,3072]{1,0:T(8,128)}, bf16[512,3072]{1,0:T(8,128)(2,1)}, f32[512,3072]{1,0:T(8,128)}, f32[512,3072]{1,0:T(8,128)}) fusion(f32[3072]{0:T(1024)S(1)} %copy-done.102, f32[512,3072]{1,0:T(8,128)S(1)} %fusion.137, bf16[768,3072]{0,1:T(8,128)(2,1)S(1)} %copy-done.126, ...), kind=kOutput, calls=%fused_computation.49 | convolution fusion | flops 2625503232 | bytes 37771264 | tf_op jit(solution)/shard_map/dot_general | solution.py:37
  368.7 38.5 %all-gather.21.cloned.1.call-done = bf16[3072,768]{1,0:T(8,128)(2,1)} async-done(((bf16[192,768]{1,0:T(8,128)(2,1)}), bf16[3072,768]{1,0:T(8,128)(2,1)}) %all-gather.21.cloned.1.call-update) | async-done | bytes 4718608 | tf_op jit(solution)/shard_map/all_gather | solution.py:132
  430.1 18.3 %convert_reduce_fusion.3 = (f32[3072]{0:T(1024)}, bf16[512,3072]{1,0:T(8,128)(2,1)}, f32[3072]{0:T(1024)}, bf16[512,3072]{1,0:T(8,128)(2,1)}) fusion(f32[512,3072]{1,0:T(8,128)} %get-tuple-element.311, f32[512,3072]{1,0:T(8,128)} %get-tuple-element.366, f32[3072]{0:T(1024)S(1)} %copy-done.103, f32[512,3072]{1,0:T(8,128)} %fusion.166, ...), kind=kOutput, calls=%fused_computation.33 | convolution fusion | flops 2469390336 | bytes 43290624 | tf_op jit(solution)/shard_map/dot_general | solution.py:47
  448.4 6.5 add_add_fusion.8
  454.9 6.2 multiply_reduce_fusion.3
  486.7 8.0 multiply_reduce_fusion.1
  494.7 6.6 multiply_convert_fusion.1
  504.6 7.8 multiply_reduce_fusion
  512.4 6.6 multiply_convert_fusion
  613.3 51.8 %reduce-scatter.33.cloned.1.call-done = f32[48,768]{1,0:T(8,128)} async-done(((f32[768,768]{1,0:T(8,128)}), f32[48,768]{1,0:T(8,128)}) %reduce-scatter.33.cloned.1.call-update) | async-done | bytes 147472
  666.9 131.3 %reduce-scatter.31.cloned.1.call-done = f32[48,768]{1,0:T(8,128)} async-done(((f32[768,768]{1,0:T(8,128)}), f32[48,768]{1,0:T(8,128)}) %reduce-scatter.31.cloned.1.call-update) | async-done | bytes 147472
  800.0 130.7 %reduce-scatter.25.cloned.1.call-done = f32[48,768]{1,0:T(8,128)} async-done(((f32[768,768]{1,0:T(8,128)}), f32[48,768]{1,0:T(8,128)}) %reduce-scatter.25.cloned.1.call-update) | async-done | bytes 147472 | tf_op jit(solution)/shard_map/reduce_scatter | solution.py:305
  930.7 133.2 %reduce-scatter.23.cloned.1.call-done = f32[48,768]{1,0:T(8,128)} async-done(((f32[768,768]{1,0:T(8,128)}), f32[48,768]{1,0:T(8,128)}) %reduce-scatter.23.cloned.1.call-update) | async-done | bytes 147472 | tf_op jit(solution)/shard_map/reduce_scatter | solution.py:300
  1063.9 175.4 %reduce-scatter.27.cloned.1.call-done = f32[768,192]{0,1:T(8,128)} async-done(((f32[768,3072]{0,1:T(8,128)}), f32[768,192]{0,1:T(8,128)}) %reduce-scatter.27.cloned.1.call-update) | async-done | bytes 589840 | tf_op jit(solution)/shard_map/reduce_scatter | solution.py:309
  1239.3 176.8 %reduce-scatter.29.cloned.1.call-done = f32[192,768]{1,0:T(8,128)} async-done(((f32[3072,768]{1,0:T(8,128)}), f32[192,768]{1,0:T(8,128)}) %reduce-scatter.29.cloned.1.call-update) | async-done | bytes 589840 | tf_op jit(solution)/shard_map/reduce_scatter | solution.py:311
  1418.1 76.0 %all-reduce.20 = (f32[768]{0:T(1024)}, f32[768]{0:T(1024)}, f32[768]{0:T(1024)}, f32[768]{0:T(1024)}, f32[768]{0:T(1024)}, /*index=5*/f32[3072]{0:T(1024)}, f32[...) all-reduce(f32[768]{0:T(1024)} %reshape.556, ...), channel_id=27, replica_groups=mesh['dp'=16,'seq'=2] {'dp'}, use_global_device_ids=true, to_apply=%region_36.37.clone | all-reduce | flops 9600 | bytes 76800
  (498 shorter events, 273.2 us)
Async XLA Ops:
  7.2 127.6 %all-gather.11.cloned.1.call-start = ((), (), s32[]{:S(2)}) async-start(), calls=%async_computation.10 | async-start | bytes 1253376 | tf_op jit(solution)/shard_map/all_gather | solution.py:124
  7.9 135.3 %all-gather.15.cloned.1.call-start = ((), (), s32[]{:S(2)}) async-start(), calls=%async_computation.12 | async-start | bytes 1253376 | tf_op jit(solution)/shard_map/all_gather | solution.py:123
  8.7 177.0 %all-gather.13.cloned.1.call-start = ((), (), s32[]{:S(2)}) async-start(), calls=%async_computation.11 | async-start | bytes 1253376 | tf_op jit(solution)/shard_map/all_gather | solution.py:121
  9.4 233.9 %all-gather.17.cloned.1.call-start = ((), (), s32[]{:S(2)}) async-start(), calls=%async_computation.13 | async-start | bytes 1253376 | tf_op jit(solution)/shard_map/all_gather | solution.py:126
  10.0 315.4 %all-gather.19.cloned.1.call-start = ((), (), s32[]{:S(2)}) async-start(), calls=%async_computation.14 | async-start | bytes 5013504 | tf_op jit(solution)/shard_map/all_gather | solution.py:130
  10.6 396.6 %all-gather.21.cloned.1.call-start = ((), (), s32[]{:S(2)}) async-start(), calls=%async_computation.15 | async-start | bytes 5013504 | tf_op jit(solution)/shard_map/all_gather | solution.py:132
  11.2 511.0 %reduce-scatter.17.cloned.1.call-start = ((), (), s32[]{:S(2)}) async-start(), calls=%async_computation.17 | async-start | bytes 2359296 | tf_op jit(solution)/shard_map/reduce_scatter | solution.py:278
  109.6 147.6 %copy-start.84 = (f32[512]{0:T(512)}, f32[512]{0:T(512)S(1)}, u32[]{:S(2)}) copy-start(f32[512]{0:T(512)S(1)} %convert_element_type.628) | copy-start | bytes 6148
  264.7 196.5 %copy-start.19 = (f32[512,768]{1,0:T(8,128)}, f32[512,768]{1,0:T(8,128)S(1)}, u32[]{:S(2)}) copy-start(f32[512,768]{1,0:T(8,128)S(1)} %get-tuple-element.361) | copy-start | bytes 4718596
  264.8 142.4 %copy-start.89 = (f32[512]{0:T(512)}, f32[512]{0:T(512)S(1)}, u32[]{:S(2)}) copy-start(f32[512]{0:T(512)S(1)} %broadcast_multiply_fusion.3) | copy-start | bytes 6148
  265.1 142.1 %copy-start.106 = (f32[512]{0:T(512)}, f32[512]{0:T(512)S(1)}, u32[]{:S(2)}) copy-start(f32[512]{0:T(512)S(1)} %fusion.116) | copy-start | bytes 6148
  473.8 51.4 %reduce-scatter.21.cloned.1.call-start = ((), (), s32[]{:S(2)}) async-start(), calls=%async_computation.19 | async-start | bytes 2359296 | tf_op jit(solution)/shard_map/reduce_scatter | solution.py:278
  486.6 45.7 %reduce-scatter.15.cloned.1.call-start = ((), (), s32[]{:S(2)}) async-start(), calls=%async_computation.16 | async-start | bytes 2359296 | tf_op jit(solution)/shard_map/reduce_scatter | solution.py:277
  504.5 30.9 %reduce-scatter.19.cloned.1.call-start = ((), (), s32[]{:S(2)}) async-start(), calls=%async_computation.18 | async-start | bytes 2359296 | tf_op jit(solution)/shard_map/reduce_scatter | solution.py:277
  522.1 142.9 %reduce-scatter.33.cloned.1.call-start = ((), (), s32[]{:S(2)}) async-start(), calls=%async_computation.25 | async-start | bytes 2506752
  532.2 266.0 %reduce-scatter.31.cloned.1.call-start = ((), (), s32[]{:S(2)}) async-start(), calls=%async_computation.24 | async-start | bytes 2506752
  542.3 388.4 %reduce-scatter.25.cloned.1.call-start = ((), (), s32[]{:S(2)}) async-start(), calls=%async_computation.21 | async-start | bytes 2506752 | tf_op jit(solution)/shard_map/reduce_scatter | solution.py:305
  546.8 517.1 %reduce-scatter.23.cloned.1.call-start = ((), (), s32[]{:S(2)}) async-start(), calls=%async_computation.20 | async-start | bytes 2506752 | tf_op jit(solution)/shard_map/reduce_scatter | solution.py:300
  562.6 676.8 %reduce-scatter.27.cloned.1.call-start = ((), (), s32[]{:S(2)}) async-start(), calls=%async_computation.22 | async-start | bytes 10027008 | tf_op jit(solution)/shard_map/reduce_scatter | solution.py:309
  573.0 843.2 %reduce-scatter.29.cloned.1.call-start = ((), (), s32[]{:S(2)}) async-start(), calls=%async_computation.23 | async-start | bytes 10027008 | tf_op jit(solution)/shard_map/reduce_scatter | solution.py:311
  583.4 929.4 %all-reduce.26.cloned.1.call-start = ((), (), s32[]{:S(2)}) async-start(), calls=%async_computation.26 | async-start | bytes 4521984 | tf_op jit(solution)/shard_map/psum | solution.py:318
  612.3 804.8 %copy-start.9 = (f32[1,256,768]{1,2,0:T(8,128)S(1)}, f32[1,256,768]{1,2,0:T(8,128)}, u32[]{:S(2)}) copy-start(f32[1,256,768]{1,2,0:T(8,128)} %reduce-scatter.21.cloned.1.call-done) | copy-start | bytes 2359300
  613.3 804.0 %copy-start.8 = (f32[1,256,768]{1,2,0:T(8,128)S(1)}, f32[1,256,768]{1,2,0:T(8,128)}, u32[]{:S(2)}) copy-start(f32[1,256,768]{1,2,0:T(8,128)} %reduce-scatter.17.cloned.1.call-done) | copy-start | bytes 2359300
  666.9 841.0 %copy-start.40 = (f32[1,256,768]{1,2,0:T(8,128)S(1)}, f32[1,256,768]{1,2,0:T(8,128)}, u32[]{:S(2)}) copy-start(f32[1,256,768]{1,2,0:T(8,128)} %reduce-scatter.15.cloned.1.call-done) | copy-start | bytes 2359300
  (127 other events, 1667.5 us)
Sparse Core Ops, SparseCore 0:
  10.8 58.9 all-gather.10
  72.7 55.0 all-gather.14
  130.6 54.9 all-gather.12
  188.3 55.0 all-gather.16
  246.0 79.3 all-gather.18
  328.0 79.0 all-gather.20
  473.9 7.6 reduce-scatter.16
  486.7 7.8 reduce-scatter.20
  504.6 7.8 reduce-scatter.14
  522.2 8.0 reduce-scatter.18
  535.2 129.7 reduce-scatter.32
  670.6 127.5 reduce-scatter.30
  803.1 127.5 reduce-scatter.24
  936.3 127.5 reduce-scatter.22
  1069.4 169.8 reduce-scatter.26
  1245.8 170.2 reduce-scatter.28
  1419.3 20.7 all-reduce.25
where the time goes:
time: 1530 us
  waiting for transfers between devices  962 us (63%)
  matrix products  232 us (15%)
  blocking collectives  168 us (11%)
  local copies, waits for them, and re-layouts  85.4 us (6%)
  other arithmetic  61.3 us (4%)
  between operations  20.1 us (1%)
    unnamed x19, waiting for transfers between devices  187 us
    reduce_scatter x1, waiting for transfers between devices, shards(): lax.psum_scatter(grad_down_matrix, 'dp', scatter_dimension=0, tiled=True)  177 us
    reduce_scatter x1, waiting for transfers between devices, shards(): lax.psum_scatter(grad_up_matrix, 'dp', scatter_dimension=1, tiled=True)  175 us
    unnamed x2, blocking collectives  155 us
    reduce_scatter x1, waiting for transfers between devices, shards(): lax.psum_scatter(grad_query_matrix, 'dp', scatter_dimension=0, tiled=True)  133 us
    reduce_scatter x1, waiting for transfers between devices, shards(): lax.psum_scatter(grad_out_matrix, 'dp', scatter_dimension=0, tiled=True)  131 us
    dot_general x12, matrix products, matmul(): return jnp.dot(left, right, preferred_element_type=jnp.float32)  65.1 us
    all_gather x1, waiting for transfers between devices, shards(): lax.all_gather(up_weight, 'dp', axis=1, tiled=True)  60.3 us
  transfers between devices with their start and end apart: 17, of which 10 were waited for; matrix products, arithmetic and copies ran while one was open for 19% of the time, Pallas kernels for 0%

commit v1 on v0

v1 whole, which is shorter than its diff:
```python
import functools
import math

import jax
import jax.numpy as jnp
from jax import lax
from jax.experimental import pallas as pl
from jax.experimental.pallas import tpu as pltpu
from jax.sharding import PartitionSpec as P

HEADS = 12
HEAD_DIM = 64
BUCKETS = 32
GROUP = 4
LANES = GROUP * HEAD_DIM
GROUPS = HEADS // GROUP
TILE = 128
NEG = -1e30
FLOOR = -1e29
EPS = 1e-05

limits = (1, 2, 3, 4, 5, 6, 7, 8, 12, 16, 23, 32, 46, 64, 91)

NN = (((1,), (0,)), ((), ()))
NT = (((1,), (1,)), ((), ()))
TN = (((0,), (0,)), ((), ()))
VMEM_SPEC = pl.BlockSpec(memory_space=pltpu.VMEM)
SMEM_SPEC = pl.BlockSpec(memory_space=pltpu.SMEM)
SDS = jax.ShapeDtypeStruct


def product(left, right, dims=NN):
    return lax.dot_general(left, right, dims, preferred_element_type=jnp.float32)


def params(semantics=None, limit=56):
    return pltpu.CompilerParams(dimension_semantics=semantics, vmem_limit_bytes=limit << 20)


def row_sum(values):
    return jnp.sum(values, axis=-1, keepdims=True)


def sort_kernel(bounds, content, query, ccot, qcot, order_row, order_col, pos_row, pos_col,
                xs_out, cs_out, mask_out):
    length = order_row.shape[1]
    down = lax.broadcasted_iota(jnp.int32, (length, length), 0)
    across = lax.broadcasted_iota(jnp.int32, (length, length), 1)
    forward = order_row[...] == down
    backward = order_col[...] == across
    rank_col = row_sum(jnp.where(forward, pos_row[...].astype(jnp.float32), 0.0))
    rank_row = jnp.sum(
        jnp.where(backward, pos_col[...].astype(jnp.float32), 0.0), axis=0, keepdims=True
    )
    place_col = lax.broadcasted_iota(jnp.int32, (length, 1), 0)
    place_row = lax.broadcasted_iota(jnp.int32, (1, length), 1)
    segment_col = jnp.zeros((length, 1), jnp.int32)
    segment_row = jnp.zeros((1, length), jnp.int32)
    for index in range(bounds.shape[0]):
        segment_col = segment_col + (place_col >= bounds[index]).astype(jnp.int32)
        segment_row = segment_row + (place_row >= bounds[index]).astype(jnp.int32)
    same = segment_col == segment_row
    mask_out[0] = jnp.where(same & (rank_row <= rank_col), 0.0, NEG)
    mask_out[1] = jnp.where(same & (rank_row < rank_col), 0.0, NEG)
    onehot = jnp.where(forward, 1.0, 0.0).astype(jnp.bfloat16)
    for source, target, at in (
        (content, xs_out, 0), (query, xs_out, 1), (ccot, cs_out, 0), (qcot, cs_out, 1),
    ):
        target[at * length : (at + 1) * length, :] = product(onehot, source[...]).astype(
            jnp.bfloat16
        )


def sort_rows(bounds, content, query, ccot, qcot, order, pos):
    length, width = content.shape
    return pl.pallas_call(
        sort_kernel,
        out_shape=(
            SDS((2 * length, width), jnp.bfloat16),
            SDS((2 * length, width), jnp.bfloat16),
            SDS((2, length, length), jnp.float32),
        ),
        in_specs=[SMEM_SPEC] + [VMEM_SPEC] * 8,
        out_specs=(VMEM_SPEC,) * 3,
        compiler_params=params(),
        name="sort_rows",
    )(bounds, content, query, ccot, qcot, order.reshape(1, length), order.reshape(length, 1),
      pos.reshape(1, length), pos.reshape(length, 1))


def unsort_kernel(order_col, values, out):
    length = order_col.shape[0]
    across = lax.broadcasted_iota(jnp.int32, (length, length), 1)
    onehot = jnp.where(order_col[...] == across, 1.0, 0.0).astype(jnp.bfloat16)
    for stream in range(2):
        out[stream] = product(
            onehot, values[stream * length : (stream + 1) * length, :]
        ).astype(jnp.bfloat16)


def unsort_rows(order, values):
    length = order.shape[0]
    width = values.shape[1]
    return pl.pallas_call(
        unsort_kernel,
        out_shape=SDS((2, length, width), jnp.bfloat16),
        in_specs=[VMEM_SPEC] * 2,
        out_specs=VMEM_SPEC,
        compiler_params=params(),
        name="unsort_rows",
    )(order.reshape(length, 1), values)


def bucket_onehot(length):
    distance = lax.broadcasted_iota(jnp.int32, (BUCKETS, 2 * length), 1) - (length - 1)
    magnitude = jnp.abs(distance)
    counted = jnp.zeros(distance.shape, jnp.int32)
    for limit in limits:
        counted = counted + (magnitude >= limit).astype(jnp.int32)
    bucket = counted + 16 * (distance > 0).astype(jnp.int32)
    return bucket == lax.broadcasted_iota(jnp.int32, distance.shape, 0)


def bias_kernel(table, out):
    length = 512
    onehot = jnp.where(bucket_onehot(length), 1.0, 0.0).astype(jnp.bfloat16)
    rows = product(table[...], onehot)
    for head in range(HEADS):
        spread = jnp.broadcast_to(rows[head : head + 1, :], (TILE, 2 * length))
        out[head] = pltpu.roll(
            spread, 2 * length - (TILE - 1), 1, stride=1, stride_axis=0
        )[:, : 2 * length - TILE]


def bias_table(table, length):
    return pl.pallas_call(
        bias_kernel,
        out_shape=SDS((HEADS, TILE, 2 * length - TILE), jnp.float32),
        in_specs=[VMEM_SPEC],
        out_specs=VMEM_SPEC,
        compiler_params=params(),
        name="bias_table",
    )(table)


def block_copies(spots, pieces, target, sems, tiles):
    count = sum(piece.shape[0] for piece in pieces)
    half = spots[count]
    copies = []
    for index, piece in enumerate(pieces):
        side = half if index < len(pieces) // 2 else 1 - half
        rows = piece.shape[2]
        for block in range(piece.shape[0]):
            at = len(copies)
            row = pl.multiple_of(spots[at] * rows, rows)
            copies.append(
                pltpu.make_async_copy(
                    piece.at[block, tiles],
                    target.at[side, :, pl.ds(row, rows), :],
                    sems.at[at],
                )
            )
    return copies


def block_stores(spots, source, outs, sems, tiles):
    count = sum(out.shape[0] for out in outs)
    half = spots[count]
    copies = []
    for index, out in enumerate(outs):
        side = half if index == 0 else 1 - half
        rows = out.shape[2]
        for block in range(out.shape[0]):
            at = len(copies)
            row = pl.multiple_of(spots[at] * rows, rows)
            copies.append(
                pltpu.make_async_copy(
                    source.at[side, :, pl.ds(row, rows), :],
                    out.at[block, tiles],
                    sems.at[at],
                )
            )
    return copies


def run_copies(copies):
    for copy in copies:
        copy.start()
    for copy in copies:
        copy.wait()


def joined(weights, index):
    return jnp.concatenate([weights[0, index], weights[1, index]], axis=1)


def head_lanes(head, shape):
    lane = lax.broadcasted_iota(jnp.int32, shape, 1)
    return (lane >= head * HEAD_DIM) & (lane < (head + 1) * HEAD_DIM)


def attend_kernel(spots, xs, mask, bias, bq, bv, *rest):
    pieces, rest = rest[:-7], rest[-7:]
    q_out, k_out, v_out, mixed_out, lse_out, weights_all, sems = rest
    length = mask.shape[1]
    group = pl.program_id(0)

    @pl.when(group == 0)
    def _():
        copies = block_copies(spots, pieces, weights_all, sems, slice(0, 3 * GROUPS))
        run_copies(copies)

    q = (product(xs[...], joined(weights_all, 3 * group)) + bq[...]).astype(jnp.bfloat16)
    q_out[...] = q
    k = product(xs[0:length, :], joined(weights_all, 3 * group + 1)).astype(jnp.bfloat16)
    k_out[...] = k
    v = product(xs[0:length, :], joined(weights_all, 3 * group + 2)) + bv[...]
    v = v.astype(jnp.bfloat16)
    v_out[...] = v
    low = jnp.bfloat16(0)
    heads_v = [jnp.where(head_lanes(h, v.shape), v, low) for h in range(GROUP)]
    for stream in range(2):
        for tile in range(length // TILE):
            at = stream * length + tile * TILE
            q_tile = q_out[at : at + TILE, :] * jnp.bfloat16(0.125)
            masked = mask[stream, tile * TILE : (tile + 1) * TILE, :]
            total = jnp.zeros((TILE, LANES), jnp.float32)
            for h in range(GROUP):
                q_head = jnp.where(head_lanes(h, q_tile.shape), q_tile, low)
                scores = product(q_head, k, NT)
                first = length - TILE - tile * TILE
                scores = scores + bias[h, :, first : first + length] + masked
                peak = jnp.maximum(jnp.max(scores, axis=-1, keepdims=True), FLOOR)
                weights = jnp.exp(scores - peak)
                summed = row_sum(weights)
                alive = summed > 0
                inverse = jnp.where(alive, 1.0 / summed, 0.0)
                probs = (weights * inverse).astype(jnp.bfloat16)
                total = total + product(probs, heads_v[h])
                lse_out[0, at : at + TILE, h : h + 1] = jnp.where(
                    alive, peak + jnp.log(summed), 0.0
                )
            mixed_out[at : at + TILE, :] = total.astype(jnp.bfloat16)


def attend(spots, xs, mask, bias, bq, bv, pieces):
    tokens, width = xs.shape
    blocks = sum(piece.shape[0] for piece in pieces)
    length = mask.shape[1]
    full = lambda g: (0, 0)
    column = lambda g: (0, g)
    return pl.pallas_call(
        attend_kernel,
        grid=(GROUPS,),
        out_shape=(
            SDS((tokens, width), jnp.bfloat16),
            SDS((length, width), jnp.bfloat16),
            SDS((length, width), jnp.bfloat16),
            SDS((tokens, width), jnp.bfloat16),
            SDS((GROUPS, tokens, 128), jnp.float32),
        ),
        in_specs=[
            SMEM_SPEC,
            pl.BlockSpec((tokens, width), full),
            pl.BlockSpec((2, length, length), lambda g: (0, 0, 0)),
            pl.BlockSpec((GROUP, TILE, bias.shape[2]), lambda g: (g, 0, 0)),
            pl.BlockSpec((1, LANES), column),
            pl.BlockSpec((1, LANES), column),
        ] + [pl.BlockSpec(memory_space=pl.ANY)] * len(pieces),
        out_specs=(
            pl.BlockSpec((tokens, LANES), column),
            pl.BlockSpec((length, LANES), column),
            pl.BlockSpec((length, LANES), column),
            pl.BlockSpec((tokens, LANES), column),
            pl.BlockSpec((1, tokens, 128), lambda g: (g, 0, 0)),
        ),
        scratch_shapes=[
            pltpu.VMEM((2, 3 * GROUPS, width, 128), jnp.bfloat16),
            pltpu.SemaphoreType.DMA((blocks,)),
        ],
        compiler_params=params(("arbitrary",)),
        name="attend",
    )(spots, xs, mask, bias, bq, bv, *pieces)


BLOCK = 256


def norm_parts(values):
    mean = jnp.mean(values, axis=-1, keepdims=True)
    center = values - mean
    spread = jnp.mean(center * center, axis=-1, keepdims=True)
    scale = lax.rsqrt(spread + EPS)
    return center * scale, scale


def norm_back(normal, scale, grad):
    mean = jnp.mean(grad, axis=-1, keepdims=True)
    inner = jnp.mean(grad * normal, axis=-1, keepdims=True)
    return scale * (grad - mean - normal * inner)


def column_sum(values):
    return jnp.sum(values, axis=0, keepdims=True)


def feed_kernel(spots, xs, mixed, cot, up_own, up_other, down_own, down_other, rows, up_bias,
                *rest):
    pieces, rest = rest[:-12], rest[-12:]
    (out, act_out, gup_out, first_out, gdown_out, gres_out, gbranch_out, gmixed_out,
     sums, up_sums, wo_all, sems) = rest
    step = pl.program_id(0)
    out_bias, mixer_gain, mixer_shift = rows[0:1, :], rows[1:2, :], rows[2:3, :]
    down_bias, final_gain, final_shift = rows[3:4, :], rows[4:5, :], rows[5:6, :]
    half = up_own.shape[0]

    @pl.when(step == 0)
    def _():
        sums[...] = jnp.zeros_like(sums)
        up_sums[...] = jnp.zeros_like(up_sums)
        tiles = slice(3 * GROUPS, 4 * GROUPS)
        run_copies(block_copies(spots, pieces, wo_all, sems, tiles))

    wo = jnp.concatenate([joined(wo_all, index) for index in range(GROUPS)], axis=1)
    branch = product(mixed[...], wo) + out_bias
    normal1, scale1 = norm_parts(xs[...].astype(jnp.float32) + branch)
    first = normal1 * mixer_gain + mixer_shift
    first_low = first.astype(jnp.bfloat16)
    first_out[...] = first_low
    slopes = []
    second = first + down_bias
    for index, (up_w, down_w) in enumerate(((up_own, down_own), (up_other, down_other))):
        lanes = slice(index * half, (index + 1) * half)
        up = product(first_low, up_w[...], NT) + up_bias[:, lanes]
        gate = 0.5 * (1.0 + lax.erf(up * math.sqrt(0.5)))
        act = (up * gate).astype(jnp.bfloat16)
        act_out[:, lanes] = act
        slopes.append(gate + up * jnp.exp(-0.5 * up * up) * (1.0 / math.sqrt(2.0 * math.pi)))
        second = second + product(act, down_w[...])
    normal2, scale2 = norm_parts(second)
    out[...] = (normal2 * final_gain + final_shift).astype(jnp.bfloat16)
    cots = cot[...].astype(jnp.float32)
    gsecond = norm_back(normal2, scale2, cots * final_gain)
    gdown = gsecond.astype(jnp.bfloat16)
    gdown_out[...] = gdown
    gfirst = gsecond
    for index, (up_w, down_w) in enumerate(((up_own, down_own), (up_other, down_other))):
        lanes = slice(index * half, (index + 1) * half)
        gup = (product(gdown, down_w[...], NT) * slopes[index]).astype(jnp.bfloat16)
        gup_out[:, lanes] = gup
        up_sums[:, lanes] += column_sum(gup.astype(jnp.float32))
        gfirst = gfirst + product(gup, up_w[...])
    gres = norm_back(normal1, scale1, gfirst * mixer_gain)
    gres_out[...] = gres
    gbranch = gres.astype(jnp.bfloat16)
    gbranch_out[...] = gbranch
    gmixed_out[...] = product(gbranch, wo, NT).astype(jnp.bfloat16)
    sums[0:1, :] += column_sum(gbranch.astype(jnp.float32))
    sums[1:2, :] += column_sum(gfirst * normal1)
    sums[2:3, :] += column_sum(gfirst)
    sums[3:4, :] += column_sum(gdown.astype(jnp.float32))
    sums[4:5, :] += column_sum(cots * normal2)
    sums[5:6, :] += column_sum(cots)


def feed(spots, xs, mixed, cot, up_own, up_other, down_own, down_other, rows, up_bias, pieces):
    tokens, width = xs.shape
    blocks = sum(piece.shape[0] for piece in pieces)
    half = up_own.shape[0]
    hidden = 2 * half
    token = pl.BlockSpec((BLOCK, width), lambda i: (i, 0))
    wide = pl.BlockSpec((BLOCK, hidden), lambda i: (i, 0))

    def whole(shape):
        return pl.BlockSpec(shape, lambda i: (0, 0), pipeline_mode=pl.Buffered(1))

    return pl.pallas_call(
        feed_kernel,
        grid=(tokens // BLOCK,),
        out_shape=(
            SDS((tokens, width), jnp.bfloat16),
            SDS((tokens, hidden), jnp.bfloat16),
            SDS((tokens, hidden), jnp.bfloat16),
            SDS((tokens, width), jnp.bfloat16),
            SDS((tokens, width), jnp.bfloat16),
            SDS((tokens, width), jnp.float32),
            SDS((tokens, width), jnp.bfloat16),
            SDS((tokens, width), jnp.bfloat16),
            SDS((8, width), jnp.float32),
            SDS((1, hidden), jnp.float32),
        ),
        in_specs=[SMEM_SPEC, token, token, token]
        + [whole((half, width))] * 4
        + [whole((8, width)), whole((1, hidden))]
        + [pl.BlockSpec(memory_space=pl.ANY)] * len(pieces),
        out_specs=(token, wide, wide, token, token, token, token, token,
                   pl.BlockSpec((8, width), lambda i: (0, 0)),
                   pl.BlockSpec((1, hidden), lambda i: (0, 0))),
        scratch_shapes=[
            pltpu.VMEM((2, GROUPS, width, 128), jnp.bfloat16),
            pltpu.SemaphoreType.DMA((blocks,)),
        ],
        compiler_params=params(("arbitrary",), 60),
        name="feed",
    )(spots, xs, mixed, cot, up_own, up_other, down_own, down_other, rows, up_bias, *pieces)


def weight_kernel(act, gup, first, gdown, down_out, up_out):
    down_out[...] = product(act[...], gdown[...], TN).astype(jnp.bfloat16)
    up_out[...] = product(gup[...], first[...], TN).astype(jnp.bfloat16)


def feed_weights(act, gup, first, gdown, start, count, chunk):
    tokens, width = first.shape
    base = start // chunk
    full = pl.BlockSpec((tokens, width), lambda i: (0, 0))
    return pl.pallas_call(
        weight_kernel,
        grid=(count // chunk,),
        out_shape=(SDS((count, width), jnp.bfloat16), SDS((count, width), jnp.bfloat16)),
        in_specs=[
            pl.BlockSpec((tokens, chunk), lambda i: (0, base + i)),
            pl.BlockSpec((tokens, chunk), lambda i: (0, base + i)),
            full, full,
        ],
        out_specs=(pl.BlockSpec((chunk, width), lambda i: (i, 0)),) * 2,
        compiler_params=params(("arbitrary",)),
        name="feed_weights",
    )(act, gup, first, gdown)


def out_weight_kernel(spots, mixed, gbranch, own, other, buffer, sems):
    grad = product(mixed[...], gbranch[...], TN).astype(jnp.bfloat16)
    for index in range(GROUPS):
        for half in range(2):
            first = index * LANES + half * 128
            buffer[half, index] = grad[:, first : first + 128]
    run_copies(block_stores(spots, buffer, (own, other), sems, slice(0, GROUPS)))


def out_weights(spots, mixed, gbranch, blocks):
    width = mixed.shape[1]
    shape = SDS((blocks, GROUPS, width // blocks, 128), jnp.bfloat16)
    return pl.pallas_call(
        out_weight_kernel,
        out_shape=(shape, shape),
        in_specs=[SMEM_SPEC] + [VMEM_SPEC] * 2,
        out_specs=(pl.BlockSpec(memory_space=pl.ANY),) * 2,
        scratch_shapes=[
            pltpu.VMEM((2, GROUPS, width, 128), jnp.bfloat16),
            pltpu.SemaphoreType.DMA((2 * blocks,)),
        ],
        compiler_params=params(),
        name="out_weights",
    )(spots, mixed, gbranch)


def attend_back_kernel(spots, xs, mask, bias, q, k, v, gmixed, lse, gres, *rest):
    pieces, rest = rest[:-14], rest[-14:]
    (gx_out, gw_own, gw_other, sums_out, gtable_out,
     probs_low, gscores_low, gdist, gx, gq, weights_all, buffer, sems, out_sems) = rest
    group = pl.program_id(0)
    length = mask.shape[1]
    low = jnp.bfloat16(0)

    @pl.when(group == 0)
    def _():
        gx[...] = gres[...]
        copies = block_copies(spots, pieces, weights_all, sems, slice(0, 3 * GROUPS))
        run_copies(copies)

    keys = k[...]
    values = v[...]
    gk = jnp.zeros((length, LANES), jnp.float32)
    gv = jnp.zeros((length, LANES), jnp.float32)
    for h in range(GROUP):
        gdist[h] = jnp.zeros(gdist.shape[1:], jnp.float32)
        for tile in range(length // TILE):
            first = length - TILE - tile * TILE
            both = None
            for stream in range(2):
                at = stream * length + tile * TILE
                rows = slice(at, at + TILE)
                q_tile = q[rows, :] * jnp.bfloat16(0.125)
                lanes = head_lanes(h, q_tile.shape)
                scores = product(jnp.where(lanes, q_tile, low), keys, NT)
                scores = scores + bias[h, :, first : first + length]
                scores = scores + mask[stream, tile * TILE : (tile + 1) * TILE, :]
                probs = jnp.exp(scores - lse[0, rows, h : h + 1])
                gprobs = product(jnp.where(lanes, gmixed[rows, :], low), values, NT)
                weighted = probs * gprobs
                gscores = weighted - probs * row_sum(weighted)
                probs_low[rows, :] = probs.astype(jnp.bfloat16)
                gscores_low[rows, :] = gscores.astype(jnp.bfloat16)
                both = gscores if both is None else both + gscores
            gdist[h, :, first : first + length] += both
        scaled = q[...] * jnp.bfloat16(0.125)
        lanes = head_lanes(h, scaled.shape)
        key_lanes = head_lanes(h, keys.shape)
        gq_head = product(gscores_low[...], jnp.where(key_lanes, keys, low))
        if h == 0:
            gq[...] = gq_head
        else:
            gq[...] += gq_head
        gk = gk + product(gscores_low[...], jnp.where(lanes, scaled, low), TN)
        gv = gv + product(probs_low[...], jnp.where(lanes, gmixed[...], low), TN)
    gq_low = (gq[...] * 0.125).astype(jnp.bfloat16)
    gk_low = gk.astype(jnp.bfloat16)
    gv_low = gv.astype(jnp.bfloat16)
    for index, grad in enumerate((
        product(xs[...], gq_low, TN),
        product(xs[0:length, :], gk_low, TN),
        product(xs[0:length, :], gv_low, TN),
    )):
        grad = grad.astype(jnp.bfloat16)
        buffer[0, index] = grad[:, :128]
        buffer[1, index] = grad[:, 128:]
    tiles = pl.ds(3 * group, 3)
    run_copies(block_stores(spots, buffer, (gw_own, gw_other), out_sems, tiles))
    sums_out[0:1, :] = column_sum(gq_low.astype(jnp.float32))
    sums_out[1:2, :] = column_sum(gv_low.astype(jnp.float32))
    gx[...] += product(gq_low, joined(weights_all, 3 * group), NT)
    gx[0:length, :] += product(gk_low, joined(weights_all, 3 * group + 1), NT) + product(
        gv_low, joined(weights_all, 3 * group + 2), NT
    )
    span = 2 * length
    pieces = []
    row_index = lax.broadcasted_iota(jnp.int32, (8, span), 0)
    for h in range(GROUP):
        wide = jnp.concatenate([gdist[h], jnp.zeros((TILE, TILE), jnp.float32)], axis=1)
        size = TILE // 2
        while size >= 8:
            wide = wide[size:, :] + pltpu.roll(wide[:size, :], size, 1)
            size //= 2
        for bit in (4, 2, 1):
            wide = jnp.where(row_index & bit == 0, pltpu.roll(wide, bit, 1), wide)
        pieces.append(column_sum(wide))
    pieces.append(jnp.zeros((8 - GROUP, span), jnp.float32))
    onehot = jnp.where(bucket_onehot(length), 1.0, 0.0)
    gtable_out[0] = lax.dot_general(
        jnp.concatenate(pieces, axis=0), onehot, NT, precision=lax.Precision.HIGHEST,
        preferred_element_type=jnp.float32,
    )

    @pl.when(group == GROUPS - 1)
    def _():
        gx_out[...] = gx[...].astype(jnp.bfloat16)


def attend_back(spots, xs, mask, bias, q, k, v, gmixed, lse, gres, pieces, blocks):
    tokens, width = xs.shape
    held = sum(piece.shape[0] for piece in pieces)
    shape = SDS((blocks, 3 * GROUPS, width // blocks, 128), jnp.bfloat16)
    anywhere = pl.BlockSpec(memory_space=pl.ANY)
    length = mask.shape[1]
    full = lambda g: (0, 0)
    column = lambda g: (0, g)
    once = pl.Buffered(1)
    return pl.pallas_call(
        attend_back_kernel,
        grid=(GROUPS,),
        out_shape=(
            SDS((tokens, width), jnp.bfloat16),
            shape,
            shape,
            SDS((8, width), jnp.float32),
            SDS((GROUPS, 8, BUCKETS), jnp.float32),
        ),
        in_specs=[
            SMEM_SPEC,
            pl.BlockSpec((tokens, width), full, pipeline_mode=once),
            pl.BlockSpec((2, length, length), lambda g: (0, 0, 0), pipeline_mode=once),
            pl.BlockSpec((GROUP, TILE, bias.shape[2]), lambda g: (g, 0, 0)),
            pl.BlockSpec((tokens, LANES), column),
            pl.BlockSpec((length, LANES), column),
            pl.BlockSpec((length, LANES), column),
            pl.BlockSpec((tokens, LANES), column),
            pl.BlockSpec((1, tokens, 128), lambda g: (g, 0, 0)),
            pl.BlockSpec((tokens, width), full, pipeline_mode=once),
        ] + [anywhere] * len(pieces),
        out_specs=(
            pl.BlockSpec((tokens, width), full),
            anywhere,
            anywhere,
            pl.BlockSpec((8, LANES), column),
            pl.BlockSpec((1, 8, BUCKETS), lambda g: (g, 0, 0)),
        ),
        scratch_shapes=[
            pltpu.VMEM((tokens, length), jnp.bfloat16),
            pltpu.VMEM((tokens, length), jnp.bfloat16),
            pltpu.VMEM((GROUP, TILE, bias.shape[2]), jnp.float32),
            pltpu.VMEM((tokens, width), jnp.float32),
            pltpu.VMEM((tokens, LANES), jnp.float32),
            pltpu.VMEM((2, 3 * GROUPS, width, 128), jnp.bfloat16),
            pltpu.VMEM((2, 3, width, 128), jnp.bfloat16),
            pltpu.SemaphoreType.DMA((held,)),
            pltpu.SemaphoreType.DMA((2 * blocks,)),
        ],
        compiler_params=params(("arbitrary",)),
        name="attend_back",
    )(spots, xs, mask, bias, q, k, v, gmixed, lse, gres, *pieces)


BOTH = ("dp", "seq")


def xor_pairs(count, by_half):
    halves = len(by_half)
    return [
        (device * halves + half, (device ^ flip) * halves + half)
        for device in range(count)
        for half, flip in enumerate(by_half)
    ]


def swap(value):
    return lax.ppermute(value, "seq", [(0, 1), (1, 0)])


def collect(value, count):
    parts = [value]
    for high in range(1, count // 4):
        parts.append(lax.ppermute(value, BOTH, xor_pairs(count, (4 * high, 4 * high))))
    near = jnp.stack(parts)
    second = lax.ppermute(near, BOTH, xor_pairs(count, (1, 2)))
    third = lax.ppermute(jnp.concatenate([near, second]), BOTH, xor_pairs(count, (2, 1)))
    return near, second, third


def offsets(count, half):
    first = jnp.where(half == 0, 1, 2)
    highs = 4 * jnp.arange(count // 4)
    near = jnp.concatenate([highs, highs ^ first])
    return jnp.concatenate([near, near ^ (3 - first)])


def spread(blocks, count):
    shape = blocks.shape[1:]
    blocks = blocks.reshape((2, 2, count // 4) + shape)
    low = jnp.bfloat16
    wide = jnp.float32
    came = lax.ppermute(blocks[1].astype(low), BOTH, xor_pairs(count, (2, 1)))
    blocks = blocks[0].astype(wide) + came.astype(wide)
    came = lax.ppermute(blocks[1].astype(low), BOTH, xor_pairs(count, (1, 2)))
    blocks = blocks[0].astype(wide) + came.astype(wide)
    total = blocks[0]
    for high in range(1, count // 4):
        came = lax.ppermute(
            blocks[high].astype(low), BOTH, xor_pairs(count, (4 * high, 4 * high))
        )
        total = total + came.astype(wide)
    return total


def reduce_blocks(own, other, count):
    total = spread(own.astype(jnp.float32) + swap(other).astype(jnp.float32), count)
    return total, swap(total)


def in_order(half, own, other):
    return jnp.where(half == 0, jnp.stack([own, other]), jnp.stack([other, own]))


def shards(count, content, query_in, content_cot, query_cot, lengths, order, query_weight,
           query_bias, key_weight, value_weight, value_bias, out_weight, out_bias, mixer_gain,
           mixer_shift, up_weight, up_bias, down_weight, down_bias, final_gain, final_shift,
           position_bias):
    low, wide = jnp.bfloat16, jnp.float32
    _, block, width = content.shape
    length = order.shape[1]
    half = lax.axis_index("seq")
    me = lax.axis_index("dp")
    rows = query_weight.shape[0]
    hidden = up_weight.shape[1]

    square = jnp.stack([query_weight, key_weight, value_weight, out_weight])
    square = square.reshape(4, rows, GROUPS, 2, 128)
    square = lax.dynamic_index_in_dim(square, half, 3, keepdims=False)
    square = jnp.transpose(square, (2, 0, 1, 3))
    square = jnp.concatenate(
        [square[:, :3].reshape(3 * GROUPS, rows, 128), square[:, 3]]
    )
    squares = collect(square, count)
    squares = squares + tuple(swap(piece) for piece in squares)

    vectors = (query_bias, value_bias, out_bias, mixer_gain, mixer_shift, down_bias, final_gain,
               final_shift, up_bias, position_bias)
    packed = jnp.concatenate(vectors)
    packed = lax.all_to_all(
        jnp.broadcast_to(packed[None], (count, packed.shape[0])), "dp", 0, 0, tiled=True
    )
    sizes = [vector.shape[0] for vector in vectors]
    starts = [sum(sizes[:index]) for index in range(len(sizes) + 1)]
    cut = [packed[:, starts[i] : starts[i + 1]] for i in range(len(sizes))]
    flat = [part.reshape(1, -1).astype(wide) for part in cut[:8]]
    table = cut[9].reshape(BUCKETS, HEADS)
    table = jnp.pad(jnp.transpose(table), ((0, 16 - HEADS), (0, 0)))

    mine = [lax.dynamic_index_in_dim(a, half, 0, keepdims=False)
            for a in (content, query_in, content_cot, query_cot)]
    theirs = [lax.dynamic_index_in_dim(a, 1 - half, 0, keepdims=False)
              for a in (content, query_in, content_cot, query_cot)]
    came = swap(jnp.stack(theirs))
    tokens = [jnp.concatenate([mine[i], came[i]]) for i in range(4)]
    pos = lax.rem(jnp.arange(length, dtype=jnp.int32) + half * block, length)
    order_row = lax.dynamic_index_in_dim(order, half, 0, keepdims=False)
    order_row = jnp.where(half == 0, order_row, jnp.roll(order_row, -block))
    bounds = jnp.cumsum(lax.dynamic_index_in_dim(lengths, half, 0, keepdims=False))[:-1]
    xs, cs, mask = sort_rows(bounds.astype(jnp.int32), *tokens, order_row, pos)
    bias = bias_table(table, length)

    flips = offsets(count, half)
    other_flips = offsets(count, 1 - half)
    chips, other_chips = me ^ flips, me ^ other_flips
    aligned = rows % 16 == 0
    if aligned:
        pieces = squares
        spots = jnp.concatenate([chips, other_chips, half[None]]).astype(jnp.int32)
        out_blocks = count
    else:
        pieces = []
        for side, places in ((squares[:3], chips), (squares[3:], other_chips)):
            joint = jnp.concatenate(side)
            ordered = jnp.take(joint, jnp.argsort(places), axis=0)
            ordered = jnp.transpose(ordered, (1, 0, 2, 3)).reshape(1, 4 * GROUPS, width, 128)
            pieces += [ordered, ordered[:0], ordered[:0]]
        pieces = tuple(piece for piece in pieces if piece.shape[0])
        spots = jnp.stack([0 * half, 0 * half, half]).astype(jnp.int32)
        out_blocks = 1

    q, k, v, mixed, lse = attend(spots, xs, mask, bias, flat[0], flat[1], pieces)

    middle = hidden // 2
    up_rows = jnp.transpose(up_weight)
    feed_own = jnp.stack([
        lax.dynamic_slice_in_dim(up_rows, half * middle, middle),
        lax.dynamic_slice_in_dim(down_weight, half * middle, middle),
    ])
    feeds = collect(feed_own, count)
    feeds = jnp.concatenate(feeds)
    feeds_other = swap(feeds)
    ups = [side[:, 0].reshape(count * middle, width) for side in (feeds, feeds_other)]
    downs = [side[:, 1].reshape(count * middle, width) for side in (feeds, feeds_other)]
    bias_parts = cut[8].reshape(count, 2, middle)
    ups_bias = []
    for side, places in ((half, chips), (1 - half, other_chips)):
        chosen = lax.dynamic_index_in_dim(bias_parts, side, 1, keepdims=False)
        pick = (places[:, None] == jnp.arange(count)[None, :]).astype(low)
        ups_bias.append(jnp.dot(pick, chosen, preferred_element_type=wide).reshape(1, -1))
    up_bias_all = jnp.concatenate(ups_bias, axis=1)
    vector_rows = jnp.concatenate(flat[2:8] + [jnp.zeros((2, width), wide)])
    out, act, gup, first, gdown, gres, gbranch, gmixed, sums, up_sums = feed(
        spots, xs, mixed, cs, ups[0], ups[1], downs[0], downs[1], vector_rows, up_bias_all, pieces
    )
    placed = unsort_rows(order_row, out)
    outs = place_rows(half, placed, block)

    share = count * middle
    gdown_other, gup_other = feed_weights(act, gup, first, gdown, share, share, share // 3)
    gdown_own, gup_own = feed_weights(act, gup, first, gdown, 0, share, share // 3)
    fshape = (count, middle, width)
    feed_grads = reduce_blocks(
        jnp.stack([gup_own.reshape(fshape), gdown_own.reshape(fshape)], axis=1),
        jnp.stack([gup_other.reshape(fshape), gdown_other.reshape(fshape)], axis=1),
        count,
    )
    feed_grads = in_order(half, *feed_grads)
    up_grad = jnp.transpose(feed_grads[:, 0].reshape(hidden, width))
    down_grad = feed_grads[:, 1].reshape(hidden, width)

    def by_device(grads):
        if aligned:
            return grads
        result = []
        for grad, places in zip(grads, (chips, other_chips)):
            parts = grad[0].reshape(grad.shape[1], count, rows, 128)
            result.append(jnp.take(jnp.transpose(parts, (1, 0, 2, 3)), places, axis=0))
        return result

    gwo = reduce_blocks(*by_device(out_weights(spots, mixed, gbranch, out_blocks)), count)
    gx, gw_own, gw_other, asums, gtable = attend_back(
        spots, xs, mask, bias, q, k, v, gmixed, lse, gres, pieces, out_blocks
    )
    grads = place_rows(half, unsort_rows(order_row, gx), block)
    gws = reduce_blocks(*by_device((gw_own, gw_other)), count)

    def square_grad(pair, tiles):
        both = in_order(half, pair[0][tiles], pair[1][tiles])
        return jnp.transpose(both, (2, 1, 0, 3)).reshape(rows, width)

    query_grad, key_grad, value_grad = (
        square_grad(gws, slice(index, None, 3)) for index in range(3)
    )
    out_grad = square_grad(gwo, slice(None))

    gtable = jnp.transpose(gtable[:, :GROUP].reshape(HEADS, BUCKETS))
    up_parts = []
    for side, places in ((half, chips), (1 - half, other_chips)):
        pick = (jnp.arange(count)[:, None] == places[None, :]).astype(wide)
        part = lax.dynamic_index_in_dim(
            up_sums.reshape(2, count, middle), jnp.where(side == half, 0, 1), 0, keepdims=False
        )
        up_parts.append(jnp.dot(pick, part, precision=lax.Precision.HIGHEST))
    up_parts = in_order(half, up_parts[0], up_parts[1])
    up_parts = jnp.transpose(up_parts, (1, 0, 2)).reshape(count, hidden)
    shares = [asums[0], asums[1], sums[0], sums[1], sums[2], sums[3], sums[4], sums[5]]
    packed = jnp.concatenate(
        [share.reshape(count, -1) for share in shares]
        + [up_parts, gtable.reshape(count, -1)],
        axis=1,
    )
    packed = jnp.sum(lax.all_to_all(packed, "dp", 0, 0, tiled=True), axis=0)
    packed = packed + swap(packed)
    ends = [packed[starts[i] : starts[i + 1]] for i in range(len(sizes))]
    return (
        outs[0], outs[1], grads[0], grads[1],
        query_grad, ends[0], key_grad, value_grad, ends[1], out_grad, ends[2], ends[3], ends[4],
        up_grad, ends[8], down_grad, ends[5], ends[6], ends[7], ends[9],
    )


def place_rows(half, placed, block):
    came = swap(placed[:, block:])
    own = placed[:, :block]
    return [
        jnp.where(half == 0, jnp.stack([own[i], came[i]]), jnp.stack([came[i], own[i]]))
        for i in range(2)
    ]


def solution(mesh):
    rows3 = P("dp", "seq", None)
    flat, first, last = P("dp"), P("dp", None), P(None, "dp")
    in_specs = (
        rows3, rows3, rows3, rows3, first, first, first, flat, first, first, flat, first, flat,
        flat, flat, last, flat, first, flat, flat, flat, flat,
    )
    out_specs = (
        rows3, rows3, rows3, rows3, first, flat, first, first, flat, first, flat, flat, flat,
        last, flat, first, flat, flat, flat, flat,
    )
    body = functools.partial(shards, mesh.shape["dp"])
    return jax.shard_map(
        body, mesh=mesh, in_specs=in_specs, out_specs=out_specs, check_vma=False
    )
```

time: 1530 us -> 459 us (0.30)
  waiting for transfers between devices: 962 us -> 120 us
  matrix products: 232 us -> 2.49 us
  blocking collectives: 168 us -> 0 us
  Pallas kernels: 0 us -> 162 us
  starting transfers between devices: 1.07 us -> 54.8 us
  other arithmetic: 61.3 us -> 33.5 us
  between operations: 20.1 us -> 2.02 us
    reduce_scatter x8 -> x0, waiting for transfers between devices: 616 us -> none  [the longest x1 177 us: shards(): lax.psum_scatter(grad_down_matrix, 'dp', scatter_dimension=0, tiled=True)]
    dot_general x52 -> x4, matrix products: 232 us -> 2.49 us  [the longest x2 2.24 us: shards(): jnp.dot(pick, chosen, preferred_element_type=wide).reshape(1, -1)]
    unnamed x19 -> x0, waiting for transfers between devices: 187 us -> none
    pallas_call x0 -> x10, Pallas kernels: none -> 162 us  [the longest x1 46.8 us: attend_back(): pl.pallas_call(attend_back_kernel, grid=(GROUPS,), out_shape=(SDS((tokens...]
    all_gather x6 -> x0, waiting for transfers between devices: 159 us -> none  [the longest x1 60.3 us: shards(): lax.all_gather(up_weight, 'dp', axis=1, tiled=True)]
    unnamed x2 -> x0, blocking collectives: 155 us -> none
    ppermute x0 -> x39, waiting for transfers between devices: none -> 118 us  [the longest x3 31.1 us: spread(): came = lax.ppermute(blocks[1].astype(low), BOTH, xor_pairs(count, (2, 1)))]
    ppermute x0 -> x39, starting transfers between devices: none -> 42.9 us  [the longest x6 14.9 us: collect(): lax.ppermute(value, BOTH, xor_pairs(count, (4 * high, 4 * high)))]
  transfers between devices with their start and end apart: 17 -> 41, of which waited for: 10 -> 14; matrix products, arithmetic and copies ran while one was open for 19% -> 21% of each run, Pallas kernels for 0% -> 26%
where the time goes in v1:
time: 459 us; the launch traced here: 451 us
  Pallas kernels  162 us (35%)
  waiting for transfers between devices  120 us (26%)
  local copies, waits for them, and re-layouts  76 us (17%)
  starting transfers between devices  54.8 us (12%)
  other arithmetic  33.5 us (7%)
    pallas_call x1, Pallas kernels, attend_back(): pl.pallas_call(attend_back_kernel, grid=(GROUPS,), out_shape=(SDS((tokens...  46.8 us
    pallas_call x1, Pallas kernels, feed(): pl.pallas_call(feed_kernel, grid=(tokens // BLOCK,), out_shape=(SDS((toke...  37.2 us
    pallas_call x1, Pallas kernels, attend(): pl.pallas_call(attend_kernel, grid=(GROUPS,), out_shape=(SDS((tokens, wid...  36.4 us
    ppermute x3, waiting for transfers between devices, spread(): came = lax.ppermute(blocks[1].astype(low), BOTH, xor_pairs(count, (2, 1)))  31.1 us
    ppermute x9, waiting for transfers between devices, spread(): lax.ppermute(blocks[high].astype(low), BOTH, xor_pairs(count, (4 * high,...  28.8 us
    ppermute x6, waiting for transfers between devices, collect(): lax.ppermute(value, BOTH, xor_pairs(count, (4 * high, 4 * high)))  19.3 us
    pallas_call x2, Pallas kernels, feed_weights(): pl.pallas_call(weight_kernel, grid=(count // chunk,), out_shape=(SDS((cou...  18 us
    ppermute x3, waiting for transfers between devices, spread(): came = lax.ppermute(blocks[1].astype(low), BOTH, xor_pairs(count, (1, 2)))  15.2 us
  transfers between devices with their start and end apart: 41, of which 14 were waited for; matrix products, arithmetic and copies ran while one was open for 21% of the time, Pallas kernels for 26%

profile of v1, /device:TPU:0, one launch (start us, length us, event | category | flops | bytes accessed | tf_op | source)
XLA Modules:
  0.0 450.7 jit_solution(12310357320587340602)
XLA Ops:
  8.3 13.5 %collective-permute-done.10 = bf16[2,96,768]{2,1,0:T(8,128)(2,1)S(1)} collective-permute-done((bf16[2,96,768]{2,1,0:T(8,128)(2,1)S(1)}, bf16[2,96,768]{2,1,0:T(8,128)(2,1)S(1)}, u32[]{:S(2)}, u32[]{:S(2)}) %collective-permute-start.10) | collective-permute-done | bytes 294944 | tf_op jit(solution)/shard_map/ppermute | solution.py:623
  21.8 5.8 %collective-permute-done.11 = bf16[2,96,768]{2,1,0:T(8,128)(2,1)S(1)} collective-permute-done((bf16[2,96,768]{2,1,0:T(8,128)(2,1)S(1)}, bf16[2,96,768]{2,1,0:T(8,128)(2,1)S(1)}, u32[]{:S(2)}, u32[]{:S(2)}) %collective-permute-start.11) | collective-permute-done | bytes 294944 | tf_op jit(solution)/shard_map/ppermute | solution.py:623
  32.8 11.2 %collective-permute-done.12 = bf16[4,2,96,768]{3,2,1,0:T(8,128)(2,1)S(1)} collective-permute-done((bf16[4,2,96,768]{3,2,1,0:T(8,128)(2,1)S(1)}, bf16[4,2,96,768]{3,2,1,0:T(8,128)(2,1)S(1)}, u32[]{:S(2)}, u32[]{:S(2)}) %collective-permute-start.12) | collective-permute-done | bytes 1179680 | tf_op jit(solution)/shard_map/ppermute | solution.py:625
  48.2 7.7 %collective-permute-start.2 = (bf16[12,48,128]{2,1,0:T(8,128)(2,1)}, bf16[12,48,128]{2,1,0:T(8,128)(2,1)S(1)}, u32[]{:S(2)}, u32[]{:S(2)}) collective-permute-start(bf16[12,48,128]{2,1,0:T(8,128)(2,1)} %get-tuple-element.146), channel_id=1, source_target_pairs={{0,16},{1,17},{2,18},{3,19},{4,20},{5,21},{6,22},{7,23},{8,24},{9,... | collective-permute-start | bytes 442376 | tf_op jit(solution)/shard_map/ppermute | solution.py:623
  57.4 6.8 %concatenate.112 = bf16[600]{0:T(1024)(128)(2,1)S(1)} concatenate(bf16[48]{0:T(256)(128)(2,1)} %param.29, bf16[48]{0:T(256)(128)(2,1)} %param.32, bf16[48]{0:T(256)(128)(2,1)} %param.34, bf16[48]{0:T(256)(128)(2,1)} %param.35, bf16[48]{0:T(256)(128)(2,1)} %param.36, bf16[48]{0:T(256)(128)(2,1)} %param.40, bf16[48]{0:T(256)(128)(2,1)} %param.41, bf16[48]{0:T(256)(128)(2,1)} %param.42, ...), dimensions={0} | concatenate | bytes 2400 | tf_op jit(solution)/shard_map/concatenate | solution.py:688
  103.1 9.5 %collective-permute-done.5.rest_2_ = bf16[8,12,48,128]{3,2,1,0:T(8,128)(2,1)S(1)} collective-permute-done((bf16[8,12,48,128]{3,2,1,0:T(8,128)(2,1)}, bf16[8,12,48,128]{3,2,1,0:T(8,128)(2,1)S(1)}, u32[]{:S(2)}, u32[]{:S(2)}) %collective-permute-start.5) | collective-permute-done | bytes 1179680 | tf_op jit(solution)/shard_map/ppermute | solution.py:626
  131.6 4.9 %bias_table.1.bias = f32[12,128,896]{2,1,0:T(8,128)} custom-call(bf16[16,32]{1,0:T(8,128)(2,1)} %pad.4.table), custom_call_target="tpu_custom_call" | custom-call | tf_op jit(solution)/shard_map/bias_table/pallas_call | solution.py:136
  144.9 6.2 %sort_rows.1 = (bf16[1024,768]{1,0:T(8,128)(2,1)}, bf16[1024,768]{1,0:T(8,128)(2,1)}, f32[2,512,512]{2,1,0:T(8,128)}) custom-call(s32[7]{0:T(128)} %slice_bitcast_fusion.26.bounds, bf16[512,768]{1,0:T(8,128)(2,1)} %pad_maximum_fusion.3.content, bf16[512,768]{1,0:T(8,128)(2,1)} %pad_maximum_fusion.4.query, bf16[512,768]{1,0:T(8,128)(2,1)} %pad_maximum_fusion.5.ccot, ...), custom_call_target="tpu_custom_call" | custom-call | tf_op jit(solution)/shard_map/sort_rows/pallas_call | solution.py:76
  152.6 36.4 %attend.1 = (bf16[1024,768]{1,0:T(8,128)(2,1)}, bf16[512,768]{1,0:T(8,128)(2,1)}, bf16[512,768]{1,0:T(8,128)(2,1)}, bf16[1024,768]{1,0:T(8,128)(2,1)}, f32[3,1024,128]{2,1,0:T(8,128)}) custom-call(s32[33]{0:T(128)} %pad_add_fusion.1.spots, bf16[1024,768]{1,0:T(8,128)(2,1)} %get-tuple-element.49.xs, f32[2,512,512]{2,1,0:T(8,128)} %get-tuple-element.50.mask, ...), custom_call_target="tpu_custom_call" | custom-call | tf_op jit(solution)/shard_map/attend/pallas_call | solution.py:252
  189.0 4.8 %fusion.50 = (bf16[16,1,96,768]{3,2,1,0:T(8,128)(2,1)}, bf16[16,1,96,768]{3,2,1,0:T(8,128)(2,1)}) fusion(bf16[16,2,96,768]{3,2,1,0:T(8,128)(2,1)} %constant_dynamic-update-slice_fusion.10), kind=kLoop, calls=%fused_computation.181 | loop fusion | bytes 9437184 | tf_op jit(solution)/shard_map/slice | solution.py:743
  193.9 4.8 %fusion.49 = (bf16[16,1,96,768]{3,2,1,0:T(8,128)(2,1)}, bf16[16,1,96,768]{3,2,1,0:T(8,128)(2,1)}) fusion(bf16[16,2,96,768]{3,2,1,0:T(8,128)(2,1)} %collective-permute-done.14), kind=kLoop, calls=%fused_computation.180 | loop fusion | bytes 9437184 | tf_op jit(solution)/shard_map/slice | solution.py:743
  198.7 37.2 %feed.1 = (bf16[1024,768]{1,0:T(8,128)(2,1)}, bf16[1024,3072]{1,0:T(8,128)(2,1)}, bf16[1024,3072]{1,0:T(8,128)(2,1)}, bf16[1024,768]{1,0:T(8,128)(2,1)}, bf16[10...) custom-call(s32[33]{0:T(128)} %pad_add_fusion.1.spots, ...), custom_call_target="tpu_custom_call" | custom-call | tf_op jit(solution)/shard_map/feed/pallas_call | solution.py:377
  235.9 9.0 %feed_weights.3 = (bf16[1536,768]{1,0:T(8,128)(2,1)}, bf16[1536,768]{1,0:T(8,128)(2,1)}) custom-call(bf16[1024,3072]{1,0:T(8,128)(2,1)} %get-tuple-element.70.act, bf16[1024,3072]{1,0:T(8,128)(2,1)} %get-tuple-element.71.gup, bf16[1024,768]{1,0:T(8,128)(2,1)} %get-tuple-element.72.first, bf16[1024,768]{1,0:T(8,128)(2,1)} %get-tuple-element.73.gdown), custom_call_target="tpu_custom_call" | custom-call | tf_op jit(solution)/shard_map/feed_weights/pallas_call | solution.py:417
  244.9 5.0 %pad_maximum_fusion = bf16[16,2,96,768]{3,2,0,1:T(8,128)(2,1)} fusion(bf16[16,1,96,768]{3,2,0,1:T(8,128)(2,1)} %bitcast.198, bf16[16,1,96,768]{3,2,0,1:T(8,128)(2,1)} %bitcast.199), kind=kLoop, calls=%fused_computation.2 | loop fusion | flops 2359296 | bytes 9437184 | tf_op jit(solution)/shard_map/stack | solution.py:764
  250.3 46.8 %attend_back.1 = (bf16[1024,768]{1,0:T(8,128)(2,1)}, bf16[16,9,48,128]{3,2,1,0:T(8,128)(2,1)}, bf16[16,9,48,128]{3,2,1,0:T(8,128)(2,1)}, f32[8,768]{1,0:T(8,128)}, f32[3,8,32]{2,1,0:T(8,128)}) custom-call(s32[33]{0:T(128)} %pad_add_fusion.1.spots, bf16[1024,768]{1,0:T(8,128)(2,1)} %get-tuple-element.49.xs, f32[2,512,512]{2,1,0:T(8,128)} %get-tuple-element.50.mask, ...), custom_call_target="tpu_custom_call" | custom-call | tf_op jit(solution)/shard_map/attend_back/pallas_call | solution.py:559
  305.1 7.2 %all-to-all-start.1 = ((f32[16,1,600]{2,1,0:T(1,128)}), f32[16,1,600]{2,1,0:T(1,128)}, u32[]{:S(2)}, u32[]{:S(2)}) async-start(f32[16,1,600]{2,1,0:T(1,128)} %copy.114), calls=%async_computation.1 | async-start | bytes 81920 | tf_op jit(solution)/shard_map/all_to_all | solution.py:812
  322.0 9.0 %feed_weights.2 = (bf16[1536,768]{1,0:T(8,128)(2,1)}, bf16[1536,768]{1,0:T(8,128)(2,1)}) custom-call(bf16[1024,3072]{1,0:T(8,128)(2,1)} %get-tuple-element.70.act, bf16[1024,3072]{1,0:T(8,128)(2,1)} %get-tuple-element.71.gup, bf16[1024,768]{1,0:T(8,128)(2,1)} %get-tuple-element.72.first, bf16[1024,768]{1,0:T(8,128)(2,1)} %get-tuple-element.73.gdown), custom_call_target="tpu_custom_call" | custom-call | tf_op jit(solution)/shard_map/feed_weights/pallas_call | solution.py:417
  331.0 4.7 %out_weights.1 = (bf16[16,3,48,128]{3,2,1,0:T(8,128)(2,1)}, bf16[16,3,48,128]{3,2,1,0:T(8,128)(2,1)}) custom-call(s32[33]{0:T(128)} %pad_add_fusion.1.spots, bf16[1024,768]{1,0:T(8,128)(2,1)} %get-tuple-element.51.mixed, bf16[1024,768]{1,0:T(8,128)(2,1)} %get-tuple-element.67.gbranch), custom_call_target="tpu_custom_call" | custom-call | tf_op jit(solution)/shard_map/out_weights/pallas_call | solution.py:444
  336.8 4.7 %convert_add_fusion = f32[16,2,96,768]{3,2,0,1:T(8,128)S(1)} fusion(bf16[16,2,96,768]{3,2,0,1:T(8,128)(2,1)} %collective-permute-done.32, bf16[16,1,96,768]{3,2,0,1:T(8,128)(2,1)S(1)} %bitcast.195, bf16[16,1,96,768]{3,2,0,1:T(8,128)(2,1)} %bitcast.196), kind=kLoop, calls=%fused_computation | loop fusion | flops 9437184 | bytes 18874368 | tf_op jit(solution)/shard_map/add | solution.py:656
  353.0 21.1 %collective-permute-done.26 = bf16[2,4,3,48,128]{4,3,2,1,0:T(8,128)(2,1)S(1)} collective-permute-done((bf16[2,4,3,48,128]{4,3,2,1,0:T(8,128)(2,1)S(1)}, bf16[2,4,3,48,128]{4,3,2,1,0:T(8,128)(2,1)S(1)}, u32[]{:S(2)}, u32[]{:S(2)}) %collective-permute-start.26) | collective-permute-done | bytes 294944 | tf_op jit(solution)/shard_map/ppermute | solution.py:642
  375.2 10.0 %collective-permute-done.18 = bf16[2,4,9,48,128]{4,3,2,1,0:T(8,128)(2,1)S(1)} collective-permute-done((bf16[2,4,9,48,128]{4,3,2,1,0:T(8,128)(2,1)S(1)}, bf16[2,4,9,48,128]{4,3,2,1,0:T(8,128)(2,1)S(1)}, u32[]{:S(2)}, u32[]{:S(2)}) %collective-permute-start.18) | collective-permute-done | bytes 884768 | tf_op jit(solution)/shard_map/ppermute | solution.py:642
  392.4 15.2 %collective-permute-done.19 = bf16[4,9,48,128]{3,2,1,0:T(8,128)(2,1)S(1)} collective-permute-done((bf16[4,9,48,128]{3,2,1,0:T(8,128)(2,1)S(1)}, bf16[4,9,48,128]{3,2,1,0:T(8,128)(2,1)S(1)}, u32[]{:S(2)}, u32[]{:S(2)}) %collective-permute-start.19) | collective-permute-done | bytes 442400 | tf_op jit(solution)/shard_map/ppermute | solution.py:644
  425.4 6.4 %collective-permute-done.37 = bf16[2,96,768]{2,1,0:T(8,128)(2,1)S(1)} collective-permute-done((bf16[2,96,768]{2,1,0:T(8,128)(2,1)S(1)}, bf16[2,96,768]{2,1,0:T(8,128)(2,1)S(1)}, u32[]{:S(2)}, u32[]{:S(2)}) %collective-permute-start.37) | collective-permute-done | bytes 294944 | tf_op jit(solution)/shard_map/ppermute | solution.py:648
  431.8 13.5 %collective-permute-done.36 = bf16[2,96,768]{2,1,0:T(8,128)(2,1)S(1)} collective-permute-done((bf16[2,96,768]{2,1,0:T(8,128)(2,1)S(1)}, bf16[2,96,768]{2,1,0:T(8,128)(2,1)S(1)}, u32[]{:S(2)}, u32[]{:S(2)}) %collective-permute-start.36) | collective-permute-done | bytes 294944 | tf_op jit(solution)/shard_map/ppermute | solution.py:648
  (320 shorter events, 147.2 us)
Async XLA Ops:
  2.6 19.2 %collective-permute-start.10 = (bf16[2,96,768]{2,1,0:T(8,128)(2,1)S(1)}, bf16[2,96,768]{2,1,0:T(8,128)(2,1)S(1)}, u32[]{:S(2)}, u32[]{:S(2)}) collective-permute-start(bf16[2,96,768]{2,1,0:T(8,128)(2,1)S(1)} %get-tuple-element.135), channel_id=1, source_target_pairs={{0,16},{1,17},{2,18},{3,19},{4,20},{5,21},{6,22},{7,23},{8,24},{9,... | collective-permute-start | bytes 884744 | tf_op jit(solution)/shard_map/ppermute | solution.py:623
  8.3 19.3 %collective-permute-start.11 = (bf16[2,96,768]{2,1,0:T(8,128)(2,1)S(1)}, bf16[2,96,768]{2,1,0:T(8,128)(2,1)S(1)}, u32[]{:S(2)}, u32[]{:S(2)}) collective-permute-start(bf16[2,96,768]{2,1,0:T(8,128)(2,1)S(1)} %get-tuple-element.135), channel_id=1, source_target_pairs={{0,24},{1,25},{2,26},{3,27},{4,28},{5,29},{6,30},{7,31},{8,16},{9,... | collective-permute-start | bytes 884744 | tf_op jit(solution)/shard_map/ppermute | solution.py:623
  45.7 33.8 %collective-permute-start.13 = (bf16[8,2,96,768]{3,2,1,0:T(8,128)(2,1)}, bf16[8,2,96,768]{3,2,1,0:T(8,128)(2,1)S(1)}, u32[]{:S(2)}, u32[]{:S(2)}) collective-permute-start(bf16[8,2,96,768]{3,2,1,0:T(8,128)(2,1)} %get-tuple-element.109), channel_id=1, source_target_pairs={{0,4},{1,3},{2,6},{3,1},{4,0},{5,7},{6,2},{7,5},{8,12},{9,11},{10,... | collective-permute-start | bytes 7077896 | tf_op jit(solution)/shard_map/ppermute | solution.py:626
  48.2 35.3 %collective-permute-start.2 = (bf16[12,48,128]{2,1,0:T(8,128)(2,1)}, bf16[12,48,128]{2,1,0:T(8,128)(2,1)S(1)}, u32[]{:S(2)}, u32[]{:S(2)}) collective-permute-start(bf16[12,48,128]{2,1,0:T(8,128)(2,1)} %get-tuple-element.146), channel_id=1, source_target_pairs={{0,16},{1,17},{2,18},{3,19},{4,20},{5,21},{6,22},{7,23},{8,24},{9,... | collective-permute-start | bytes 442376 | tf_op jit(solution)/shard_map/ppermute | solution.py:623
  55.9 27.6 %collective-permute-start.1 = (bf16[12,48,128]{2,1,0:T(8,128)(2,1)}, bf16[12,48,128]{2,1,0:T(8,128)(2,1)}, u32[]{:S(2)}, u32[]{:S(2)}) collective-permute-start(bf16[12,48,128]{2,1,0:T(8,128)(2,1)} %get-tuple-element.146), channel_id=1, source_target_pairs={{0,8},{1,9},{2,10},{3,11},{4,12},{5,13},{6,14},{7,15},{8,0},{9,1},... | collective-permute-start | bytes 442376 | tf_op jit(solution)/shard_map/ppermute | solution.py:623
  55.9 27.6 %collective-permute-start.3 = (bf16[12,48,128]{2,1,0:T(8,128)(2,1)}, bf16[12,48,128]{2,1,0:T(8,128)(2,1)}, u32[]{:S(2)}, u32[]{:S(2)}) collective-permute-start(bf16[12,48,128]{2,1,0:T(8,128)(2,1)} %get-tuple-element.146), channel_id=1, source_target_pairs={{0,24},{1,25},{2,26},{3,27},{4,28},{5,29},{6,30},{7,31},{8,16},{9,... | collective-permute-start | bytes 442376 | tf_op jit(solution)/shard_map/ppermute | solution.py:623
  68.9 31.7 %all-to-all-start = ((bf16[16,2,300]{2,1,0:T(2,128)(2,1)}), bf16[16,2,300]{2,1,0:T(2,128)(2,1)}, u32[]{:S(2)}, u32[]{:S(2)}) async-start(bf16[16,2,300]{2,1,0:T(2,128)(2,1)} %reshape.489), calls=%async_computation | async-start | bytes 49152 | tf_op jit(solution)/shard_map/all_to_all | solution.py:689
  78.6 61.0 %collective-permute-start = (bf16[4,256,768]{2,1,0:T(8,128)(2,1)}, bf16[4,256,768]{2,1,0:T(8,128)(2,1)}, u32[]{:S(2)}, u32[]{:S(2)}) collective-permute-start(bf16[4,256,768]{2,1,0:T(8,128)(2,1)} %pad_maximum_fusion.1), channel_id=1, source_target_pairs={{0,1},{1,0},{2,3},{3,2},{4,5},{5,4},{6,7},{7,6},{8,9},{9,8},{10,11... | collective-permute-start | bytes 4718600 | tf_op jit(solution)/shard_map/ppermute | solution.py:617
  81.2 112.6 %collective-permute-start.14 = (bf16[16,2,96,768]{3,2,1,0:T(8,128)(2,1)}, bf16[16,2,96,768]{3,2,1,0:T(8,128)(2,1)}, u32[]{:S(2)}, u32[]{:S(2)}) collective-permute-start(bf16[16,2,96,768]{3,2,1,0:T(8,128)(2,1)} %constant_dynamic-update-slice_fusion.10), channel_id=1, source_target_pairs={{0,1},{1,0},{2,3},{3,2},{4,5},{5,4},{6,7},{7,6},{8,9},{9,8},{10,11... | collective-permute-start | bytes 14155784 | tf_op jit(solution)/shard_map/ppermute | solution.py:617
  112.6 38.6 %collective-permute-start.8 = (bf16[8,12,48,128]{3,2,1,0:T(8,128)(2,1)S(1)}, bf16[8,12,48,128]{3,2,1,0:T(8,128)(2,1)S(1)}, u32[]{:S(2)}, u32[]{:S(2)}) collective-permute-start(bf16[8,12,48,128]{3,2,1,0:T(8,128)(2,1)S(1)} %collective-permute-done.5.rest_2_), channel_id=1, source_target_pairs={{0,1},{1,0},{2,3},{3,2},{4,5},{5,4},{6,7},{7,6},{8,9},{9,8},{10,11... | collective-permute-start | bytes 3538952 | tf_op jit(solution)/shard_map/ppermute | solution.py:617
  249.9 86.9 %collective-permute-start.32 = (bf16[16,2,96,768]{3,2,0,1:T(8,128)(2,1)}, bf16[16,2,96,768]{3,2,0,1:T(8,128)(2,1)}, u32[]{:S(2)}, u32[]{:S(2)}) collective-permute-start(bf16[16,2,96,768]{3,2,0,1:T(8,128)(2,1)} %pad_maximum_fusion), channel_id=1, source_target_pairs={{0,1},{1,0},{2,3},{3,2},{4,5},{5,4},{6,7},{7,6},{8,9},{9,8},{10,11... | collective-permute-start | bytes 14155784 | tf_op jit(solution)/shard_map/ppermute | solution.py:617
  312.3 33.9 %collective-permute-start.17 = (bf16[16,9,48,128]{3,2,1,0:T(8,128)(2,1)}, bf16[16,9,48,128]{3,2,1,0:T(8,128)(2,1)}, u32[]{:S(2)}, u32[]{:S(2)}) collective-permute-start(bf16[16,9,48,128]{3,2,1,0:T(8,128)(2,1)} %get-tuple-element.62), channel_id=1, source_target_pairs={{0,1},{1,0},{2,3},{3,2},{4,5},{5,4},{6,7},{7,6},{8,9},{9,8},{10,11... | collective-permute-start | bytes 5308424 | tf_op jit(solution)/shard_map/ppermute | solution.py:617
  342.1 43.8 %collective-permute-start.33 = (bf16[2,4,2,96,768]{4,3,2,1,0:T(8,128)(2,1)S(1)}, bf16[2,4,2,96,768]{4,3,2,1,0:T(8,128)(2,1)S(1)}, u32[]{:S(2)}, u32[]{:S(2)}) collective-permute-start(bf16[2,4,2,96,768]{4,3,2,1,0:T(8,128)(2,1)S(1)} %copy.118), channel_id=1, source_target_pairs={{0,4},{1,3},{2,6},{3,1},{4,0},{5,7},{6,2},{7,5},{8,12},{9,11},{10,... | collective-permute-start | bytes 7077896 | tf_op jit(solution)/shard_map/ppermute | solution.py:642
  344.9 29.3 %collective-permute-start.26 = (bf16[2,4,3,48,128]{4,3,2,1,0:T(8,128)(2,1)S(1)}, bf16[2,4,3,48,128]{4,3,2,1,0:T(8,128)(2,1)S(1)}, u32[]{:S(2)}, u32[]{:S(2)}) collective-permute-start(bf16[2,4,3,48,128]{4,3,2,1,0:T(8,128)(2,1)S(1)} %bitcast.210), channel_id=1, source_target_pairs={{0,4},{1,3},{2,6},{3,1},{4,0},{5,7},{6,2},{7,5},{8,12},{9,11},{10,... | collective-permute-start | bytes 884744 | tf_op jit(solution)/shard_map/ppermute | solution.py:642
  348.8 36.4 %collective-permute-start.18 = (bf16[2,4,9,48,128]{4,3,2,1,0:T(8,128)(2,1)S(1)}, bf16[2,4,9,48,128]{4,3,2,1,0:T(8,128)(2,1)S(1)}, u32[]{:S(2)}, u32[]{:S(2)}) collective-permute-start(bf16[2,4,9,48,128]{4,3,2,1,0:T(8,128)(2,1)S(1)} %bitcast.205), channel_id=1, source_target_pairs={{0,4},{1,3},{2,6},{3,1},{4,0},{5,7},{6,2},{7,5},{8,12},{9,11},{10,... | collective-permute-start | bytes 2654216 | tf_op jit(solution)/shard_map/ppermute | solution.py:642
  386.6 22.0 %collective-permute-start.34 = (bf16[4,2,96,768]{3,2,1,0:T(8,128)(2,1)S(1)}, bf16[4,2,96,768]{3,2,1,0:T(8,128)(2,1)S(1)}, u32[]{:S(2)}, u32[]{:S(2)}) collective-permute-start(bf16[4,2,96,768]{3,2,1,0:T(8,128)(2,1)S(1)} %fusion.1), channel_id=1, source_target_pairs={{0,2},{1,5},{2,0},{3,7},{4,6},{5,1},{6,4},{7,3},{8,10},{9,13},{10,... | collective-permute-start | bytes 3538952 | tf_op jit(solution)/shard_map/ppermute | solution.py:644
  387.5 20.1 %collective-permute-start.19 = (bf16[4,9,48,128]{3,2,1,0:T(8,128)(2,1)S(1)}, bf16[4,9,48,128]{3,2,1,0:T(8,128)(2,1)S(1)}, u32[]{:S(2)}, u32[]{:S(2)}) collective-permute-start(bf16[4,9,48,128]{3,2,1,0:T(8,128)(2,1)S(1)} %fusion.6), channel_id=1, source_target_pairs={{0,2},{1,5},{2,0},{3,7},{4,6},{5,1},{6,4},{7,3},{8,10},{9,13},{10,... | collective-permute-start | bytes 1327112 | tf_op jit(solution)/shard_map/ppermute | solution.py:644
  388.9 22.3 %collective-permute-start.28 = (bf16[3,48,128]{2,1,0:T(8,128)(2,1)S(1)}, bf16[3,48,128]{2,1,0:T(8,128)(2,1)S(1)}, u32[]{:S(2)}, u32[]{:S(2)}) collective-permute-start(bf16[3,48,128]{2,1,0:T(8,128)(2,1)S(1)} %get-tuple-element.142), channel_id=1, source_target_pairs={{0,8},{1,9},{2,10},{3,11},{4,12},{5,13},{6,14},{7,15},{8,0},{9,1},... | collective-permute-start | bytes 110600 | tf_op jit(solution)/shard_map/ppermute | solution.py:648
  389.7 22.1 %collective-permute-start.30 = (bf16[3,48,128]{2,1,0:T(8,128)(2,1)S(1)}, bf16[3,48,128]{2,1,0:T(8,128)(2,1)S(1)}, u32[]{:S(2)}, u32[]{:S(2)}) collective-permute-start(bf16[3,48,128]{2,1,0:T(8,128)(2,1)S(1)} %get-tuple-element.143), channel_id=1, source_target_pairs={{0,24},{1,25},{2,26},{3,27},{4,28},{5,29},{6,30},{7,31},{8,16},{9,... | collective-permute-start | bytes 110600 | tf_op jit(solution)/shard_map/ppermute | solution.py:648
  391.8 21.6 %collective-permute-start.29 = (bf16[3,48,128]{2,1,0:T(8,128)(2,1)S(1)}, bf16[3,48,128]{2,1,0:T(8,128)(2,1)S(1)}, u32[]{:S(2)}, u32[]{:S(2)}) collective-permute-start(bf16[3,48,128]{2,1,0:T(8,128)(2,1)S(1)} %get-tuple-element.144), channel_id=1, source_target_pairs={{0,16},{1,17},{2,18},{3,19},{4,20},{5,21},{6,22},{7,23},{8,24},{9,... | collective-permute-start | bytes 110600 | tf_op jit(solution)/shard_map/ppermute | solution.py:648
  413.5 18.3 %collective-permute-start.37 = (bf16[2,96,768]{2,1,0:T(8,128)(2,1)S(1)}, bf16[2,96,768]{2,1,0:T(8,128)(2,1)S(1)}, u32[]{:S(2)}, u32[]{:S(2)}) collective-permute-start(bf16[2,96,768]{2,1,0:T(8,128)(2,1)S(1)} %get-tuple-element.107), channel_id=1, source_target_pairs={{0,24},{1,25},{2,26},{3,27},{4,28},{5,29},{6,30},{7,31},{8,16},{9,... | collective-permute-start | bytes 884744 | tf_op jit(solution)/shard_map/ppermute | solution.py:648
  416.3 28.9 %collective-permute-start.36 = (bf16[2,96,768]{2,1,0:T(8,128)(2,1)S(1)}, bf16[2,96,768]{2,1,0:T(8,128)(2,1)S(1)}, u32[]{:S(2)}, u32[]{:S(2)}) collective-permute-start(bf16[2,96,768]{2,1,0:T(8,128)(2,1)S(1)} %get-tuple-element.108), channel_id=1, source_target_pairs={{0,16},{1,17},{2,18},{3,19},{4,20},{5,21},{6,22},{7,23},{8,24},{9,... | collective-permute-start | bytes 884744 | tf_op jit(solution)/shard_map/ppermute | solution.py:648
  417.0 28.5 %collective-permute-start.31 = (f32[3,48,128]{2,1,0:T(8,128)S(1)}, f32[3,48,128]{2,1,0:T(8,128)S(1)}, u32[]{:S(2)}, u32[]{:S(2)}) collective-permute-start(f32[3,48,128]{2,1,0:T(8,128)S(1)} %fusion.23), channel_id=1, source_target_pairs={{0,1},{1,0},{2,3},{3,2},{4,5},{5,4},{6,7},{7,6},{8,9},{9,8},{10,11... | collective-permute-start | bytes 221192 | tf_op jit(solution)/shard_map/ppermute | solution.py:617
  421.2 24.3 %collective-permute-start.23 = (f32[9,48,128]{2,1,0:T(8,128)S(1)}, f32[9,48,128]{2,1,0:T(8,128)S(1)}, u32[]{:S(2)}, u32[]{:S(2)}) collective-permute-start(f32[9,48,128]{2,1,0:T(8,128)S(1)} %fusion.11), channel_id=1, source_target_pairs={{0,1},{1,0},{2,3},{3,2},{4,5},{5,4},{6,7},{7,6},{8,9},{9,8},{10,11... | collective-permute-start | bytes 663560 | tf_op jit(solution)/shard_map/ppermute | solution.py:617
  (60 other events, 492.5 us)

commit v2 on v1

v2 whole, which is shorter than its diff:
```python
import functools
import math

import jax
import jax.numpy as jnp
from jax import lax
from jax.experimental import pallas as pl
from jax.experimental.pallas import tpu as pltpu
from jax.sharding import PartitionSpec as P

HEADS = 12
HEAD_DIM = 64
BUCKETS = 32
GROUP = 4
LANES = GROUP * HEAD_DIM
GROUPS = HEADS // GROUP
TILE = 128
TILES = 4
NEG = -1e30
FLOOR = -1e29
EPS = 1e-05

limits = (1, 2, 3, 4, 5, 6, 7, 8, 12, 16, 23, 32, 46, 64, 91)

NN = (((1,), (0,)), ((), ()))
NT = (((1,), (1,)), ((), ()))
TN = (((0,), (0,)), ((), ()))
VMEM_SPEC = pl.BlockSpec(memory_space=pltpu.VMEM)
HBM_SPEC = pl.BlockSpec(memory_space=pltpu.HBM)
SCALE = 1.6e6
SMEM_SPEC = pl.BlockSpec(memory_space=pltpu.SMEM)
SDS = jax.ShapeDtypeStruct


def cost(micros):
    return pl.CostEstimate(
        flops=0, bytes_accessed=int(micros * SCALE), transcendentals=0
    )


def product(left, right, dims=NN):
    return lax.dot_general(left, right, dims, preferred_element_type=jnp.float32)


def params(semantics=None, limit=56):
    return pltpu.CompilerParams(dimension_semantics=semantics, vmem_limit_bytes=limit << 20)


def row_sum(values):
    return jnp.sum(values, axis=-1, keepdims=True)


ME, HALF = 0, 1
VECTORS, UP_SLOT, TABLE_SLOT = 10, 8, 9
VECTOR_TILE = 4 * GROUPS
GRAD_TILES = VECTOR_TILE + 1
FULL = 60


def in_hbm(*values):
    return [pltpu.with_memory_space_constraint(value, pltpu.HBM) for value in values]


def run_copies(copies):
    for copy in copies:
        copy.start()
    for copy in copies:
        copy.wait()


def pack_kernel(ids, content, query, ccot, qcot, wq, wk, wv, wo, up, down, *rest):
    vectors, rest = rest[:VECTORS], rest[VECTORS:]
    (theirs, square, feed, slots, tokens, squares, feeds, turned, in_sems, out_sems) = rest
    half = ids[HALF]
    share = feed.shape[1]
    loads = []

    def load(source, target):
        copy = pltpu.make_async_copy(source, target, in_sems.at[len(loads)])
        copy.start()
        loads.append(copy)

    for index, weight in enumerate((wq, wk, wv, wo)):
        for group in range(GROUPS):
            lane = pl.multiple_of(group * LANES + half * 128, 128)
            place = 3 * group + index if index < 3 else 3 * GROUPS + group
            load(weight.at[:, pl.ds(lane, 128)], squares.at[place])
    for index, source in enumerate((content, query, ccot, qcot)):
        load(source.at[1 - half], tokens.at[index])
    rows = pl.ds(pl.multiple_of(half * share, share), share)
    load(down.at[rows, :], feeds)
    turned[...] = jnp.transpose(up[...].astype(jnp.float32)).astype(jnp.bfloat16)
    slots[...] = jnp.zeros_like(slots)
    for index, vector in enumerate(vectors):
        slots[index : index + 1, : vector.shape[1]] = vector[...]
    for copy in loads[: 4 * GROUPS]:
        copy.wait()
    stores = [
        pltpu.make_async_copy(squares, square, out_sems.at[0]),
        pltpu.make_async_copy(turned.at[rows, :], feed.at[0], out_sems.at[1]),
        pltpu.make_async_copy(tokens, theirs, out_sems.at[2]),
        pltpu.make_async_copy(feeds, feed.at[1], out_sems.at[3]),
    ]
    stores[0].start()
    stores[1].start()
    for copy in loads[4 * GROUPS :]:
        copy.wait()
    stores[2].start()
    stores[3].start()
    for copy in stores:
        copy.wait()


def pack(ids, content, query, ccot, qcot, wq, wk, wv, wo, up, down, vectors):
    _, block, width = content.shape
    rows = wq.shape[0]
    hidden = up.shape[1]
    return pl.pallas_call(
        pack_kernel,
        out_shape=(
            SDS((4, block, width), jnp.bfloat16),
            SDS((4 * GROUPS, rows, 128), jnp.bfloat16),
            SDS((2, hidden // 2, width), jnp.bfloat16),
            SDS((16, 256), jnp.bfloat16),
        ),
        in_specs=[SMEM_SPEC] + [HBM_SPEC] * 8 + [VMEM_SPEC, HBM_SPEC] + [VMEM_SPEC] * VECTORS,
        out_specs=(HBM_SPEC,) * 3 + (VMEM_SPEC,),
        scratch_shapes=[
            pltpu.VMEM((4, block, width), jnp.bfloat16),
            pltpu.VMEM((4 * GROUPS, rows, 128), jnp.bfloat16),
            pltpu.VMEM((hidden // 2, width), jnp.bfloat16),
            pltpu.VMEM((hidden, width), jnp.bfloat16),
            pltpu.SemaphoreType.DMA((4 * GROUPS + 5,)),
            pltpu.SemaphoreType.DMA((4,)),
        ],
        cost_estimate=cost(4),
        compiler_params=params(None, FULL),
        name="pack",
    )(ids, *in_hbm(content, query, ccot, qcot, wq, wk, wv, wo), up, *in_hbm(down),
      *(vector.reshape(1, -1) for vector in vectors))


def order_onehot(ids, order):
    length = order.shape[1]
    row = order[pl.ds(ids[HALF], 1), :]
    down = lax.broadcasted_iota(jnp.int32, (length, length), 0)
    return jnp.where(row == down, 1.0, 0.0).astype(jnp.bfloat16)


def sort_kernel(ids, lengths, content, query, ccot, qcot, came, order,
                xs_out, cs_out, mask_out, held, sems):
    length = order.shape[1]
    block = content.shape[1]
    half = ids[HALF]
    copies = []
    for index, source in enumerate((content, query, ccot, qcot)):
        for place, rows in ((half, source.at[half]), (1 - half, came.at[index])):
            here = pl.ds(pl.multiple_of(place * block, block), block)
            copies.append(
                pltpu.make_async_copy(rows, held.at[index, here], sems.at[len(copies)])
            )
    for copy in copies:
        copy.start()
    onehot = order_onehot(ids, order)
    lane = lax.broadcasted_iota(jnp.int32, (8, length), 1)
    line = lax.broadcasted_iota(jnp.int32, (8, length), 0)
    digits = jnp.where(line == 0, lane // 16, jnp.where(line == 1, lane % 16, 0))
    digits = product(digits.astype(jnp.float32).astype(jnp.bfloat16), onehot, NT)
    rank_row = digits[0:1, :] * 16.0 + digits[1:2, :]
    across = lax.broadcasted_iota(jnp.int32, (length, length), 1).astype(jnp.float32)
    rank_col = row_sum(onehot.astype(jnp.float32) * across)
    place_col = lax.broadcasted_iota(jnp.int32, (length, 1), 0)
    place_row = lax.broadcasted_iota(jnp.int32, (1, length), 1)
    segment_col = jnp.zeros((length, 1), jnp.int32)
    segment_row = jnp.zeros((1, length), jnp.int32)
    bound = jnp.int32(0)
    for index in range(lengths.shape[1] - 1):
        bound = bound + lengths[half, index]
        segment_col = segment_col + (place_col >= bound).astype(jnp.int32)
        segment_row = segment_row + (place_row >= bound).astype(jnp.int32)
    same = segment_col == segment_row
    mask_out[0] = jnp.where(same & (rank_row <= rank_col), 0.0, NEG).astype(jnp.bfloat16)
    mask_out[1] = jnp.where(same & (rank_row < rank_col), 0.0, NEG).astype(jnp.bfloat16)
    for copy in copies:
        copy.wait()
    for source, target, at in ((0, xs_out, 0), (1, xs_out, 1), (2, cs_out, 0), (3, cs_out, 1)):
        target[at * length : (at + 1) * length, :] = product(onehot, held[source]).astype(
            jnp.bfloat16
        )


def sort_rows(ids, lengths, tokens, came, order):
    length = order.shape[1]
    width = came.shape[2]
    return pl.pallas_call(
        sort_kernel,
        out_shape=(
            SDS((2 * length, width), jnp.bfloat16),
            SDS((2 * length, width), jnp.bfloat16),
            SDS((2, length, length), jnp.bfloat16),
        ),
        in_specs=[SMEM_SPEC] * 2 + [HBM_SPEC] * 5 + [VMEM_SPEC],
        out_specs=(VMEM_SPEC,) * 3,
        scratch_shapes=[
            pltpu.VMEM((4, length, width), jnp.bfloat16),
            pltpu.SemaphoreType.DMA((8,)),
        ],
        cost_estimate=cost(5),
        compiler_params=params(None, FULL),
        name="sort_rows",
    )(ids, lengths, *in_hbm(*tokens, came), order)


def put_back(ids, onehot, source, scratch, own, send, sems):
    length = onehot.shape[0]
    block = own.shape[1]
    for stream in range(2):
        rows = product(onehot, source(stream), TN).astype(jnp.bfloat16)
        scratch[0, stream] = rows[:block, :]
        scratch[1, stream] = rows[block:, :]
    run_copies([
        pltpu.make_async_copy(scratch.at[ids[HALF]], own, sems.at[0]),
        pltpu.make_async_copy(scratch.at[1 - ids[HALF]], send, sems.at[1]),
    ])


def unsort_kernel(ids, order, values, own, send, held, scratch, sems):
    length = order.shape[1]
    copy = pltpu.make_async_copy(values, held, sems.at[2])
    copy.start()
    onehot = order_onehot(ids, order)
    copy.wait()
    put_back(
        ids, onehot, lambda s: held[s * length : (s + 1) * length, :], scratch, own, send, sems
    )


def unsort_rows(ids, order, values):
    length = order.shape[1]
    width = values.shape[1]
    shape = SDS((2, length // 2, width), jnp.bfloat16)
    return pl.pallas_call(
        unsort_kernel,
        out_shape=(shape, shape),
        in_specs=[SMEM_SPEC, VMEM_SPEC, HBM_SPEC],
        out_specs=(HBM_SPEC, HBM_SPEC),
        scratch_shapes=[
            pltpu.VMEM((2 * length, width), jnp.bfloat16),
            pltpu.VMEM((2, 2, length // 2, width), jnp.bfloat16),
            pltpu.SemaphoreType.DMA((3,)),
        ],
        cost_estimate=cost(3),
        compiler_params=params(None, FULL),
        name="unsort_rows",
    )(ids, order, *in_hbm(values))


SPAN = 5 * TILE
TURN = 6 * TILE


def bucket_onehot():
    distance = lax.broadcasted_iota(jnp.int32, (BUCKETS, TURN), 1) - (3 * TILE - 1)
    magnitude = jnp.abs(distance)
    counted = jnp.zeros(distance.shape, jnp.int32)
    for limit in limits:
        counted = counted + (magnitude >= limit).astype(jnp.int32)
    bucket = counted + 16 * (distance > 0).astype(jnp.int32)
    return bucket == lax.broadcasted_iota(jnp.int32, distance.shape, 0)


def block_flip(ids, own, far, block, count):
    place = ids[HALF] if own else 1 - ids[HALF]
    first = jnp.where(place == 0, 1, 2)
    high = count // 2
    flip = jnp.int32(4 * (block % high))
    if block >= high:
        flip = flip ^ first
    return flip ^ (3 - first) if far else flip


def block_places(ids, pieces):
    places = []
    for index, piece in enumerate(pieces):
        own = index < len(pieces) // 2
        place = ids[HALF] if own else 1 - ids[HALF]
        for block in range(piece.shape[0]):
            if len(pieces) == 2:
                places.append((index, block, place, 0))
            else:
                flip = block_flip(ids, own, index % 2 == 1, block, piece.shape[0])
                places.append((index, block, place, ids[ME] ^ flip))
    return places


def block_copies(ids, pieces, target, sems, tiles):
    copies = []
    for index, block, place, chip in block_places(ids, pieces):
        rows = pieces[index].shape[2]
        here = pl.ds(pl.multiple_of(chip * rows, rows), rows)
        copies.append(
            pltpu.make_async_copy(
                pieces[index].at[block, tiles], target.at[place, :, here, :],
                sems.at[len(copies)],
            )
        )
    return copies


def block_stores(ids, source, outs, sems, tiles):
    copies = []
    for index, block, place, chip in block_places(ids, outs):
        rows = outs[index].shape[2]
        here = pl.ds(pl.multiple_of(chip * rows, rows), rows)
        copies.append(
            pltpu.make_async_copy(
                source.at[place, :, here, :], outs[index].at[block, tiles],
                sems.at[len(copies)],
            )
        )
    return copies


def joined(weights, index):
    return jnp.concatenate([weights[0, index], weights[1, index]], axis=1)


def store_shapes(pieces, tiles):
    return tuple(SDS((p.shape[0], tiles) + p.shape[2:], jnp.bfloat16) for p in pieces)


def vectors_kernel(width, sizes, ids, near, far, rows_out, up_out, bias_out):
    count = 2 * near.shape[0]
    half = ids[HALF]
    high = count // 4
    total = jnp.zeros((16, width), jnp.float32)
    table = jnp.zeros((16, width), jnp.float32)
    blank = jnp.zeros((16, width - 256), jnp.float32)
    slot = lax.broadcasted_iota(jnp.int32, (16, width), 0)
    blocks = [[], []]
    for side, part in enumerate((near, far)):
        for block in range(part.shape[0]):
            chip = ids[ME] ^ block_flip(ids, True, side == 1, block, part.shape[0])
            values = jnp.concatenate([part[block].astype(jnp.float32), blank], axis=1)
            blocks[side].append(values)
            total = total + pltpu.roll(
                jnp.where(slot < UP_SLOT, values, 0.0), chip * sizes[0], 1
            )
            table = table + pltpu.roll(
                jnp.where(slot == TABLE_SLOT, values, 0.0), chip * sizes[TABLE_SLOT], 1
            )
    rows_out[...] = total[2:10, :]
    rows_out[6:8, :] = total[0:2, :]
    share = sizes[UP_SLOT] // 2
    lane = lax.broadcasted_iota(jnp.int32, (16, width), 1)
    keep = (slot == UP_SLOT) & (lane < share)
    near_blocks, far_blocks = blocks
    order = (
        (half, near_blocks[:high] + near_blocks[high:]),
        (1 - half, near_blocks[:high] + far_blocks[:high]),
        (half, far_blocks[:high] + far_blocks[high:]),
        (1 - half, near_blocks[high:] + far_blocks[high:]),
    )
    for index, (place, parts) in enumerate(order):
        joint = jnp.zeros((16, width), jnp.float32)
        for block, values in enumerate(parts):
            values = pltpu.roll(values, lax.rem(width - place * share, width), 1)
            joint = joint + pltpu.roll(jnp.where(keep, values, 0.0), block * share, 1)
        up_out[:, index * width : (index + 1) * width] = joint[UP_SLOT : UP_SLOT + 1, :]
    flat = table[TABLE_SLOT : TABLE_SLOT + 1, : BUCKETS * HEADS]
    entry = lax.broadcasted_iota(jnp.int32, (16, BUCKETS * HEADS), 1)
    head = lax.broadcasted_iota(jnp.int32, (16, BUCKETS * HEADS), 0)
    spread_heads = jnp.where(entry % HEADS == head, flat, 0.0).astype(jnp.bfloat16)
    place = lax.broadcasted_iota(jnp.int32, (BUCKETS, BUCKETS * HEADS), 1) // HEADS
    bucket = lax.broadcasted_iota(jnp.int32, (BUCKETS, BUCKETS * HEADS), 0)
    folded = product(spread_heads, jnp.where(place == bucket, 1.0, 0.0).astype(jnp.bfloat16), NT)
    onehot = jnp.where(bucket_onehot(), 1.0, 0.0).astype(jnp.bfloat16)
    rows = product(folded.astype(jnp.bfloat16), onehot)
    for head in range(HEADS):
        spread = jnp.broadcast_to(rows[head : head + 1, :], (TILE, TURN))
        turned = pltpu.roll(spread, TURN - (TILE - 1), 1, stride=1, stride_axis=0)
        bias_out[head] = turned[:, :SPAN].astype(jnp.bfloat16)


def vectors_to_all(ids, near, far, width, sizes):
    return pl.pallas_call(
        functools.partial(vectors_kernel, width, sizes),
        out_shape=(
            SDS((8, width), jnp.float32),
            SDS((1, 4 * width), jnp.float32),
            SDS((HEADS, TILE, SPAN), jnp.bfloat16),
        ),
        in_specs=[SMEM_SPEC] + [VMEM_SPEC] * 2,
        out_specs=(VMEM_SPEC,) * 3,
        cost_estimate=cost(6),
        compiler_params=params(None, FULL),
        name="vectors",
    )(ids, near, far)


def head_lanes(head, shape):
    lane = lax.broadcasted_iota(jnp.int32, shape, 1)
    return (lane >= head * HEAD_DIM) & (lane < (head + 1) * HEAD_DIM)


def head_stack(values):
    low = jnp.zeros((), values.dtype)
    return jnp.concatenate(
        [jnp.where(head_lanes(h, values.shape), values, low) for h in range(GROUP)]
    )


def head_merge(stack, rows):
    total = stack[(GROUP - 1) * rows :, :]
    for h in range(GROUP - 1):
        part = stack[h * rows : (h + 1) * rows, :]
        total = jnp.where(head_lanes(h, part.shape), part, total)
    return total


def widen(values, lanes):
    return jnp.concatenate([values] * (lanes // 128), axis=1)


def by_width(ids, lengths, tile, body):
    half = ids[HALF]
    begin, end = tile * TILE, (tile + 1) * TILE
    bound = jnp.int32(0)
    low, high = jnp.int32(0), jnp.int32(TILES * TILE)
    for index in range(lengths.shape[1] - 1):
        bound = bound + lengths[half, index]
        low = jnp.where(bound <= begin, bound, low)
        high = jnp.where(bound >= end, jnp.minimum(bound, high), high)
    first = low // TILE
    width = jnp.maximum((high + TILE - 1) // TILE - first, 2)
    first = pl.multiple_of(jnp.minimum(first, TILES - width) * TILE, TILE)
    for count in range(2, TILES + 1):
        pl.when(width == count)(functools.partial(body, first, count * TILE))


def attend_kernel(ids, lengths, xs, mask, bias, rows, *rest):
    pieces, rest = rest[:-8], rest[-8:]
    q_out, k_out, v_out, mixed_out, lse_out, weights, values, sems = rest
    length = mask.shape[1]
    group = pl.program_id(0)

    def weight_copies(index):
        tiles = pl.ds(3 * index, 3)
        return block_copies(ids, pieces, weights.at[:, tiles], sems.at[index], tiles)

    @pl.when(group == 0)
    def _():
        for index in range(GROUPS):
            for copy in weight_copies(index):
                copy.start()

    for index in range(GROUPS):
        @pl.when(group == index)
        def _():
            for copy in weight_copies(index):
                copy.wait()

    q = product(xs[...], joined(weights, 3 * group)) + rows[6:7, :]
    q_out[...] = q.astype(jnp.bfloat16)
    k = product(xs[0:length, :], joined(weights, 3 * group + 1))
    k_out[...] = k.astype(jnp.bfloat16)
    v = product(xs[0:length, :], joined(weights, 3 * group + 2)) + rows[7:8, :]
    v_out[...] = v.astype(jnp.bfloat16)

    wide_lanes = lax.broadcasted_iota(jnp.int32, v.shape, 1) < 128
    one = jnp.ones((), jnp.bfloat16)
    values[0] = jnp.where(wide_lanes, v_out[...], one)
    values[1] = jnp.where(wide_lanes, one, v_out[...])

    def tile_step(tile, carry):
        def body(first, keys):
            there = pl.ds(first, keys)
            near = pl.ds(pl.multiple_of((2 - tile) * TILE + first, TILE), keys)
            here = pl.ds(pl.multiple_of(tile * TILE, TILE), TILE)
            key = k_out[there, :]
            for stream in range(2):
                at = pl.ds(pl.multiple_of(stream * length + tile * TILE, TILE), TILE)
                scores = product(head_stack(q_out[at, :] * jnp.bfloat16(0.125)), key, NT)
                masked = mask[stream, here, there].astype(jnp.float32)
                weights, peaks, logs = [], [], []
                for h in range(GROUP):
                    part = scores[h * TILE : (h + 1) * TILE, :] + bias[h, :, near].astype(jnp.float32) + masked
                    peak = jnp.maximum(jnp.max(part, axis=-1, keepdims=True), FLOOR)
                    weights.append(jnp.exp(part - peak).astype(jnp.bfloat16))
                    peaks.append(peak)
                for pair in range(2):
                    both = jnp.concatenate(weights[2 * pair : 2 * pair + 2])
                    both = product(both, values[pair, there, :])
                    top = slice(pair * 128, pair * 128 + 128)
                    low = slice(128 - pair * 128, 256 - pair * 128)
                    parts = []
                    for h in range(2):
                        rows = slice(h * TILE, (h + 1) * TILE)
                        summed = both[rows, low]
                        alive = summed > 0
                        inverse = jnp.where(alive, 1.0 / summed, 0.0)
                        parts.append(both[rows, top] * inverse)
                        logs.append(
                            jnp.where(alive, peaks[2 * pair + h] + jnp.log(summed), 0.0)
                        )
                    lane = lax.broadcasted_iota(jnp.int32, parts[0].shape, 1)
                    mixed = jnp.where(lane < HEAD_DIM, parts[0], parts[1])
                    mixed_out[at, top] = mixed.astype(jnp.bfloat16)
                packed = logs[0]
                for h in range(1, GROUP):
                    packed = jnp.where(lane == h, logs[h], packed)
                lse_out[0, at, :] = packed

        by_width(ids, lengths, tile, body)
        return carry

    lax.fori_loop(0, length // TILE, tile_step, 0)


def attend(ids, lengths, xs, mask, bias, rows, pieces):
    tokens, width = xs.shape
    length = mask.shape[1]
    blocks = sum(piece.shape[0] for piece in pieces)
    full = lambda g: (0, 0)
    column = lambda g: (0, g)
    once = pl.Buffered(1)
    return pl.pallas_call(
        attend_kernel,
        grid=(GROUPS,),
        out_shape=(
            SDS((tokens, width), jnp.bfloat16),
            SDS((length, width), jnp.bfloat16),
            SDS((length, width), jnp.bfloat16),
            SDS((tokens, width), jnp.bfloat16),
            SDS((GROUPS, tokens, 128), jnp.float32),
        ),
        in_specs=[
            SMEM_SPEC,
            SMEM_SPEC,
            pl.BlockSpec((tokens, width), full, pipeline_mode=once),
            pl.BlockSpec((2, length, length), lambda g: (0, 0, 0), pipeline_mode=once),
            pl.BlockSpec((GROUP, TILE, SPAN), lambda g: (g, 0, 0)),
            pl.BlockSpec((8, LANES), column),
        ] + [HBM_SPEC] * len(pieces),
        out_specs=(
            pl.BlockSpec((tokens, LANES), column),
            pl.BlockSpec((length, LANES), column),
            pl.BlockSpec((length, LANES), column),
            pl.BlockSpec((tokens, LANES), column),
            pl.BlockSpec((1, tokens, 128), lambda g: (g, 0, 0)),
        ),
        scratch_shapes=[
            pltpu.VMEM((2, 3 * GROUPS, width, 128), jnp.bfloat16),
            pltpu.VMEM((2, length, LANES), jnp.bfloat16),
            pltpu.SemaphoreType.DMA((GROUPS, blocks)),
        ],
        cost_estimate=cost(18),
        compiler_params=params(("arbitrary",), FULL),
        name="attend",
    )(ids, lengths, xs, mask, bias, rows, *in_hbm(*pieces))


def norm_parts(values):
    mean = jnp.mean(values, axis=-1, keepdims=True)
    center = values - mean
    spread = jnp.mean(center * center, axis=-1, keepdims=True)
    scale = lax.rsqrt(spread + EPS)
    return center * scale, scale


def norm_back(normal, scale, grad):
    mean = jnp.mean(grad, axis=-1, keepdims=True)
    inner = jnp.mean(grad * normal, axis=-1, keepdims=True)
    return scale * (grad - mean - normal * inner)


def column_sum(values):
    return jnp.sum(values, axis=0, keepdims=True)


BLOCK = 256


def feed_kernel(ids, xs, mixed, cot, rows, up_bias, near_own, near_other, far_own, far_other,
                *rest):
    pieces, rest = rest[:-14], rest[-14:]
    (out, act_out, gup_out, first_out, gdown_out, gres_out, gbranch_out, gmixed_out,
     sums, up_sums, up_all, down_all, wo_all, sems) = rest
    step = pl.program_id(0)
    units = up_all.shape[0] // 4
    parts = (near_own, near_other, far_own, far_other)

    @pl.when(step == 0)
    def _():
        sums[...] = jnp.zeros_like(sums)
        up_sums[...] = jnp.zeros_like(up_sums)
        copies = block_copies(ids, pieces, wo_all, sems, slice(3 * GROUPS, 4 * GROUPS))
        share = near_own.shape[2]
        for index, part in enumerate(parts):
            for block in range(part.shape[0]):
                here = slice(index * units + block * share, index * units + (block + 1) * share)
                for which, target in ((0, up_all), (1, down_all)):
                    copies.append(
                        pltpu.make_async_copy(
                            part.at[block, which], target.at[here, :], sems.at[len(copies)]
                        )
                    )
        run_copies(copies)

    wo = jnp.concatenate([joined(wo_all, index) for index in range(GROUPS)], axis=1)
    branch = product(mixed[...], wo) + rows[0:1, :]
    normal1, scale1 = norm_parts(xs[...].astype(jnp.float32) + branch)
    first = normal1 * rows[1:2, :] + rows[2:3, :]
    first_low = first.astype(jnp.bfloat16)
    first_out[...] = first_low
    slopes = []
    second = first + rows[3:4, :]
    for index in range(2):
        here = slice(2 * index * units, 2 * (index + 1) * units)
        up = product(first_low, up_all[here, :], NT) + up_bias[:, here]
        gate = 0.5 + 0.5 * lax.erf(up * math.sqrt(0.5))
        act = (up * gate).astype(jnp.bfloat16)
        act_out[:, here] = act
        slopes.append(gate + up * jnp.exp(-0.5 * up * up) * (1.0 / math.sqrt(2.0 * math.pi)))
        second = second + product(act, down_all[here, :])
    normal2, scale2 = norm_parts(second)
    gain = rows[4:5, :]
    out[...] = (normal2 * gain + rows[5:6, :]).astype(jnp.bfloat16)
    cots = cot[...].astype(jnp.float32)
    gsecond = norm_back(normal2, scale2, cots * gain)
    gdown = gsecond.astype(jnp.bfloat16)
    gdown_out[...] = gdown
    gfirst = gsecond
    for index in range(2):
        here = slice(2 * index * units, 2 * (index + 1) * units)
        gup = (product(gdown, down_all[here, :], NT) * slopes[index]).astype(jnp.bfloat16)
        gup_out[:, here] = gup
        up_sums[:, here] += column_sum(gup.astype(jnp.float32))
        gfirst = gfirst + product(gup, up_all[here, :])
    gres = norm_back(normal1, scale1, gfirst * rows[1:2, :])
    gres_out[...] = gres
    gbranch = gres.astype(jnp.bfloat16)
    gbranch_out[...] = gbranch
    gmixed_out[...] = product(gbranch, wo, NT).astype(jnp.bfloat16)
    sums[0:1, :] += column_sum(gbranch.astype(jnp.float32))
    sums[1:2, :] += column_sum(gfirst * normal1)
    sums[2:3, :] += column_sum(gfirst)
    sums[3:4, :] += column_sum(gdown.astype(jnp.float32))
    sums[4:5, :] += column_sum(cots * normal2)
    sums[5:6, :] += column_sum(cots)


def feed(ids, xs, mixed, cot, rows, up_bias, feeds, pieces):
    tokens, width = xs.shape
    hidden = up_bias.shape[1]
    token = pl.BlockSpec((BLOCK, width), lambda i: (i, 0))
    wide = pl.BlockSpec((BLOCK, hidden), lambda i: (i, 0))
    held = sum(piece.shape[0] for piece in pieces) + 2 * sum(part.shape[0] for part in feeds)
    low = SDS((tokens, width), jnp.bfloat16)
    return pl.pallas_call(
        feed_kernel,
        grid=(tokens // BLOCK,),
        out_shape=(
            low,
            SDS((tokens, hidden), jnp.bfloat16),
            SDS((tokens, hidden), jnp.bfloat16),
            low,
            low,
            SDS((tokens, width), jnp.float32),
            low,
            low,
            SDS((8, width), jnp.float32),
            SDS((1, hidden), jnp.float32),
        ),
        in_specs=[
            SMEM_SPEC, token, token, token,
            pl.BlockSpec((8, width), lambda i: (0, 0)),
            pl.BlockSpec((1, hidden), lambda i: (0, 0)),
        ] + [HBM_SPEC] * (4 + len(pieces)),
        out_specs=(token, wide, wide, token, token, token, token, token,
                   pl.BlockSpec((8, width), lambda i: (0, 0)),
                   pl.BlockSpec((1, hidden), lambda i: (0, 0))),
        scratch_shapes=[
            pltpu.VMEM((hidden, width), jnp.bfloat16),
            pltpu.VMEM((hidden, width), jnp.bfloat16),
            pltpu.VMEM((2, GROUPS, width, 128), jnp.bfloat16),
            pltpu.SemaphoreType.DMA((held,)),
        ],
        cost_estimate=cost(36),
        compiler_params=params(("arbitrary",), FULL),
        name="feed",
    )(ids, xs, mixed, cot, rows, up_bias, *in_hbm(*feeds, *pieces))


def feed_weights_kernel(act, gup, first, gdown, own, other):
    which = pl.program_id(1)

    def put(grad):
        share = own.shape[2]
        grad = grad.astype(jnp.bfloat16)

        def store(out):
            for block in range(out.shape[0]):
                out[block, 0] = grad[block * share : (block + 1) * share, :]

        pl.when(pl.program_id(0) == 0)(lambda: store(other))
        pl.when(pl.program_id(0) == 1)(lambda: store(own))

    pl.when(which == 0)(lambda: put(product(gup[...], first[...], TN)))
    pl.when(which == 1)(lambda: put(product(act[...], gdown[...], TN)))


def feed_weights(part, act, gup, first, gdown, shape):
    tokens, width = first.shape
    units = shape[0] * shape[2]
    full = pl.BlockSpec((tokens, width), lambda s, u: (0, 0), pipeline_mode=pl.Buffered(1))
    lanes = pl.BlockSpec((tokens, units), lambda s, u: (0, 2 * part + 1 - s))
    block = (shape[0], 1) + shape[2:]
    return pl.pallas_call(
        feed_weights_kernel,
        grid=(2, 2),
        out_shape=(SDS(shape, jnp.bfloat16),) * 2,
        in_specs=[lanes, lanes, full, full],
        out_specs=(
            pl.BlockSpec(block, lambda s, u: (0, s * u, 0, 0)),
            pl.BlockSpec(block, lambda s, u: (0, jnp.maximum(s, u), 0, 0)),
        ),
        cost_estimate=cost(9),
        compiler_params=params(("arbitrary", "arbitrary"), FULL),
        name="feed_weights",
    )(act, gup, first, gdown)


def out_weights_kernel(ids, mixed, gbranch, *rest):
    outs, (buffer, sems) = rest[:-2], rest[-2:]
    grad = product(mixed[...], gbranch[...], TN).astype(jnp.bfloat16)
    for index in range(GROUPS):
        for half in range(2):
            lane = index * LANES + half * 128
            buffer[half, index] = grad[:, lane : lane + 128]
    run_copies(block_stores(ids, buffer, outs, sems, slice(3 * GROUPS, 4 * GROUPS)))


def out_weights(ids, mixed, gbranch, pieces):
    tokens, width = mixed.shape
    blocks = sum(piece.shape[0] for piece in pieces)
    full = pl.BlockSpec((tokens, width), lambda i: (0, 0))
    return pl.pallas_call(
        out_weights_kernel,
        grid=(1,),
        out_shape=store_shapes(pieces, GRAD_TILES),
        in_specs=[SMEM_SPEC, full, full],
        out_specs=(HBM_SPEC,) * len(pieces),
        scratch_shapes=[
            pltpu.VMEM((2, GROUPS, width, 128), jnp.bfloat16),
            pltpu.SemaphoreType.DMA((blocks,)),
        ],
        cost_estimate=cost(4),
        compiler_params=params(("arbitrary",), FULL),
        name="out_weights",
    )(ids, mixed, gbranch)


def attend_back_kernel(ids_rows, ids, lengths, order, mask, bias, q, k, v, mixed, gmixed, lse, sums,
                       up_sums, xs_far, gres, *rest):
    scratch = rest[-17:]
    count = (len(rest) - 17 - 2) // 3
    pieces = rest[:count]
    own, send, *gw_outs = rest[2 * count : -17]
    (vectors, turned, vector_sems, gk, gv, gdist, gx, gq, inner, weights, buffer, xs, rows_out, sems, in_sems, out_sems,
     row_sems) = scratch
    group = pl.program_id(0)
    length = mask.shape[1]
    rows = xs.shape[1] // (2 * gw_outs[0].shape[0]) if count > 2 else ids_rows
    loads = block_copies(ids, pieces, weights, sems, slice(0, 3 * GROUPS)) + [
        pltpu.make_async_copy(xs_far, xs, in_sems.at[0]),
        pltpu.make_async_copy(gres, gx, in_sems.at[1]),
    ]

    def stores(index):
        slot = index % 2
        return block_stores(
            ids, buffer.at[slot], gw_outs, out_sems.at[slot], pl.ds(3 * index, 3)
        )

    @pl.when(group == 0)
    def _():
        for copy in loads:
            copy.start()

    gdist[...] = jnp.zeros_like(gdist)
    gk[...] = jnp.zeros_like(gk)
    gv[...] = jnp.zeros_like(gv)

    lane = lax.broadcasted_iota(jnp.int32, (LANES, GROUP * 128), 0) // HEAD_DIM
    head = lax.broadcasted_iota(jnp.int32, (LANES, GROUP * 128), 1) // 128
    adder = jnp.where(lane == head, 1.0, 0.0).astype(jnp.bfloat16)
    crossed = mixed[...].astype(jnp.float32) * gmixed[...].astype(jnp.float32)
    inner[...] = product(crossed.astype(jnp.bfloat16), adder)

    def tile_step(tile, carry):
        def body(first, keys):
            there = pl.ds(first, keys)
            near = pl.ds(pl.multiple_of((2 - tile) * TILE + first, TILE), keys)
            here = pl.ds(pl.multiple_of(tile * TILE, TILE), TILE)
            key = k[there, :]
            value = v[there, :]
            at = [
                pl.ds(pl.multiple_of(stream * length + tile * TILE, TILE), TILE)
                for stream in range(2)
            ]
            query = jnp.concatenate([head_stack(q[at[s], :] * jnp.bfloat16(0.125)) for s in range(2)])
            gmix = jnp.concatenate([head_stack(gmixed[at[s], :]) for s in range(2)])
            scores = product(query, key, NT)
            gprobs = product(gmix, value, NT)
            masked = [mask[s, here, there].astype(jnp.float32) for s in range(2)]
            probs_low = [None] * (2 * GROUP)
            gscores_low = [None] * (2 * GROUP)
            for h in range(GROUP):
                both = None
                near_bias = bias[h, :, near].astype(jnp.float32)
                for stream in range(2):
                    index = stream * GROUP + h
                    part = slice(index * TILE, (index + 1) * TILE)
                    score = scores[part, :] + near_bias + masked[stream]
                    probs = jnp.exp(score - lse[0, at[stream], h : h + 1])
                    lanes = slice(h * 128, (h + 1) * 128)
                    gscores = probs * (gprobs[part, :] - widen(inner[at[stream], lanes], keys))
                    probs_low[index] = probs.astype(jnp.bfloat16)
                    gscores_low[index] = gscores.astype(jnp.bfloat16)
                    both = gscores if both is None else both + gscores
                gdist[h, :, near] += both
            probs_low = jnp.concatenate(probs_low)
            gscores_low = jnp.concatenate(gscores_low)
            gv[there, :] += product(probs_low, gmix, TN)
            gk[there, :] += product(gscores_low, query, TN)
            back = product(gscores_low, key)
            for stream in range(2):
                part = slice(stream * GROUP * TILE, (stream + 1) * GROUP * TILE)
                gq[at[stream], :] = head_merge(back[part, :], TILE)

        by_width(ids, lengths, tile, body)
        return carry

    lax.fori_loop(0, length // TILE, tile_step, 0)
    gq_low = (gq[...] * 0.125).astype(jnp.bfloat16)
    gk_low = gk[...].astype(jnp.bfloat16)
    gv_low = gv[...].astype(jnp.bfloat16)

    @pl.when(group == 0)
    def _():
        for copy in loads:
            copy.wait()

    @pl.when(group == 2)
    def _():
        for copy in stores(0):
            copy.wait()

    slot = lax.rem(group, 2)
    for index, grad in enumerate((
        product(xs[...], gq_low, TN),
        product(xs[0:length, :], gk_low, TN),
        product(xs[0:length, :], gv_low, TN),
    )):
        grad = grad.astype(jnp.bfloat16)
        buffer[slot, 0, index] = grad[:, :128]
        buffer[slot, 1, index] = grad[:, 128:]
    for index in range(GROUPS):
        @pl.when(group == index)
        def _():
            for copy in stores(index):
                copy.start()

    gx[...] += product(gq_low, joined(weights, 3 * group), NT)
    gx[0:length, :] += product(gk_low, joined(weights, 3 * group + 1), NT) + product(
        gv_low, joined(weights, 3 * group + 2), NT
    )
    lanes = pl.ds(pl.multiple_of(group * LANES, LANES), LANES)
    vectors[0:1, lanes] = column_sum(gq_low.astype(jnp.float32))
    vectors[1:2, lanes] = column_sum(gv_low.astype(jnp.float32))
    span = TURN
    pieces_sum = []
    row_index = lax.broadcasted_iota(jnp.int32, (8, span), 0)
    for h in range(GROUP):
        wide = jnp.concatenate([gdist[h], jnp.zeros((TILE, TILE), jnp.float32)], axis=1)
        size = TILE // 2
        while size >= 8:
            wide = wide[size:, :] + pltpu.roll(wide[:size, :], size, 1)
            size //= 2
        for bit in (4, 2, 1):
            wide = jnp.where(row_index & bit == 0, pltpu.roll(wide, bit, 1), wide)
        pieces_sum.append(column_sum(wide))
    pieces_sum.append(jnp.zeros((8 - GROUP, span), jnp.float32))
    onehot = jnp.where(bucket_onehot(), 1.0, 0.0)
    by_bucket = lax.dot_general(
        jnp.concatenate(pieces_sum, axis=0), onehot, NT, precision=lax.Precision.HIGHEST,
        preferred_element_type=jnp.float32,
    )
    width = xs.shape[1]
    parts = width // rows
    each = BUCKETS * HEADS // parts
    lane = lax.broadcasted_iota(jnp.int32, (BUCKETS, width), 1)
    entry = lane // rows * each + lane % rows
    bucket = lax.broadcasted_iota(jnp.int32, (BUCKETS, width), 0)
    chosen = (entry // HEADS == bucket) & (lane % rows < each)
    table = lax.dot_general(
        by_bucket, jnp.where(chosen, 1.0, 0.0), NN, precision=lax.Precision.HIGHEST,
        preferred_element_type=jnp.float32,
    )
    head = lax.broadcasted_iota(jnp.int32, table.shape, 0)
    lane = lax.broadcasted_iota(jnp.int32, table.shape, 1)
    entry = lane // rows * each + lane % rows
    right = (head < GROUP) & (entry % HEADS == GROUP * group + head)
    table = column_sum(jnp.where(right, table, 0.0))

    @pl.when(group == 0)
    def _():
        vectors[12:13, :] = table

    @pl.when(group > 0)
    def _():
        vectors[12:13, :] += table

    @pl.when(group == GROUPS - 1)
    def _():
        put_back(
            ids, order_onehot(ids, order),
            lambda s: gx[s * length : (s + 1) * length, :].astype(jnp.bfloat16),
            rows_out, own, send, row_sems,
        )
        vectors[2:8, :] = sums[0:6, :]
        vectors[8:12, :] = up_slots(ids, up_sums, rows, parts // 2)
        vectors[13:, :] = jnp.zeros((128 - 13, width), jnp.float32)
        tile = jnp.transpose(vectors[...]).astype(jnp.bfloat16)
        turned[0, 0] = tile
        turned[1, 0] = tile
        last = block_stores(
            ids, turned, gw_outs, vector_sems, slice(VECTOR_TILE, VECTOR_TILE + 1)
        )
        for copy in last:
            copy.start()
        for copy in stores(1) + stores(2) + last:
            copy.wait()


def up_slots(ids, up_sums, rows, blocks):
    width = up_sums.shape[1] // 4
    share = 2 * rows
    slot = lax.broadcasted_iota(jnp.int32, (8, width), 0)
    lane = lax.broadcasted_iota(jnp.int32, (8, width), 1)
    total = jnp.zeros((8, width), jnp.float32)
    for index in range(4):
        own = index % 2 == 0
        place = ids[HALF] if own else 1 - ids[HALF]
        part = jnp.broadcast_to(up_sums[:, index * width : (index + 1) * width], (8, width))
        for block in range(blocks):
            chip = ids[ME] ^ block_flip(ids, own, index >= 2, block, blocks)
            for quarter in range(2):
                shift = (width - block * share - quarter * rows) % width
                values = pltpu.roll(part, shift, 1) if shift else part
                keep = (lane < rows) & (slot == 2 * place + quarter)
                total = total + pltpu.roll(jnp.where(keep, values, 0.0), chip * rows, 1)
    return total[0:4, :]


def attend_back(ids, lengths, order, xs, mask, bias, q, k, v, mixed, gmixed, lse, sums, up_sums,
                gres, pieces, grads, rows_each):
    tokens, width = xs.shape
    length = mask.shape[1]
    blocks = sum(piece.shape[0] for piece in pieces)
    column = lambda g: (0, g)
    rows = SDS((2, length // 2, width), jnp.bfloat16)
    first = 15 + len(pieces)
    return pl.pallas_call(
        functools.partial(attend_back_kernel, rows_each),
        grid=(GROUPS,),
        out_shape=(
            rows,
            rows,
        ) + store_shapes(pieces, GRAD_TILES),
        input_output_aliases={first + index: 2 + index for index in range(len(pieces))},
        in_specs=[
            SMEM_SPEC,
            SMEM_SPEC,
            VMEM_SPEC,
            pl.BlockSpec((2, length, length), lambda g: (0, 0, 0), pipeline_mode=pl.Buffered(1)),
            pl.BlockSpec((GROUP, TILE, SPAN), lambda g: (g, 0, 0)),
            pl.BlockSpec((tokens, LANES), column),
            pl.BlockSpec((length, LANES), column),
            pl.BlockSpec((length, LANES), column),
            pl.BlockSpec((tokens, LANES), column),
            pl.BlockSpec((tokens, LANES), column),
            pl.BlockSpec((1, tokens, 128), lambda g: (g, 0, 0)),
            pl.BlockSpec((8, width), lambda g: (0, 0)),
            pl.BlockSpec((1, 4 * width), lambda g: (0, 0)),
        ] + [HBM_SPEC] * (2 + 2 * len(pieces)),
        out_specs=(HBM_SPEC,) * (2 + len(pieces)),
        scratch_shapes=[
            pltpu.VMEM((128, width), jnp.float32),
            pltpu.VMEM((2, 1, width, 128), jnp.bfloat16),
            pltpu.SemaphoreType.DMA((blocks,)),
            pltpu.VMEM((length, LANES), jnp.float32),
            pltpu.VMEM((length, LANES), jnp.float32),
            pltpu.VMEM((GROUP, TILE, SPAN), jnp.float32),
            pltpu.VMEM((tokens, width), jnp.float32),
            pltpu.VMEM((tokens, LANES), jnp.float32),
            pltpu.VMEM((tokens, GROUP * 128), jnp.float32),
            pltpu.VMEM((2, 3 * GROUPS, width, 128), jnp.bfloat16),
            pltpu.VMEM((2, 2, 3, width, 128), jnp.bfloat16),
            pltpu.VMEM((tokens, width), jnp.bfloat16),
            pltpu.VMEM((2, 2, length // 2, width), jnp.bfloat16),
            pltpu.SemaphoreType.DMA((blocks,)),
            pltpu.SemaphoreType.DMA((2,)),
            pltpu.SemaphoreType.DMA((2, blocks)),
            pltpu.SemaphoreType.DMA((2,)),
        ],
        cost_estimate=cost(27),
        compiler_params=params(("arbitrary",), FULL),
        name="attend_back",
    )(ids, lengths, order, mask, bias, q, k, v, mixed, gmixed, lse, sums, up_sums,
      *in_hbm(xs, gres, *pieces, *grads))


def finish_kernel(ids, own, came, wq, wk, wv, wo, *vectors):
    half = ids[HALF]
    for place in range(2):
        mine = half == place
        for index, out in enumerate((wq, wk, wv, wo)):
            for group in range(GROUPS):
                tile = 3 * group + index if index < 3 else 3 * GROUPS + group
                lane = group * LANES + place * 128
                out[:, lane : lane + 128] = jnp.where(mine, own[tile], came[tile])
    turned = jnp.transpose(own[VECTOR_TILE])
    rows = own.shape[1]
    for index, out in enumerate(vectors):
        if index == UP_SLOT:
            for quarter in range(4):
                out[:, quarter * rows : (quarter + 1) * rows] = turned[8 + quarter : 9 + quarter, :]
        else:
            at = 12 if index == TABLE_SLOT else index
            out[...] = turned[at : at + 1, : out.shape[1]]


def finish(ids, own, came, sizes):
    rows = own.shape[1]
    width = LANES * GROUPS
    outs = (SDS((rows, width), jnp.float32),) * 4
    outs += tuple(SDS((1, size), jnp.float32) for size in sizes)
    return pl.pallas_call(
        finish_kernel,
        out_shape=outs,
        in_specs=[SMEM_SPEC, VMEM_SPEC, VMEM_SPEC],
        out_specs=(VMEM_SPEC,) * len(outs),
        cost_estimate=cost(2),
        compiler_params=params(None, FULL),
        name="finish",
    )(ids, own, came)


BOTH = ("dp", "seq")


def xor_pairs(count, by_half):
    halves = len(by_half)
    return [
        (device * halves + half, (device ^ flip) * halves + half)
        for device in range(count)
        for half, flip in enumerate(by_half)
    ]


def swap(value):
    return lax.ppermute(value, "seq", [(0, 1), (1, 0)])


def high_parts(value, count):
    return [
        lax.ppermute(value, BOTH, xor_pairs(count, (4 * high, 4 * high)))
        for high in range(1, count // 4)
    ]


def low_round(value, count):
    return jnp.concatenate([value, lax.ppermute(value, BOTH, xor_pairs(count, (1, 2)))])


def last_round(value, count):
    return lax.ppermute(value, BOTH, xor_pairs(count, (2, 1)))


def offsets(count, half):
    first = jnp.where(half == 0, 1, 2)
    highs = 4 * jnp.arange(count // 4)
    near = jnp.concatenate([highs, highs ^ first])
    return jnp.concatenate([near, near ^ (3 - first)])


def after(value, *others):
    return lax.optimization_barrier((value,) + others)[0]


def wide(value):
    return value.astype(jnp.float32)


def low(value):
    return value.astype(jnp.bfloat16)


def in_order(half, own, other):
    return jnp.where(half == 0, jnp.stack([own, other]), jnp.stack([other, own]))


def shards(count, content, query_in, content_cot, query_cot, lengths, order, query_weight,
           query_bias, key_weight, value_weight, value_bias, out_weight, out_bias, mixer_gain,
           mixer_shift, up_weight, up_bias, down_weight, down_bias, final_gain, final_shift,
           position_bias):
    _, block, width = content.shape
    length = order.shape[1]
    half = lax.axis_index("seq")
    me = lax.axis_index("dp")
    rows = query_weight.shape[0]
    hidden = up_weight.shape[1]
    share = hidden // 2
    near_count = count // 2

    ids = jnp.stack([me, half]).astype(jnp.int32)
    vectors = (query_bias, value_bias, out_bias, mixer_gain, mixer_shift, down_bias, final_gain,
               final_shift, up_bias, position_bias)
    sizes = [vector.shape[0] for vector in vectors]
    theirs, square, feed_own, slots = pack(
        ids, content, query_in, content_cot, query_cot, query_weight, key_weight, value_weight,
        out_weight, up_weight, down_weight, vectors,
    )

    square_parts = high_parts(square, count)
    slots_high = jnp.stack([slots] + high_parts(slots, count))
    came = swap(theirs)
    xs, cs, mask = sort_rows(
        ids, lengths, (content, query_in, content_cot, query_cot), came, order
    )
    square_parts = lax.optimization_barrier((square_parts, xs, slots_high))[0]
    square_near = low_round(jnp.stack([square] + square_parts), count)
    feed_own = after(feed_own, square_parts)
    feed_parts = high_parts(feed_own, count)
    slots_near = low_round(slots_high, count)
    square_near = after(square_near, slots_near)
    square_far = last_round(square_near, count)
    slots_far = last_round(slots_near, count)
    near_swapped = swap(square_near)
    square_far = after(square_far, slots_far, near_swapped)
    far_swapped = swap(square_far)
    feed_parts = lax.optimization_barrier((feed_parts, square_far))[0]
    feed_near = low_round(jnp.stack([feed_own] + feed_parts), count)
    vector_rows, up_biases, bias = vectors_to_all(ids, slots_near, slots_far, width, sizes)
    feed_near = after(feed_near, far_swapped, bias)
    pieces = (square_near, square_far, near_swapped, far_swapped)

    flips = offsets(count, half)
    other_flips = offsets(count, 1 - half)
    chips, other_chips = me ^ flips, me ^ other_flips
    aligned = rows % 16 == 0
    if not aligned:
        ordered = []
        for side, places in ((pieces[:2], chips), (pieces[2:], other_chips)):
            joint = jnp.take(jnp.concatenate(side), jnp.argsort(places), axis=0)
            ordered.append(
                jnp.transpose(joint, (1, 0, 2, 3)).reshape(1, 4 * GROUPS, width, 128)
            )
        pieces = tuple(ordered)

    q, k, v, mixed, lse = attend(ids, lengths, xs, mask, bias, vector_rows, pieces)
    feed_far = last_round(feed_near, count)
    feed_far = after(feed_far, mixed)

    feeds = (feed_near, swap(feed_near), feed_far, swap(feed_far))
    out, act, gup, first, gdown, gres, gbranch, gmixed, sums, up_sums = feed(
        ids, xs, mixed, cs, vector_rows, up_biases, feeds, pieces
    )
    shape = (near_count, 2, share, width)
    far_own, far_other = feed_weights(1, act, gup, first, gdown, shape)

    def by_device(grads):
        if aligned:
            return grads
        result = []
        for grad, places in zip(grads, (chips, other_chips)):
            parts = grad[0].reshape(grad.shape[1], count, rows, 128)
            parts = jnp.take(jnp.transpose(parts, (1, 0, 2, 3)), places, axis=0)
            result += [parts[:near_count], parts[near_count:]]
        return result

    def swapped_sum(own, other):
        return wide(own) + wide(swap(other))

    def halved(total):
        return total.reshape((2, total.shape[0] // 2) + total.shape[1:])

    def high_parts_of(total, count):
        return [
            lax.ppermute(low(total[high]), BOTH, xor_pairs(count, (4 * high, 4 * high)))
            for high in range(1, count // 4)
        ]

    def own_sum(total, parts):
        total = total[0]
        for part in parts:
            total = total + wide(part)
        return total

    gwo = out_weights(ids, after(mixed, far_own), gbranch, pieces)
    far = low(swapped_sum(far_own, far_other))
    gdown, far, _ = lax.optimization_barrier((gdown, far, gwo[0]))
    far = last_round(far, count)
    near_own, near_other = feed_weights(0, act, gup, first, gdown, shape)
    far, near_other = lax.optimization_barrier((far, near_other))
    near_came = swap(near_other)
    outs = unsort_rows(ids, order, after(out, far))
    near_came, near_own, far, _ = lax.optimization_barrier(
        (near_came, near_own, far, outs[0])
    )
    near = wide(near_own) + wide(near_came) + wide(far)
    gmixed, near = lax.optimization_barrier((gmixed, near))
    gfeed_came = lax.ppermute(low(halved(near)[1]), BOTH, xor_pairs(count, (1, 2)))
    grad_own, grad_send, *gws = attend_back(
        ids, lengths, order, xs, mask, bias, q, k, v, mixed, gmixed, lse, sums, up_sums, gres,
        pieces, gwo, rows,
    )
    gfeed_came, *gws = lax.optimization_barrier((gfeed_came, *gws))
    gfeed = halved(near)[0] + wide(gfeed_came)
    gfeed_parts = high_parts_of(gfeed, count)
    outs = place_rows(half, *outs)
    gws = by_device(gws)
    gw_far = last_round(low(swapped_sum(gws[1], gws[3])), count)
    near_came = swap(gws[2])
    gw_far, near_came = lax.optimization_barrier((gw_far, near_came))
    gw = wide(gws[0]) + wide(near_came) + wide(gw_far)
    gw_came = lax.ppermute(low(halved(gw)[1]), BOTH, xor_pairs(count, (1, 2)))
    gw_came, gfeed_parts = lax.optimization_barrier((gw_came, gfeed_parts))
    gw = halved(gw)[0] + wide(gw_came)
    gw_parts = high_parts_of(gw, count)
    gfeed = own_sum(gfeed, gfeed_parts)
    gfeed = in_order(half, gfeed, swap(gfeed))
    up_grad = jnp.transpose(gfeed[:, 0].reshape(hidden, width))
    down_grad = gfeed[:, 1].reshape(hidden, width)
    gw = own_sum(gw, gw_parts)
    query_grad, key_grad, value_grad, out_grad, *ends = finish(ids, gw, swap(gw), sizes)
    ends = [end.reshape(-1) for end in ends]
    grads = place_rows(half, grad_own, grad_send)

    return (
        outs[0], outs[1], grads[0], grads[1],
        query_grad, ends[0], key_grad, value_grad, ends[1], out_grad, ends[2], ends[3], ends[4],
        up_grad, ends[8], down_grad, ends[5], ends[6], ends[7], ends[9],
    )


def place_rows(half, own, send):
    came = swap(send)
    return [
        jnp.where(half == 0, jnp.stack([own[i], came[i]]), jnp.stack([came[i], own[i]]))
        for i in range(2)
    ]


def solution(mesh):
    rows3 = P("dp", "seq", None)
    flat, first, last = P("dp"), P("dp", None), P(None, "dp")
    in_specs = (
        rows3, rows3, rows3, rows3, first, first, first, flat, first, first, flat, first, flat,
        flat, flat, last, flat, first, flat, flat, flat, flat,
    )
    out_specs = (
        rows3, rows3, rows3, rows3, first, flat, first, first, flat, first, flat, flat, flat,
        last, flat, first, flat, flat, flat, flat,
    )
    body = functools.partial(shards, mesh.shape["dp"])
    return jax.shard_map(
        body, mesh=mesh, in_specs=in_specs, out_specs=out_specs, check_vma=False
    )
```

time: 459 us -> 352 us (0.77)
  local copies, waits for them, and re-layouts: 76 us -> 25.1 us
  starting transfers between devices: 54.8 us -> 38.9 us
  other arithmetic: 33.5 us -> 18.3 us
  Pallas kernels: 162 us -> 149 us
  waiting for transfers between devices: 120 us -> 114 us
    slice x24 -> x3, local copies, waits for them, and re-layouts: 16.5 us -> 1.29 us  [the longest x1 1.09 us: shards(): down_grad = gfeed[:, 1].reshape(hidden, width)]
    pallas_call x1, Pallas kernels: 36.4 us -> 22.4 us  [attend(): pl.pallas_call(attend_kernel, grid=(GROUPS,), out_shape=(SDS((tokens, wid...]
    all_to_all x2 -> x0, starting transfers between devices: 11.9 us -> none  [the longest x1 7.17 us: shards(): packed = jnp.sum(lax.all_to_all(packed, 'dp', 0, 0, tiled=True), axis=0)]
    ppermute x25, waiting for transfers between devices: 118 us -> 107 us  [the longest x5 44.5 us: last_round(): return lax.ppermute(value, BOTH, xor_pairs(count, (2, 1)))]
    convert_element_type x15 -> x2, local copies, waits for them, and re-layouts: 9.96 us -> 0.09 us  [low(): return value.astype(jnp.bfloat16)]
    concatenate x7 -> x3, local copies, waits for them, and re-layouts: 12.7 us -> 3.06 us  [low_round(): jnp.concatenate([value, lax.ppermute(value, BOTH, xor_pairs(count, (1, 2)...]
    reshape x15 -> x1, local copies, waits for them, and re-layouts: 9 us -> 1.22 us  [pack(): vector.reshape(1, -1)]
    ppermute x14 -> x13, waiting for transfers between devices: 0.04 us -> 6.94 us  [swap(): return lax.ppermute(value, 'seq', [(0, 1), (1, 0)])]
  transfers between devices with their start and end apart: 41 -> 38, of which waited for: 14 -> 18; matrix products, arithmetic and copies ran while one was open for 21% -> 6% of each run, Pallas kernels for 26% -> 27%
where the time goes in v2:
time: 352 us; the launch traced here: 347 us
  Pallas kernels  149 us (42%)
  waiting for transfers between devices  114 us (32%)
  starting transfers between devices  38.9 us (11%)
  local copies, waits for them, and re-layouts  25.1 us (7%)
  other arithmetic  18.3 us (5%)
    ppermute x5, waiting for transfers between devices, last_round(): return lax.ppermute(value, BOTH, xor_pairs(count, (2, 1)))  44.5 us
    pallas_call x1, Pallas kernels, attend_back(): pl.pallas_call(functools.partial(attend_back_kernel, rows_each), grid=(GR...  40.4 us
    pallas_call x1, Pallas kernels, feed(): pl.pallas_call(feed_kernel, grid=(tokens // BLOCK,), out_shape=(low, SDS(...  37.6 us
    ppermute x6, waiting for transfers between devices, high_parts_of(): lax.ppermute(low(total[high]), BOTH, xor_pairs(count, (4 * high, 4 * high)))  34.2 us
    pallas_call x2, Pallas kernels, feed_weights(): pl.pallas_call(feed_weights_kernel, grid=(2, 2), out_shape=(SDS(shape, jn...  22.9 us
    pallas_call x1, Pallas kernels, attend(): pl.pallas_call(attend_kernel, grid=(GROUPS,), out_shape=(SDS((tokens, wid...  22.4 us
    unnamed x55, local copies, waits for them, and re-layouts  18 us
    ppermute x3, waiting for transfers between devices, low_round(): lax.ppermute(value, BOTH, xor_pairs(count, (1, 2)))  14.9 us
  transfers between devices with their start and end apart: 38, of which 18 were waited for; matrix products, arithmetic and copies ran while one was open for 6% of the time, Pallas kernels for 27%

profile of v2, /device:TPU:0, one launch (start us, length us, event | category | flops | bytes accessed | tf_op | source)
XLA Modules:
  0.0 346.9 jit_solution(17814699646872534455)
XLA Ops:
  4.4 4.6 %pack.1 = (bf16[4,256,768]{2,1,0:T(8,128)(2,1)}, bf16[12,48,128]{2,1,0:T(8,128)(2,1)}, bf16[2,96,768]{2,1,0:T(8,128)(2,1)}, bf16[16,256]{1,0:T(8,128)(2,1)}) custom-call(s32[2]{0:T(128)} %pad_add_fusion.ids, bf16[2,256,768]{2,1,0:T(8,128)(2,1)} %content.3, bf16[2,256,768]{2,1,0:T(8,128)(2,1)} %query.3, bf16[2,256,768]{2,1,0:T(8,128)(2,1)} %ccot.3, ...), custom_call_target="tpu_custom_call" | custom-call | bytes 6400000 | tf_op jit(solution)/shard_map/pack/pallas_call | solution.py:118
  9.5 4.7 %collective-permute-start.3 = (bf16[16,256]{1,0:T(8,128)(2,1)}, bf16[16,256]{1,0:T(8,128)(2,1)S(1)}, u32[]{:S(2)}, u32[]{:S(2)}) collective-permute-start(bf16[16,256]{1,0:T(8,128)(2,1)} %get-tuple-element.111), channel_id=1, source_target_pairs={{0,24},{1,25},{2,26},{3,27},{4,28},{5,29},{6,30},{7,31},{8,16},{9,... | collective-permute-start | bytes 24584 | tf_op jit(solution)/shard_map/ppermute | solution.py:1079
  27.9 6.3 %sort_rows.1 = (bf16[1024,768]{1,0:T(8,128)(2,1)}, bf16[1024,768]{1,0:T(8,128)(2,1)}, bf16[2,512,512]{2,1,0:T(8,128)(2,1)}) custom-call(s32[2]{0:T(128)} %pad_add_fusion.ids, s32[2,8]{1,0:T(2,128)} %lengths.5, bf16[2,256,768]{2,1,0:T(8,128)(2,1)} %content.3, bf16[2,256,768]{2,1,0:T(8,128)(2,1)} %query.3, bf16[2,256,768]{2,1,0:T(8,128)(2,1)} %ccot.3, ...), custom_call_target="tpu_custom_call" | custom-call | bytes 8000000 | tf_op jit(solution)/shard_map/sort_rows/pallas_call | solution.py:195
  36.1 8.2 %collective-permute-done.9 = bf16[4,12,48,128]{3,2,1,0:T(8,128)(2,1)S(1)} collective-permute-done((bf16[4,12,48,128]{3,2,1,0:T(8,128)(2,1)S(1)}, bf16[4,12,48,128]{3,2,1,0:T(8,128)(2,1)S(1)}, u32[]{:S(2)}, u32[]{:S(2)}) %collective-permute-start.9) | collective-permute-done | bytes 589856 | tf_op jit(solution)/shard_map/ppermute | solution.py:1085
  50.3 11.1 %collective-permute-done.5.far = bf16[8,16,256]{2,1,0:T(8,128)(2,1)S(1)} collective-permute-done((bf16[8,16,256]{2,1,0:T(8,128)(2,1)}, bf16[8,16,256]{2,1,0:T(8,128)(2,1)S(1)}, u32[]{:S(2)}, u32[]{:S(2)}) %collective-permute-start.5) | collective-permute-done | bytes 65568 | tf_op jit(solution)/shard_map/ppermute | solution.py:1089
  62.9 12.4 %collective-permute-done.14 = bf16[2,96,768]{2,1,0:T(8,128)(2,1)S(1)} collective-permute-done((bf16[2,96,768]{2,1,0:T(8,128)(2,1)S(1)}, bf16[2,96,768]{2,1,0:T(8,128)(2,1)S(1)}, u32[]{:S(2)}, u32[]{:S(2)}) %collective-permute-start.14) | collective-permute-done | bytes 294944 | tf_op jit(solution)/shard_map/ppermute | solution.py:1079
  79.1 3.8 %vectors.1 = (f32[8,768]{1,0:T(8,128)}, f32[1,3072]{1,0:T(1,128)}, bf16[12,128,640]{2,1,0:T(8,128)(2,1)}) custom-call(s32[2]{0:T(128)} %pad_add_fusion.ids, bf16[8,16,256]{2,1,0:T(8,128)(2,1)} %constant_dynamic-update-slice_fusion.near, bf16[8,16,256]{2,1,0:T(8,128)(2,1)} %copy-done.19), custom_call_target="tpu_custom_call" | custom-call | bytes 9600000 | tf_op jit(solution)/shard_map/vectors/pallas_call | solution.py:386
  87.7 6.2 %collective-permute-done.16 = bf16[4,2,96,768]{3,2,1,0:T(8,128)(2,1)} collective-permute-done((bf16[4,2,96,768]{3,2,1,0:T(8,128)(2,1)}, bf16[4,2,96,768]{3,2,1,0:T(8,128)(2,1)}, u32[]{:S(2)}, u32[]{:S(2)}) %collective-permute-start.16) | collective-permute-done | bytes 1179680 | tf_op jit(solution)/shard_map/ppermute | solution.py:1085
  98.0 22.4 %attend.1 = (bf16[1024,768]{1,0:T(8,128)(2,1)}, bf16[512,768]{1,0:T(8,128)(2,1)}, bf16[512,768]{1,0:T(8,128)(2,1)}, bf16[1024,768]{1,0:T(8,128)(2,1)}, f32[3,1024,128]{2,1,0:T(8,128)}) custom-call(s32[2]{0:T(128)} %pad_add_fusion.ids, s32[2,8]{1,0:T(2,128)} %lengths.5, bf16[1024,768]{1,0:T(8,128)(2,1)} %get-tuple-element.109.xs.xs_far, ...), custom_call_target="tpu_custom_call" | custom-call | bytes 28800000 | tf_op jit(solution)/shard_map/attend/pallas_call | solution.py:527
  120.4 5.0 %collective-permute-done.18.far_own = bf16[8,2,96,768]{3,2,1,0:T(8,128)(2,1)S(1)} collective-permute-done((bf16[8,2,96,768]{3,2,1,0:T(8,128)(2,1)}, bf16[8,2,96,768]{3,2,1,0:T(8,128)(2,1)S(1)}, u32[]{:S(2)}, u32[]{:S(2)}) %collective-permute-start.18) | collective-permute-done | bytes 2359328 | tf_op jit(solution)/shard_map/ppermute | solution.py:1089
  125.4 4.5 %collective-permute-done.19.far_other = bf16[8,2,96,768]{3,2,1,0:T(8,128)(2,1)S(1)} collective-permute-done((bf16[8,2,96,768]{3,2,1,0:T(8,128)(2,1)S(1)}, bf16[8,2,96,768]{3,2,1,0:T(8,128)(2,1)S(1)}, u32[]{:S(2)}, u32[]{:S(2)}) %collective-permute-start.19) | collective-permute-done | bytes 2359328 | tf_op jit(solution)/shard_map/ppermute | solution.py:1074
  131.4 37.6 %feed.1 = (bf16[1024,768]{1,0:T(8,128)(2,1)}, bf16[1024,3072]{1,0:T(8,128)(2,1)}, bf16[1024,3072]{1,0:T(8,128)(2,1)}, bf16[1024,768]{1,0:T(8,128)(2,1)}, bf16[10...) custom-call(s32[2]{0:T(128)} %pad_add_fusion.ids, ...), custom_call_target="tpu_custom_call" | custom-call | bytes 57600000 | tf_op jit(solution)/shard_map/feed/pallas_call | solution.py:660
  168.9 11.6 %feed_weights.2 = (bf16[8,2,96,768]{3,2,1,0:T(8,128)(2,1)}, bf16[8,2,96,768]{3,2,1,0:T(8,128)(2,1)}) custom-call(bf16[1024,3072]{1,0:T(8,128)(2,1)} %get-tuple-element.132.act, bf16[1024,3072]{1,0:T(8,128)(2,1)} %get-tuple-element.133.gup, bf16[1024,768]{1,0:T(8,128)(2,1)} %get-tuple-element.134.first, bf16[1024,768]{1,0:T(8,128)(2,1)} %get-tuple-element.141.gdown), custom_call_target="tpu_custom_call" | custom-call | bytes 14400000 | tf_op jit(solution)/shard_map/feed_weights/pallas_call | solution.py:719
  180.7 4.8 %out_weights.1 = (bf16[8,13,48,128]{3,2,1,0:T(8,128)(2,1)}, bf16[8,13,48,128]{3,2,1,0:T(8,128)(2,1)}, bf16[8,13,48,128]{3,2,1,0:T(8,128)(2,1)}, bf16[8,13,48,128]{3,2,1,0:T(8,128)(2,1)}) custom-call(s32[2]{0:T(128)} %pad_add_fusion.ids, bf16[1024,768]{1,0:T(8,128)(2,1)} %get-tuple-element.137.mixed, bf16[1024,768]{1,0:T(8,128)(2,1)} %get-tuple-element.138.gbranch), custom_call_target="tpu_custom_call" | custom-call | bytes 6400000 | tf_op jit(solution)/shard_map/out_weights/pallas_call | solution.py:748
  185.5 3.7 %add_convert_fusion = bf16[8,2,96,768]{3,2,1,0:T(8,128)(2,1)} fusion(bf16[8,2,96,768]{3,2,1,0:T(8,128)(2,1)} %collective-permute-done.20, bf16[8,2,96,768]{3,2,1,0:T(8,128)(2,1)S(1)} %copy-done.7), kind=kLoop, calls=%fused_computation.1 | loop fusion | flops 4718592 | bytes 7077888 | tf_op jit(solution)/shard_map/convert_element_type | solution.py:1108
  190.9 11.3 %feed_weights.3 = (bf16[8,2,96,768]{3,2,1,0:T(8,128)(2,1)}, bf16[8,2,96,768]{3,2,1,0:T(8,128)(2,1)}) custom-call(bf16[1024,3072]{1,0:T(8,128)(2,1)} %get-tuple-element.132.act, bf16[1024,3072]{1,0:T(8,128)(2,1)} %get-tuple-element.133.gup, bf16[1024,768]{1,0:T(8,128)(2,1)} %get-tuple-element.134.first, bf16[1024,768]{1,0:T(8,128)(2,1)} %get-tuple-element.141.gdown), custom_call_target="tpu_custom_call" | custom-call | bytes 14400000 | tf_op jit(solution)/shard_map/feed_weights/pallas_call | solution.py:719
  202.2 16.1 %collective-permute-done.21 = bf16[8,2,96,768]{3,2,1,0:T(8,128)(2,1)S(1)} collective-permute-done((bf16[8,2,96,768]{3,2,1,0:T(8,128)(2,1)}, bf16[8,2,96,768]{3,2,1,0:T(8,128)(2,1)S(1)}, u32[]{:S(2)}, u32[]{:S(2)}) %collective-permute-start.21) | collective-permute-done | bytes 2359328 | tf_op jit(solution)/shard_map/ppermute | solution.py:1089
  218.3 4.3 %unsort_rows.1 = (bf16[2,256,768]{2,1,0:T(8,128)(2,1)}, bf16[2,256,768]{2,1,0:T(8,128)(2,1)}) custom-call(s32[2]{0:T(128)} %pad_add_fusion.ids, s32[2,512]{1,0:T(2,128)} %order.5, bf16[1024,768]{1,0:T(8,128)(2,1)} %get-tuple-element.144.values), custom_call_target="tpu_custom_call" | custom-call | bytes 4800000 | tf_op jit(solution)/shard_map/unsort_rows/pallas_call | solution.py:242
  230.5 40.4 %attend_back.1 = (bf16[2,256,768]{2,1,0:T(8,128)(2,1)}, bf16[2,256,768]{2,1,0:T(8,128)(2,1)}, bf16[8,13,48,128]{3,2,1,0:T(8,128)(2,1)}, bf16[8,13,48,128]{3,2,1,...) custom-call(s32[2]{0:T(128)} %pad_add_fusion.ids, ...), custom_call_target="tpu_custom_call", output_to_operand_aliasing={{2}: (19, {}), {3}: (20, {}), {4}: (21, {}), {5}: (22, {})} | custom-call | bytes 43200000 | tf_op jit(solution)/shard_map/attend_back/pallas_call | solution.py:975
  282.0 12.3 %collective-permute-done.27 = bf16[8,13,48,128]{3,2,1,0:T(8,128)(2,1)S(1)} collective-permute-done((bf16[8,13,48,128]{3,2,1,0:T(8,128)(2,1)}, bf16[8,13,48,128]{3,2,1,0:T(8,128)(2,1)S(1)}, u32[]{:S(2)}, u32[]{:S(2)}) %collective-permute-start.27) | collective-permute-done | bytes 1277984 | tf_op jit(solution)/shard_map/ppermute | solution.py:1089
  302.5 5.5 %collective-permute-done.32 = bf16[2,96,768]{2,1,0:T(8,128)(2,1)S(1)} collective-permute-done((bf16[2,96,768]{2,1,0:T(8,128)(2,1)S(1)}, bf16[2,96,768]{2,1,0:T(8,128)(2,1)S(1)}, u32[]{:S(2)}, u32[]{:S(2)}) %collective-permute-start.32) | collective-permute-done | bytes 294944 | tf_op jit(solution)/shard_map/ppermute | solution.py:1202
  308.0 15.5 %collective-permute-done.31 = bf16[2,96,768]{2,1,0:T(8,128)(2,1)S(1)} collective-permute-done((bf16[2,96,768]{2,1,0:T(8,128)(2,1)S(1)}, bf16[2,96,768]{2,1,0:T(8,128)(2,1)S(1)}, u32[]{:S(2)}, u32[]{:S(2)}) %collective-permute-start.31) | collective-permute-done | bytes 294944 | tf_op jit(solution)/shard_map/ppermute | solution.py:1202
  331.0 3.9 %collective-permute-done.35 = bf16[13,48,128]{2,1,0:T(8,128)(2,1)S(1)} collective-permute-done((bf16[13,48,128]{2,1,0:T(8,128)(2,1)S(1)}, bf16[13,48,128]{2,1,0:T(8,128)(2,1)S(1)}, u32[]{:S(2)}, u32[]{:S(2)}) %collective-permute-start.35) | collective-permute-done | bytes 159776 | tf_op jit(solution)/shard_map/ppermute | solution.py:1202
  335.0 5.7 %collective-permute-done.34 = bf16[13,48,128]{2,1,0:T(8,128)(2,1)S(1)} collective-permute-done((bf16[13,48,128]{2,1,0:T(8,128)(2,1)S(1)}, bf16[13,48,128]{2,1,0:T(8,128)(2,1)S(1)}, u32[]{:S(2)}, u32[]{:S(2)}) %collective-permute-start.34) | collective-permute-done | bytes 159776 | tf_op jit(solution)/shard_map/ppermute | solution.py:1202
  (146 shorter events, 83.4 us)
Async XLA Ops:
  9.0 17.7 %collective-permute-start = (bf16[4,256,768]{2,1,0:T(8,128)(2,1)}, bf16[4,256,768]{2,1,0:T(8,128)(2,1)S(1)}, u32[]{:S(2)}, u32[]{:S(2)}) collective-permute-start(bf16[4,256,768]{2,1,0:T(8,128)(2,1)} %get-tuple-element.108), channel_id=1, source_target_pairs={{0,1},{1,0},{2,3},{3,2},{4,5},{5,4},{6,7},{7,6},{8,9},{9,8},{10,11... | collective-permute-start | bytes 4718600 | tf_op jit(solution)/shard_map/ppermute | solution.py:1074
  14.8 19.4 %collective-permute-start.8 = (bf16[12,48,128]{2,1,0:T(8,128)(2,1)}, bf16[12,48,128]{2,1,0:T(8,128)(2,1)S(1)}, u32[]{:S(2)}, u32[]{:S(2)}) collective-permute-start(bf16[12,48,128]{2,1,0:T(8,128)(2,1)} %get-tuple-element.114), channel_id=1, source_target_pairs={{0,24},{1,25},{2,26},{3,27},{4,28},{5,29},{6,30},{7,31},{8,16},{9,... | collective-permute-start | bytes 442376 | tf_op jit(solution)/shard_map/ppermute | solution.py:1079
  20.8 13.4 %collective-permute-start.7 = (bf16[12,48,128]{2,1,0:T(8,128)(2,1)}, bf16[12,48,128]{2,1,0:T(8,128)(2,1)S(1)}, u32[]{:S(2)}, u32[]{:S(2)}) collective-permute-start(bf16[12,48,128]{2,1,0:T(8,128)(2,1)} %get-tuple-element.114), channel_id=1, source_target_pairs={{0,16},{1,17},{2,18},{3,19},{4,20},{5,21},{6,22},{7,23},{8,24},{9,... | collective-permute-start | bytes 442376 | tf_op jit(solution)/shard_map/ppermute | solution.py:1079
  20.8 13.4 %collective-permute-start.6 = (bf16[12,48,128]{2,1,0:T(8,128)(2,1)}, bf16[12,48,128]{2,1,0:T(8,128)(2,1)S(1)}, u32[]{:S(2)}, u32[]{:S(2)}) collective-permute-start(bf16[12,48,128]{2,1,0:T(8,128)(2,1)} %get-tuple-element.114), channel_id=1, source_target_pairs={{0,8},{1,9},{2,10},{3,11},{4,12},{5,13},{6,14},{7,15},{8,0},{9,1},... | collective-permute-start | bytes 442376 | tf_op jit(solution)/shard_map/ppermute | solution.py:1079
  44.4 18.5 %collective-permute-start.11 = (bf16[8,12,48,128]{3,2,1,0:T(8,128)(2,1)S(1)}, bf16[8,12,48,128]{3,2,1,0:T(8,128)(2,1)S(1)}, u32[]{:S(2)}, u32[]{:S(2)}) collective-permute-start(bf16[8,12,48,128]{3,2,1,0:T(8,128)(2,1)S(1)} %constant_dynamic-update-slice_fusion.5.rest_0_), channel_id=1, source_target_pairs={{0,1},{1,0},{2,3},{3,2},{4,5},{5,4},{6,7},{7,6},{8,9},{9,8},{10,11... | collective-permute-start | bytes 3538952 | tf_op jit(solution)/shard_map/ppermute | solution.py:1074
  44.4 18.4 %collective-permute-start.10 = (bf16[8,12,48,128]{3,2,1,0:T(8,128)(2,1)S(1)}, bf16[8,12,48,128]{3,2,1,0:T(8,128)(2,1)S(1)}, u32[]{:S(2)}, u32[]{:S(2)}) collective-permute-start(bf16[8,12,48,128]{3,2,1,0:T(8,128)(2,1)S(1)} %constant_dynamic-update-slice_fusion.5.rest_0_), channel_id=1, source_target_pairs={{0,4},{1,3},{2,6},{3,1},{4,0},{5,7},{6,2},{7,5},{8,12},{9,11},{10,... | collective-permute-start | bytes 3538952 | tf_op jit(solution)/shard_map/ppermute | solution.py:1089
  46.2 15.3 %collective-permute-start.5 = (bf16[8,16,256]{2,1,0:T(8,128)(2,1)}, bf16[8,16,256]{2,1,0:T(8,128)(2,1)S(1)}, u32[]{:S(2)}, u32[]{:S(2)}) collective-permute-start(bf16[8,16,256]{2,1,0:T(8,128)(2,1)} %constant_dynamic-update-slice_fusion.near), channel_id=1, source_target_pairs={{0,4},{1,3},{2,6},{3,1},{4,0},{5,7},{6,2},{7,5},{8,12},{9,11},{10,... | collective-permute-start | bytes 196616 | tf_op jit(solution)/shard_map/ppermute | solution.py:1089
  46.5 16.3 %collective-permute-start.15 = (bf16[2,96,768]{2,1,0:T(8,128)(2,1)S(1)}, bf16[2,96,768]{2,1,0:T(8,128)(2,1)S(1)}, u32[]{:S(2)}, u32[]{:S(2)}) collective-permute-start(bf16[2,96,768]{2,1,0:T(8,128)(2,1)S(1)} %copy-done.10), channel_id=1, source_target_pairs={{0,24},{1,25},{2,26},{3,27},{4,28},{5,29},{6,30},{7,31},{8,16},{9,... | collective-permute-start | bytes 884744 | tf_op jit(solution)/shard_map/ppermute | solution.py:1079
  50.3 25.0 %collective-permute-start.14 = (bf16[2,96,768]{2,1,0:T(8,128)(2,1)S(1)}, bf16[2,96,768]{2,1,0:T(8,128)(2,1)S(1)}, u32[]{:S(2)}, u32[]{:S(2)}) collective-permute-start(bf16[2,96,768]{2,1,0:T(8,128)(2,1)S(1)} %copy-done.10), channel_id=1, source_target_pairs={{0,16},{1,17},{2,18},{3,19},{4,20},{5,21},{6,22},{7,23},{8,24},{9,... | collective-permute-start | bytes 884744 | tf_op jit(solution)/shard_map/ppermute | solution.py:1079
  61.4 14.8 %collective-permute-start.13 = (bf16[2,96,768]{2,1,0:T(8,128)(2,1)S(1)}, bf16[2,96,768]{2,1,0:T(8,128)(2,1)S(1)}, u32[]{:S(2)}, u32[]{:S(2)}) collective-permute-start(bf16[2,96,768]{2,1,0:T(8,128)(2,1)S(1)} %copy-done.10), channel_id=1, source_target_pairs={{0,8},{1,9},{2,10},{3,11},{4,12},{5,13},{6,14},{7,15},{8,0},{9,1},... | collective-permute-start | bytes 884744 | tf_op jit(solution)/shard_map/ppermute | solution.py:1079
  77.4 16.5 %collective-permute-start.16 = (bf16[4,2,96,768]{3,2,1,0:T(8,128)(2,1)}, bf16[4,2,96,768]{3,2,1,0:T(8,128)(2,1)}, u32[]{:S(2)}, u32[]{:S(2)}) collective-permute-start(bf16[4,2,96,768]{3,2,1,0:T(8,128)(2,1)} %pad_maximum_fusion), channel_id=1, source_target_pairs={{0,2},{1,5},{2,0},{3,7},{4,6},{5,1},{6,4},{7,3},{8,10},{9,13},{10,... | collective-permute-start | bytes 3538952 | tf_op jit(solution)/shard_map/ppermute | solution.py:1085
  79.1 17.3 %collective-permute-start.12 = (bf16[8,12,48,128]{3,2,1,0:T(8,128)(2,1)S(1)}, bf16[8,12,48,128]{3,2,1,0:T(8,128)(2,1)}, u32[]{:S(2)}, u32[]{:S(2)}) collective-permute-start(bf16[8,12,48,128]{3,2,1,0:T(8,128)(2,1)S(1)} %collective-permute-done.10.rest_1_), channel_id=1, source_target_pairs={{0,1},{1,0},{2,3},{3,2},{4,5},{5,4},{6,7},{7,6},{8,9},{9,8},{10,11... | collective-permute-start | bytes 3538952 | tf_op jit(solution)/shard_map/ppermute | solution.py:1074
  96.3 29.1 %collective-permute-start.18 = (bf16[8,2,96,768]{3,2,1,0:T(8,128)(2,1)}, bf16[8,2,96,768]{3,2,1,0:T(8,128)(2,1)S(1)}, u32[]{:S(2)}, u32[]{:S(2)}) collective-permute-start(bf16[8,2,96,768]{3,2,1,0:T(8,128)(2,1)} %constant_dynamic-update-slice_fusion.10.near_own), channel_id=1, source_target_pairs={{0,4},{1,3},{2,6},{3,1},{4,0},{5,7},{6,2},{7,5},{8,12},{9,11},{10,... | collective-permute-start | bytes 7077896 | tf_op jit(solution)/shard_map/ppermute | solution.py:1089
  98.0 27.4 %collective-permute-start.17 = (bf16[8,2,96,768]{3,2,1,0:T(8,128)(2,1)}, bf16[8,2,96,768]{3,2,1,0:T(8,128)(2,1)}, u32[]{:S(2)}, u32[]{:S(2)}) collective-permute-start(bf16[8,2,96,768]{3,2,1,0:T(8,128)(2,1)} %constant_dynamic-update-slice_fusion.10.near_own), channel_id=1, source_target_pairs={{0,1},{1,0},{2,3},{3,2},{4,5},{5,4},{6,7},{7,6},{8,9},{9,8},{10,11... | collective-permute-start | bytes 7077896 | tf_op jit(solution)/shard_map/ppermute | solution.py:1074
  189.2 29.1 %collective-permute-start.21 = (bf16[8,2,96,768]{3,2,1,0:T(8,128)(2,1)}, bf16[8,2,96,768]{3,2,1,0:T(8,128)(2,1)S(1)}, u32[]{:S(2)}, u32[]{:S(2)}) collective-permute-start(bf16[8,2,96,768]{3,2,1,0:T(8,128)(2,1)} %add_convert_fusion), channel_id=1, source_target_pairs={{0,4},{1,3},{2,6},{3,1},{4,0},{5,7},{6,2},{7,5},{8,12},{9,11},{10,... | collective-permute-start | bytes 7077896 | tf_op jit(solution)/shard_map/ppermute | solution.py:1089
  228.8 42.1 %collective-permute-start.25 = (bf16[4,2,96,768]{3,2,1,0:T(8,128)(2,1)S(1)}, bf16[4,2,96,768]{3,2,1,0:T(8,128)(2,1)S(1)}, u32[]{:S(2)}, u32[]{:S(2)}) collective-permute-start(bf16[4,2,96,768]{3,2,1,0:T(8,128)(2,1)S(1)} %slice.149), channel_id=1, source_target_pairs={{0,2},{1,5},{2,0},{3,7},{4,6},{5,1},{6,4},{7,3},{8,10},{9,13},{10,... | collective-permute-start | bytes 3538952 | tf_op jit(solution)/shard_map/ppermute | solution.py:1225
  276.9 17.5 %collective-permute-start.27 = (bf16[8,13,48,128]{3,2,1,0:T(8,128)(2,1)}, bf16[8,13,48,128]{3,2,1,0:T(8,128)(2,1)S(1)}, u32[]{:S(2)}, u32[]{:S(2)}) collective-permute-start(bf16[8,13,48,128]{3,2,1,0:T(8,128)(2,1)} %add_convert_fusion.1), channel_id=1, source_target_pairs={{0,4},{1,3},{2,6},{3,1},{4,0},{5,7},{6,2},{7,5},{8,12},{9,11},{10,... | collective-permute-start | bytes 3833864 | tf_op jit(solution)/shard_map/ppermute | solution.py:1089
  295.0 28.5 %collective-permute-start.29 = (bf16[4,13,48,128]{3,2,1,0:T(8,128)(2,1)S(1)}, bf16[4,13,48,128]{3,2,1,0:T(8,128)(2,1)S(1)}, u32[]{:S(2)}, u32[]{:S(2)}) collective-permute-start(bf16[4,13,48,128]{3,2,1,0:T(8,128)(2,1)S(1)} %slice.150), channel_id=1, source_target_pairs={{0,2},{1,5},{2,0},{3,7},{4,6},{5,1},{6,4},{7,3},{8,10},{9,13},{10,... | collective-permute-start | bytes 1916936 | tf_op jit(solution)/shard_map/ppermute | solution.py:1239
  296.1 11.9 %collective-permute-start.32 = (bf16[2,96,768]{2,1,0:T(8,128)(2,1)S(1)}, bf16[2,96,768]{2,1,0:T(8,128)(2,1)S(1)}, u32[]{:S(2)}, u32[]{:S(2)}) collective-permute-start(bf16[2,96,768]{2,1,0:T(8,128)(2,1)S(1)} %get-tuple-element.202), channel_id=1, source_target_pairs={{0,24},{1,25},{2,26},{3,27},{4,28},{5,29},{6,30},{7,31},{8,16},{9,... | collective-permute-start | bytes 884744 | tf_op jit(solution)/shard_map/ppermute | solution.py:1202
  299.8 23.7 %collective-permute-start.31 = (bf16[2,96,768]{2,1,0:T(8,128)(2,1)S(1)}, bf16[2,96,768]{2,1,0:T(8,128)(2,1)S(1)}, u32[]{:S(2)}, u32[]{:S(2)}) collective-permute-start(bf16[2,96,768]{2,1,0:T(8,128)(2,1)S(1)} %get-tuple-element.203), channel_id=1, source_target_pairs={{0,16},{1,17},{2,18},{3,19},{4,20},{5,21},{6,22},{7,23},{8,24},{9,... | collective-permute-start | bytes 884744 | tf_op jit(solution)/shard_map/ppermute | solution.py:1202
  299.8 23.7 %collective-permute-start.30 = (bf16[2,96,768]{2,1,0:T(8,128)(2,1)S(1)}, bf16[2,96,768]{2,1,0:T(8,128)(2,1)S(1)}, u32[]{:S(2)}, u32[]{:S(2)}) collective-permute-start(bf16[2,96,768]{2,1,0:T(8,128)(2,1)S(1)} %get-tuple-element.204), channel_id=1, source_target_pairs={{0,8},{1,9},{2,10},{3,11},{4,12},{5,13},{6,14},{7,15},{8,0},{9,1},... | collective-permute-start | bytes 884744 | tf_op jit(solution)/shard_map/ppermute | solution.py:1202
  302.0 38.9 %collective-permute-start.24 = (bf16[2,256,768]{2,1,0:T(8,128)(2,1)S(1)}, bf16[2,256,768]{2,1,0:T(8,128)(2,1)S(1)}, u32[]{:S(2)}, u32[]{:S(2)}) collective-permute-start(bf16[2,256,768]{2,1,0:T(8,128)(2,1)S(1)} %copy-done.20), channel_id=1, source_target_pairs={{0,1},{1,0},{2,3},{3,2},{4,5},{5,4},{6,7},{7,6},{8,9},{9,8},{10,11... | collective-permute-start | bytes 2359304 | tf_op jit(solution)/shard_map/ppermute | solution.py:1074
  326.5 14.2 %collective-permute-start.34 = (bf16[13,48,128]{2,1,0:T(8,128)(2,1)S(1)}, bf16[13,48,128]{2,1,0:T(8,128)(2,1)S(1)}, u32[]{:S(2)}, u32[]{:S(2)}) collective-permute-start(bf16[13,48,128]{2,1,0:T(8,128)(2,1)S(1)} %get-tuple-element.215), channel_id=1, source_target_pairs={{0,16},{1,17},{2,18},{3,19},{4,20},{5,21},{6,22},{7,23},{8,24},{9,... | collective-permute-start | bytes 479240 | tf_op jit(solution)/shard_map/ppermute | solution.py:1202
  327.4 17.8 %collective-permute-start.37 = (f32[2,96,768]{2,1,0:T(8,128)S(1)}, f32[2,96,768]{2,1,0:T(8,128)S(1)}, u32[]{:S(2)}, u32[]{:S(2)}) collective-permute-start(f32[2,96,768]{2,1,0:T(8,128)S(1)} %fusion.2), channel_id=1, source_target_pairs={{0,1},{1,0},{2,3},{3,2},{4,5},{5,4},{6,7},{7,6},{8,9},{9,8},{10,11... | collective-permute-start | bytes 1769480 | tf_op jit(solution)/shard_map/ppermute | solution.py:1074
  (35 other events, 263.6 us)

commit v3 on v2

--- a/solution.py
+++ b/solution.py
@@ -52,8 +52,7 @@
 
 ME, HALF = 0, 1
 VECTORS, UP_SLOT, TABLE_SLOT = 10, 8, 9
-VECTOR_TILE = 4 * GROUPS
-GRAD_TILES = VECTOR_TILE + 1
+FIRST_TILES, LAST_TILES = 3 * GROUPS, 4
 FULL = 60
 
 
@@ -70,7 +69,7 @@
 
 def pack_kernel(ids, content, query, ccot, qcot, wq, wk, wv, wo, up, down, *rest):
     vectors, rest = rest[:VECTORS], rest[VECTORS:]
-    (theirs, square, feed, slots, tokens, squares, feeds, turned, in_sems, out_sems) = rest
+    (theirs, square, feed, slots, tokens, squares, feeds, in_sems, out_sems) = rest
     half = ids[HALF]
     share = feed.shape[1]
     loads = []
@@ -88,8 +87,8 @@
     for index, source in enumerate((content, query, ccot, qcot)):
         load(source.at[1 - half], tokens.at[index])
     rows = pl.ds(pl.multiple_of(half * share, share), share)
-    load(down.at[rows, :], feeds)
-    turned[...] = jnp.transpose(up[...].astype(jnp.float32)).astype(jnp.bfloat16)
+    load(up.at[rows, :], feeds.at[0])
+    load(down.at[rows, :], feeds.at[1])
     slots[...] = jnp.zeros_like(slots)
     for index, vector in enumerate(vectors):
         slots[index : index + 1, : vector.shape[1]] = vector[...]
@@ -97,16 +96,14 @@
         copy.wait()
     stores = [
         pltpu.make_async_copy(squares, square, out_sems.at[0]),
-        pltpu.make_async_copy(turned.at[rows, :], feed.at[0], out_sems.at[1]),
-        pltpu.make_async_copy(tokens, theirs, out_sems.at[2]),
-        pltpu.make_async_copy(feeds, feed.at[1], out_sems.at[3]),
+        pltpu.make_async_copy(tokens, theirs, out_sems.at[1]),
+        pltpu.make_async_copy(feeds, feed, out_sems.at[2]),
     ]
     stores[0].start()
-    stores[1].start()
     for copy in loads[4 * GROUPS :]:
         copy.wait()
+    stores[1].start()
     stores[2].start()
-    stores[3].start()
     for copy in stores:
         copy.wait()
 
@@ -114,7 +111,7 @@
 def pack(ids, content, query, ccot, qcot, wq, wk, wv, wo, up, down, vectors):
     _, block, width = content.shape
     rows = wq.shape[0]
-    hidden = up.shape[1]
+    hidden = up.shape[0]
     return pl.pallas_call(
         pack_kernel,
         out_shape=(
@@ -123,20 +120,19 @@
             SDS((2, hidden // 2, width), jnp.bfloat16),
             SDS((16, 256), jnp.bfloat16),
         ),
-        in_specs=[SMEM_SPEC] + [HBM_SPEC] * 8 + [VMEM_SPEC, HBM_SPEC] + [VMEM_SPEC] * VECTORS,
+        in_specs=[SMEM_SPEC] + [HBM_SPEC] * 10 + [VMEM_SPEC] * VECTORS,
         out_specs=(HBM_SPEC,) * 3 + (VMEM_SPEC,),
         scratch_shapes=[
             pltpu.VMEM((4, block, width), jnp.bfloat16),
             pltpu.VMEM((4 * GROUPS, rows, 128), jnp.bfloat16),
-            pltpu.VMEM((hidden // 2, width), jnp.bfloat16),
-            pltpu.VMEM((hidden, width), jnp.bfloat16),
-            pltpu.SemaphoreType.DMA((4 * GROUPS + 5,)),
-            pltpu.SemaphoreType.DMA((4,)),
+            pltpu.VMEM((2, hidden // 2, width), jnp.bfloat16),
+            pltpu.SemaphoreType.DMA((4 * GROUPS + 6,)),
+            pltpu.SemaphoreType.DMA((3,)),
         ],
         cost_estimate=cost(4),
         compiler_params=params(None, FULL),
         name="pack",
-    )(ids, *in_hbm(content, query, ccot, qcot, wq, wk, wv, wo), up, *in_hbm(down),
+    )(ids, *in_hbm(content, query, ccot, qcot, wq, wk, wv, wo, up, down),
       *(vector.reshape(1, -1) for vector in vectors))
 
 
@@ -589,12 +585,10 @@
     step = pl.program_id(0)
     units = up_all.shape[0] // 4
     parts = (near_own, near_other, far_own, far_other)
-
-    @pl.when(step == 0)
-    def _():
-        sums[...] = jnp.zeros_like(sums)
-        up_sums[...] = jnp.zeros_like(up_sums)
-        copies = block_copies(ids, pieces, wo_all, sems, slice(3 * GROUPS, 4 * GROUPS))
+    held = sum(piece.shape[0] for piece in pieces)
+
+    def weight_copies():
+        copies = []
         share = near_own.shape[2]
         for index, part in enumerate(parts):
             for block in range(part.shape[0]):
@@ -602,13 +596,23 @@
                 for which, target in ((0, up_all), (1, down_all)):
                     copies.append(
                         pltpu.make_async_copy(
-                            part.at[block, which], target.at[here, :], sems.at[len(copies)]
+                            part.at[block, which], target.at[here, :],
+                            sems.at[held + len(copies)],
                         )
                     )
+        return copies
+
+    @pl.when(step == 0)
+    def _():
+        sums[...] = jnp.zeros_like(sums)
+        up_sums[...] = jnp.zeros_like(up_sums)
+        copies = block_copies(ids, pieces, wo_all, sems, slice(3 * GROUPS, 4 * GROUPS))
+        copies += weight_copies()
         run_copies(copies)
 
     wo = jnp.concatenate([joined(wo_all, index) for index in range(GROUPS)], axis=1)
     branch = product(mixed[...], wo) + rows[0:1, :]
+
     normal1, scale1 = norm_parts(xs[...].astype(jnp.float32) + branch)
     first = normal1 * rows[1:2, :] + rows[2:3, :]
     first_low = first.astype(jnp.bfloat16)
@@ -738,7 +742,7 @@
         for half in range(2):
             lane = index * LANES + half * 128
             buffer[half, index] = grad[:, lane : lane + 128]
-    run_copies(block_stores(ids, buffer, outs, sems, slice(3 * GROUPS, 4 * GROUPS)))
+    run_copies(block_stores(ids, buffer, outs, sems, slice(2 * GROUPS, 3 * GROUPS)))
 
 
 def out_weights(ids, mixed, gbranch, pieces):
@@ -748,7 +752,7 @@
     return pl.pallas_call(
         out_weights_kernel,
         grid=(1,),
-        out_shape=store_shapes(pieces, GRAD_TILES),
+        out_shape=store_shapes(pieces, FIRST_TILES),
         in_specs=[SMEM_SPEC, full, full],
         out_specs=(HBM_SPEC,) * len(pieces),
         scratch_shapes=[
@@ -761,32 +765,40 @@
     )(ids, mixed, gbranch)
 
 
-def attend_back_kernel(ids_rows, ids, lengths, order, mask, bias, q, k, v, mixed, gmixed, lse, sums,
+def attend_back_kernel(ids_rows, base, steps, ids, lengths, order, mask, bias, q, k, v, mixed, gmixed, lse, sums,
                        up_sums, xs_far, gres, *rest):
     scratch = rest[-17:]
-    count = (len(rest) - 17 - 2) // 3
+    done = base + steps == GROUPS
+    count = (len(rest) - 17 - 2) // (2 if done else 3)
     pieces = rest[:count]
-    own, send, *gw_outs = rest[2 * count : -17]
+    if done:
+        own, send, *gw_outs = rest[count:-17]
+    else:
+        gx_out, vectors_out, *gw_outs = rest[2 * count : -17]
     (vectors, turned, vector_sems, gk, gv, gdist, gx, gq, inner, weights, buffer, xs, rows_out, sems, in_sems, out_sems,
      row_sems) = scratch
-    group = pl.program_id(0)
+    step = pl.program_id(0)
+    group = base + step
+    tiles = slice(3 * base, 3 * (base + steps))
     length = mask.shape[1]
     rows = xs.shape[1] // (2 * gw_outs[0].shape[0]) if count > 2 else ids_rows
-    loads = block_copies(ids, pieces, weights, sems, slice(0, 3 * GROUPS)) + [
+    loads = block_copies(ids, pieces, weights, sems, tiles) + [
         pltpu.make_async_copy(xs_far, xs, in_sems.at[0]),
         pltpu.make_async_copy(gres, gx, in_sems.at[1]),
     ]
 
     def stores(index):
-        slot = index % 2
         return block_stores(
-            ids, buffer.at[slot], gw_outs, out_sems.at[slot], pl.ds(3 * index, 3)
+            ids, buffer.at[index], gw_outs, out_sems.at[index],
+            slice(0, 3) if done else pl.ds(3 * (base + index), 3),
         )
 
-    @pl.when(group == 0)
+    @pl.when(step == 0)
     def _():
         for copy in loads:
             copy.start()
+        if base:
+            vectors[0:16, :] = sums[8:24, :]
 
     gdist[...] = jnp.zeros_like(gdist)
     gk[...] = jnp.zeros_like(gk)
@@ -847,34 +859,28 @@
     gk_low = gk[...].astype(jnp.bfloat16)
     gv_low = gv[...].astype(jnp.bfloat16)
 
-    @pl.when(group == 0)
+    @pl.when(step == 0)
     def _():
         for copy in loads:
             copy.wait()
 
-    @pl.when(group == 2)
-    def _():
-        for copy in stores(0):
-            copy.wait()
-
-    slot = lax.rem(group, 2)
     for index, grad in enumerate((
         product(xs[...], gq_low, TN),
         product(xs[0:length, :], gk_low, TN),
         product(xs[0:length, :], gv_low, TN),
     )):
         grad = grad.astype(jnp.bfloat16)
-        buffer[slot, 0, index] = grad[:, :128]
-        buffer[slot, 1, index] = grad[:, 128:]
-    for index in range(GROUPS):
-        @pl.when(group == index)
+        buffer[step, 0, index] = grad[:, :128]
+        buffer[step, 1, index] = grad[:, 128:]
+    for index in range(steps):
+        @pl.when(step == index)
         def _():
             for copy in stores(index):
                 copy.start()
 
-    gx[...] += product(gq_low, joined(weights, 3 * group), NT)
-    gx[0:length, :] += product(gk_low, joined(weights, 3 * group + 1), NT) + product(
-        gv_low, joined(weights, 3 * group + 2), NT
+    gx[...] += product(gq_low, joined(weights, 3 * step), NT)
+    gx[0:length, :] += product(gk_low, joined(weights, 3 * step + 1), NT) + product(
+        gv_low, joined(weights, 3 * step + 2), NT
     )
     lanes = pl.ds(pl.multiple_of(group * LANES, LANES), LANES)
     vectors[0:1, lanes] = column_sum(gq_low.astype(jnp.float32))
@@ -914,15 +920,19 @@
     right = (head < GROUP) & (entry % HEADS == GROUP * group + head)
     table = column_sum(jnp.where(right, table, 0.0))
 
-    @pl.when(group == 0)
-    def _():
+    if base:
+        vectors[12:13, :] += table
+    else:
         vectors[12:13, :] = table
 
-    @pl.when(group > 0)
-    def _():
-        vectors[12:13, :] += table
-
-    @pl.when(group == GROUPS - 1)
+    if not done:
+        for copy in stores(0):
+            copy.wait()
+        vectors_out[...] = vectors[0:16, :]
+        run_copies([pltpu.make_async_copy(gx, gx_out, in_sems.at[0])])
+        return
+
+    @pl.when(step == steps - 1)
     def _():
         put_back(
             ids, order_onehot(ids, order),
@@ -936,11 +946,12 @@
         turned[0, 0] = tile
         turned[1, 0] = tile
         last = block_stores(
-            ids, turned, gw_outs, vector_sems, slice(VECTOR_TILE, VECTOR_TILE + 1)
+            ids, turned, gw_outs, vector_sems, slice(3, LAST_TILES)
         )
         for copy in last:
             copy.start()
-        for copy in stores(1) + stores(2) + last:
+        waits = [copy for index in range(steps) for copy in stores(index)]
+        for copy in waits + last:
             copy.wait()
 
 
@@ -964,38 +975,41 @@
     return total[0:4, :]
 
 
-def attend_back(ids, lengths, order, xs, mask, bias, q, k, v, mixed, gmixed, lse, sums, up_sums,
-                gres, pieces, grads, rows_each):
+def attend_back(base, steps, ids, lengths, order, xs, mask, bias, q, k, v, mixed, gmixed, lse,
+                sums, up_sums, gres, pieces, grads, rows_each):
     tokens, width = xs.shape
     length = mask.shape[1]
     blocks = sum(piece.shape[0] for piece in pieces)
-    column = lambda g: (0, g)
+    done = base + steps == GROUPS
+    column = lambda g: (0, base + g)
     rows = SDS((2, length // 2, width), jnp.bfloat16)
     first = 15 + len(pieces)
+    if done:
+        outs, out_specs = (rows, rows), (HBM_SPEC, HBM_SPEC)
+    else:
+        outs = (SDS((tokens, width), jnp.float32), SDS((16, width), jnp.float32))
+        out_specs = (HBM_SPEC, pl.BlockSpec((16, width), lambda g: (0, 0)))
     return pl.pallas_call(
-        functools.partial(attend_back_kernel, rows_each),
-        grid=(GROUPS,),
-        out_shape=(
-            rows,
-            rows,
-        ) + store_shapes(pieces, GRAD_TILES),
-        input_output_aliases={first + index: 2 + index for index in range(len(pieces))},
+        functools.partial(attend_back_kernel, rows_each, base, steps),
+        grid=(steps,),
+        out_shape=outs + store_shapes(pieces, LAST_TILES if done else FIRST_TILES),
+        input_output_aliases={first + index: 2 + index for index in range(len(grads))},
         in_specs=[
             SMEM_SPEC,
             SMEM_SPEC,
             VMEM_SPEC,
             pl.BlockSpec((2, length, length), lambda g: (0, 0, 0), pipeline_mode=pl.Buffered(1)),
-            pl.BlockSpec((GROUP, TILE, SPAN), lambda g: (g, 0, 0)),
+            pl.BlockSpec((GROUP, TILE, SPAN), lambda g: (base + g, 0, 0)),
             pl.BlockSpec((tokens, LANES), column),
             pl.BlockSpec((length, LANES), column),
             pl.BlockSpec((length, LANES), column),
             pl.BlockSpec((tokens, LANES), column),
             pl.BlockSpec((tokens, LANES), column),
-            pl.BlockSpec((1, tokens, 128), lambda g: (g, 0, 0)),
-            pl.BlockSpec((8, width), lambda g: (0, 0)),
+            pl.BlockSpec((1, tokens, 128), lambda g: (base + g, 0, 0)),
+            pl.BlockSpec(sums.shape, lambda g: (0, 0)),
             pl.BlockSpec((1, 4 * width), lambda g: (0, 0)),
-        ] + [HBM_SPEC] * (2 + 2 * len(pieces)),
-        out_specs=(HBM_SPEC,) * (2 + len(pieces)),
+        ] + [HBM_SPEC] * (2 + len(pieces) + len(grads)),
+        out_specs=out_specs + (HBM_SPEC,) * len(pieces),
         scratch_shapes=[
             pltpu.VMEM((128, width), jnp.float32),
             pltpu.VMEM((2, 1, width, 128), jnp.bfloat16),
@@ -1006,20 +1020,26 @@
             pltpu.VMEM((tokens, width), jnp.float32),
             pltpu.VMEM((tokens, LANES), jnp.float32),
             pltpu.VMEM((tokens, GROUP * 128), jnp.float32),
-            pltpu.VMEM((2, 3 * GROUPS, width, 128), jnp.bfloat16),
-            pltpu.VMEM((2, 2, 3, width, 128), jnp.bfloat16),
+            pltpu.VMEM((2, 3 * steps, width, 128), jnp.bfloat16),
+            pltpu.VMEM((steps, 2, 3, width, 128), jnp.bfloat16),
             pltpu.VMEM((tokens, width), jnp.bfloat16),
             pltpu.VMEM((2, 2, length // 2, width), jnp.bfloat16),
             pltpu.SemaphoreType.DMA((blocks,)),
             pltpu.SemaphoreType.DMA((2,)),
-            pltpu.SemaphoreType.DMA((2, blocks)),
+            pltpu.SemaphoreType.DMA((steps, blocks)),
             pltpu.SemaphoreType.DMA((2,)),
         ],
-        cost_estimate=cost(27),
+        cost_estimate=cost(14 * steps),
         compiler_params=params(("arbitrary",), FULL),
         name="attend_back",
     )(ids, lengths, order, mask, bias, q, k, v, mixed, gmixed, lse, sums, up_sums,
       *in_hbm(xs, gres, *pieces, *grads))
+
+
+def grad_tile(index, group):
+    if index == 3:
+        return 2 * GROUPS + group
+    return index + (3 * group if group < GROUPS - 1 else FIRST_TILES)
 
 
 def finish_kernel(ids, own, came, wq, wk, wv, wo, *vectors):
@@ -1028,10 +1048,10 @@
         mine = half == place
         for index, out in enumerate((wq, wk, wv, wo)):
             for group in range(GROUPS):
-                tile = 3 * group + index if index < 3 else 3 * GROUPS + group
+                tile = grad_tile(index, group)
                 lane = group * LANES + place * 128
                 out[:, lane : lane + 128] = jnp.where(mine, own[tile], came[tile])
-    turned = jnp.transpose(own[VECTOR_TILE])
+    turned = jnp.transpose(own[FIRST_TILES + 3])
     rows = own.shape[1]
     for index, out in enumerate(vectors):
         if index == UP_SLOT:
@@ -1074,11 +1094,12 @@
     return lax.ppermute(value, "seq", [(0, 1), (1, 0)])
 
 
+def high_part(value, high, count):
+    return lax.ppermute(value, BOTH, xor_pairs(count, (4 * high, 4 * high)))
+
+
 def high_parts(value, count):
-    return [
-        lax.ppermute(value, BOTH, xor_pairs(count, (4 * high, 4 * high)))
-        for high in range(1, count // 4)
-    ]
+    return [high_part(value, high, count) for high in range(1, count // 4)]
 
 
 def low_round(value, count):
@@ -1131,26 +1152,33 @@
     sizes = [vector.shape[0] for vector in vectors]
     theirs, square, feed_own, slots = pack(
         ids, content, query_in, content_cot, query_cot, query_weight, key_weight, value_weight,
-        out_weight, up_weight, down_weight, vectors,
+        out_weight, jnp.transpose(up_weight), down_weight, vectors,
     )
 
     square_parts = high_parts(square, count)
+    came = swap(theirs)
+    slots = after(slots, came)
     slots_high = jnp.stack([slots] + high_parts(slots, count))
-    came = swap(theirs)
     xs, cs, mask = sort_rows(
         ids, lengths, (content, query_in, content_cot, query_cot), came, order
     )
-    square_parts = lax.optimization_barrier((square_parts, xs, slots_high))[0]
+    feed_early = high_part(after(feed_own, came), 2, count)
+    square_parts, xs, slots_high = lax.optimization_barrier((square_parts, xs, slots_high))
     square_near = low_round(jnp.stack([square] + square_parts), count)
-    feed_own = after(feed_own, square_parts)
-    feed_parts = high_parts(feed_own, count)
     slots_near = low_round(slots_high, count)
-    square_near = after(square_near, slots_near)
+    square_near, slots_near, feed_early = lax.optimization_barrier(
+        (square_near, slots_near, feed_early)
+    )
     square_far = last_round(square_near, count)
     slots_far = last_round(slots_near, count)
     near_swapped = swap(square_near)
     square_far = after(square_far, slots_far, near_swapped)
     far_swapped = swap(square_far)
+    feed_later = after(feed_own, square_near)
+    feed_parts = [
+        feed_early if high == 2 else high_part(feed_later, high, count)
+        for high in range(1, count // 4)
+    ]
     feed_parts = lax.optimization_barrier((feed_parts, square_far))[0]
     feed_near = low_round(jnp.stack([feed_own] + feed_parts), count)
     vector_rows, up_biases, bias = vectors_to_all(ids, slots_near, slots_far, width, sizes)
@@ -1210,34 +1238,67 @@
         return total
 
     gwo = out_weights(ids, after(mixed, far_own), gbranch, pieces)
-    far = low(swapped_sum(far_own, far_other))
-    gdown, far, _ = lax.optimization_barrier((gdown, far, gwo[0]))
-    far = last_round(far, count)
+    far_came, _ = lax.optimization_barrier((swap(far_other), gwo[0]))
+    far_first, far_second = (
+        low(wide(halved(far_own)[part]) + wide(halved(far_came)[part])) for part in range(2)
+    )
+    gmixed, far_first, far_second = lax.optimization_barrier((gmixed, far_first, far_second))
+    far_first = last_round(far_first, count)
+    heads = functools.partial(
+        attend_back, ids=ids, lengths=lengths, order=order, xs=xs, mask=mask, bias=bias, q=q, k=k,
+        v=v, mixed=mixed, lse=lse, up_sums=up_sums, pieces=pieces, rows_each=rows,
+    )
+    gx, head_sums, *gws = heads(0, 1, gmixed=gmixed, sums=sums, gres=gres, grads=gwo)
+    gdown, far_first, far_second, gx = lax.optimization_barrier(
+        (gdown, far_first, far_second, gx)
+    )
+    far_second = last_round(far_second, count)
     near_own, near_other = feed_weights(0, act, gup, first, gdown, shape)
-    far, near_other = lax.optimization_barrier((far, near_other))
+    far_second, near_own, near_other = lax.optimization_barrier(
+        (far_second, near_own, near_other)
+    )
     near_came = swap(near_other)
-    outs = unsort_rows(ids, order, after(out, far))
-    near_came, near_own, far, _ = lax.optimization_barrier(
-        (near_came, near_own, far, outs[0])
-    )
-    near = wide(near_own) + wide(near_came) + wide(far)
-    gmixed, near = lax.optimization_barrier((gmixed, near))
-    gfeed_came = lax.ppermute(low(halved(near)[1]), BOTH, xor_pairs(count, (1, 2)))
-    grad_own, grad_send, *gws = attend_back(
-        ids, lengths, order, xs, mask, bias, q, k, v, mixed, gmixed, lse, sums, up_sums, gres,
-        pieces, gwo, rows,
-    )
-    gfeed_came, *gws = lax.optimization_barrier((gfeed_came, *gws))
-    gfeed = halved(near)[0] + wide(gfeed_came)
-    gfeed_parts = high_parts_of(gfeed, count)
+    outs = unsort_rows(ids, order, after(out, far_second))
+    near_came, near_own, _ = lax.optimization_barrier((near_came, near_own, outs[0]))
+    far_halves = (far_first, far_second)
+    near_halves = [
+        wide(halved(near_own)[part]) + wide(halved(near_came)[part]) + wide(far_halves[part])
+        for part in range(2)
+    ]
+    gx, to_send = lax.optimization_barrier((gx, low(near_halves[1])))
+    gfeed_came = lax.ppermute(to_send, BOTH, xor_pairs(count, (1, 2)))
+    gx, head_sums, *gws = result = heads(
+        1, 1, gmixed=gmixed, sums=jnp.concatenate([sums, head_sums]), gres=gx, grads=gws
+    )
+    gfeed_came, gx = lax.optimization_barrier((gfeed_came, gx))
+    gfeed = near_halves[0] + wide(gfeed_came)
+    gfeed_low = [low(gfeed[high]) for high in range(1, count // 4)]
+    gx, gfeed_low = lax.optimization_barrier((gx, gfeed_low))
+    early = high_part(gfeed_low[1], 2, count)
+    most = by_device(result[2:])
+    most_came = [swap(part) for part in most[2:]]
+    grad_own, grad_send, *gws = heads(
+        2, 1, gmixed=gmixed, sums=jnp.concatenate([sums, head_sums]), gres=gx, grads=()
+    )
+    early, most_came, gws = lax.optimization_barrier((early, most_came, gws))
+    last = by_device(gws)
+    most_far = last_round(low(wide(most[1]) + wide(most_came[1])), count)
+    last_came = [swap(part) for part in last[2:]]
+    last_far = last_round(low(wide(last[1]) + wide(last_came[1])), count)
+    gfeed_parts = [
+        early if high == 2 else high_part(gfeed_low[high - 1], high, count)
+        for high in range(1, count // 4)
+    ]
     outs = place_rows(half, *outs)
-    gws = by_device(gws)
-    gw_far = last_round(low(swapped_sum(gws[1], gws[3])), count)
-    near_came = swap(gws[2])
-    gw_far, near_came = lax.optimization_barrier((gw_far, near_came))
-    gw = wide(gws[0]) + wide(near_came) + wide(gw_far)
+    grads = place_rows(half, grad_own, grad_send)
+    most_far, last_far, last_came, gfeed_parts = lax.optimization_barrier(
+        (most_far, last_far, last_came, gfeed_parts)
+    )
+    gw = jnp.concatenate([
+        wide(most[0]) + wide(most_came[0]) + wide(most_far),
+        wide(last[0]) + wide(last_came[0]) + wide(last_far),
+    ], axis=1)
     gw_came = lax.ppermute(low(halved(gw)[1]), BOTH, xor_pairs(count, (1, 2)))
-    gw_came, gfeed_parts = lax.optimization_barrier((gw_came, gfeed_parts))
     gw = halved(gw)[0] + wide(gw_came)
     gw_parts = high_parts_of(gw, count)
     gfeed = own_sum(gfeed, gfeed_parts)
@@ -1247,8 +1308,6 @@
     gw = own_sum(gw, gw_parts)
     query_grad, key_grad, value_grad, out_grad, *ends = finish(ids, gw, swap(gw), sizes)
     ends = [end.reshape(-1) for end in ends]
-    grads = place_rows(half, grad_own, grad_send)
-
     return (
         outs[0], outs[1], grads[0], grads[1],
         query_grad, ends[0], key_grad, value_grad, ends[1], out_grad, ends[2], ends[3], ends[4],

time: 352 us -> 320 us (0.909)
  waiting for transfers between devices: 114 us -> 86.2 us
  local copies, waits for them, and re-layouts: 25.1 us -> 14.3 us
    ppermute x6 -> x3, waiting for transfers between devices: 34.2 us -> 11.1 us  [high_parts_of(): lax.ppermute(low(total[high]), BOTH, xor_pairs(count, (4 * high, 4 * high)))]
    ppermute x5 -> x7, waiting for transfers between devices: 44.5 us -> 25 us  [last_round(): return lax.ppermute(value, BOTH, xor_pairs(count, (2, 1)))]
    unnamed x55 -> x74, local copies, waits for them, and re-layouts: 18 us -> 8.27 us
    ppermute x1, waiting for transfers between devices: 0.01 us -> 7.96 us  [shards(): gw_came = lax.ppermute(low(halved(gw)[1]), BOTH, xor_pairs(count, (1, 2)))]
    ppermute x13 -> x15, starting transfers between devices: 1.48 us -> 7.01 us  [swap(): return lax.ppermute(value, 'seq', [(0, 1), (1, 0)])]
    ppermute x10 -> x13, waiting for transfers between devices: 13.4 us -> 17.9 us  [the longest x12 17.9 us: high_part(): return lax.ppermute(value, BOTH, xor_pairs(count, (4 * high, 4 * high)))]
    ppermute x6 -> x3, starting transfers between devices: 8 us -> 3.55 us  [high_parts_of(): lax.ppermute(low(total[high]), BOTH, xor_pairs(count, (4 * high, 4 * high)))]
    pallas_call x1 -> x3, Pallas kernels: 40.4 us -> 43.9 us  [attend_back(): pl.pallas_call(functools.partial(attend_back_kernel, rows_each, base, ste...]
  transfers between devices with their start and end apart: 38 -> 42, of which waited for: 18 -> 20; matrix products, arithmetic and copies ran while one was open for 6% -> 7% of each run, Pallas kernels for 27% -> 30%
where the time goes in v3:
time: 320 us; the launch traced here: 314 us
  Pallas kernels  150 us (47%)
  waiting for transfers between devices  86.2 us (27%)
  starting transfers between devices  40.1 us (13%)
  other arithmetic  21.3 us (7%)
  local copies, waits for them, and re-layouts  14.3 us (4%)
    pallas_call x3, Pallas kernels, attend_back(): pl.pallas_call(functools.partial(attend_back_kernel, rows_each, base, ste...  43.9 us
    pallas_call x1, Pallas kernels, feed(): pl.pallas_call(feed_kernel, grid=(tokens // BLOCK,), out_shape=(low, SDS(...  37.5 us
    ppermute x7, waiting for transfers between devices, last_round(): return lax.ppermute(value, BOTH, xor_pairs(count, (2, 1)))  25 us
    pallas_call x2, Pallas kernels, feed_weights(): pl.pallas_call(feed_weights_kernel, grid=(2, 2), out_shape=(SDS(shape, jn...  22.9 us
    pallas_call x1, Pallas kernels, attend(): pl.pallas_call(attend_kernel, grid=(GROUPS,), out_shape=(SDS((tokens, wid...  20.1 us
    ppermute x12, waiting for transfers between devices, high_part(): return lax.ppermute(value, BOTH, xor_pairs(count, (4 * high, 4 * high)))  17.9 us
    ppermute x12, starting transfers between devices, high_part(): return lax.ppermute(value, BOTH, xor_pairs(count, (4 * high, 4 * high)))  17.1 us
    ppermute x3, waiting for transfers between devices, low_round(): lax.ppermute(value, BOTH, xor_pairs(count, (1, 2)))  15.6 us
  transfers between devices with their start and end apart: 42, of which 20 were waited for; matrix products, arithmetic and copies ran while one was open for 7% of the time, Pallas kernels for 30%

profile of v3, /device:TPU:0, one launch (start us, length us, event | category | flops | bytes accessed | tf_op | source)
XLA Modules:
  0.0 313.6 jit_solution(1039434150898764092)
XLA Ops:
  2.5 4.4 %pack.1 = (bf16[4,256,768]{2,1,0:T(8,128)(2,1)}, bf16[12,48,128]{2,1,0:T(8,128)(2,1)}, bf16[2,96,768]{2,1,0:T(8,128)(2,1)}, bf16[16,256]{1,0:T(8,128)(2,1)}) custom-call(s32[2]{0:T(128)} %pad_add_fusion.ids, bf16[2,256,768]{2,1,0:T(8,128)(2,1)} %content.3, bf16[2,256,768]{2,1,0:T(8,128)(2,1)} %query.3, bf16[2,256,768]{2,1,0:T(8,128)(2,1)} %ccot.3, ...), custom_call_target="tpu_custom_call" | custom-call | bytes 6400000 | tf_op jit(solution)/shard_map/pack/pallas_call | solution.py:115
  10.7 5.0 %collective-permute-start.6 = (bf16[16,256]{1,0:T(8,128)(2,1)}, bf16[16,256]{1,0:T(8,128)(2,1)S(1)}, u32[]{:S(2)}, u32[]{:S(2)}) collective-permute-start(bf16[16,256]{1,0:T(8,128)(2,1)} %get-tuple-element.144), channel_id=1, source_target_pairs={{0,24},{1,25},{2,26},{3,27},{4,28},{5,29},{6,30},{7,31},{8,16},{9,... | collective-permute-start | bytes 24584 | tf_op jit(solution)/shard_map/ppermute | solution.py:1098
  21.7 6.4 %sort_rows.1 = (bf16[1024,768]{1,0:T(8,128)(2,1)}, bf16[1024,768]{1,0:T(8,128)(2,1)}, bf16[2,512,512]{2,1,0:T(8,128)(2,1)}) custom-call(s32[2]{0:T(128)} %pad_add_fusion.ids, s32[2,8]{1,0:T(2,128)} %lengths.9, bf16[2,256,768]{2,1,0:T(8,128)(2,1)} %content.3, bf16[2,256,768]{2,1,0:T(8,128)(2,1)} %query.3, bf16[2,256,768]{2,1,0:T(8,128)(2,1)} %ccot.3, ...), custom_call_target="tpu_custom_call" | custom-call | bytes 8000000 | tf_op jit(solution)/shard_map/sort_rows/pallas_call | solution.py:191
  32.9 8.1 %collective-permute-done.8 = bf16[4,16,256]{2,1,0:T(8,128)(2,1)S(1)} collective-permute-done((bf16[4,16,256]{2,1,0:T(8,128)(2,1)S(1)}, bf16[4,16,256]{2,1,0:T(8,128)(2,1)S(1)}, u32[]{:S(2)}, u32[]{:S(2)}) %collective-permute-start.8) | collective-permute-done | bytes 32800 | tf_op jit(solution)/shard_map/ppermute | solution.py:1106
  41.1 3.7 %collective-permute-done.9 = bf16[2,96,768]{2,1,0:T(8,128)(2,1)S(1)} collective-permute-done((bf16[2,96,768]{2,1,0:T(8,128)(2,1)S(1)}, bf16[2,96,768]{2,1,0:T(8,128)(2,1)S(1)}, u32[]{:S(2)}, u32[]{:S(2)}) %collective-permute-start.9) | collective-permute-done | bytes 294944 | tf_op jit(solution)/shard_map/ppermute | solution.py:1098
  48.8 12.9 %collective-permute-done.10.far = bf16[8,16,256]{2,1,0:T(8,128)(2,1)S(1)} collective-permute-done((bf16[8,16,256]{2,1,0:T(8,128)(2,1)S(1)}, bf16[8,16,256]{2,1,0:T(8,128)(2,1)S(1)}, u32[]{:S(2)}, u32[]{:S(2)}) %collective-permute-start.10) | collective-permute-done | bytes 65568 | tf_op jit(solution)/shard_map/ppermute | solution.py:1110
  67.7 3.7 %vectors.1 = (f32[8,768]{1,0:T(8,128)}, f32[1,3072]{1,0:T(1,128)}, bf16[12,128,640]{2,1,0:T(8,128)(2,1)}) custom-call(s32[2]{0:T(128)} %pad_add_fusion.ids, bf16[8,16,256]{2,1,0:T(8,128)(2,1)} %copy-done.25, bf16[8,16,256]{2,1,0:T(8,128)(2,1)} %copy-done.27), custom_call_target="tpu_custom_call" | custom-call | bytes 9600000 | tf_op jit(solution)/shard_map/vectors/pallas_call | solution.py:382
  74.7 7.5 %collective-permute-done.16 = bf16[4,2,96,768]{3,2,1,0:T(8,128)(2,1)} collective-permute-done((bf16[4,2,96,768]{3,2,1,0:T(8,128)(2,1)}, bf16[4,2,96,768]{3,2,1,0:T(8,128)(2,1)}, u32[]{:S(2)}, u32[]{:S(2)}) %collective-permute-start.16) | collective-permute-done | bytes 1179680 | tf_op jit(solution)/shard_map/ppermute | solution.py:1106
  86.2 20.1 %attend.1 = (bf16[1024,768]{1,0:T(8,128)(2,1)}, bf16[512,768]{1,0:T(8,128)(2,1)}, bf16[512,768]{1,0:T(8,128)(2,1)}, bf16[1024,768]{1,0:T(8,128)(2,1)}, f32[3,1024,128]{2,1,0:T(8,128)}) custom-call(s32[2]{0:T(128)} %pad_add_fusion.ids, s32[2,8]{1,0:T(2,128)} %lengths.9, bf16[1024,768]{1,0:T(8,128)(2,1)} %get-tuple-element.145.xs.xs_far, ...), custom_call_target="tpu_custom_call" | custom-call | bytes 28800000 | tf_op jit(solution)/shard_map/attend/pallas_call | solution.py:523
  106.3 7.4 %collective-permute-done.18.far_own = bf16[8,2,96,768]{3,2,1,0:T(8,128)(2,1)S(1)} collective-permute-done((bf16[8,2,96,768]{3,2,1,0:T(8,128)(2,1)}, bf16[8,2,96,768]{3,2,1,0:T(8,128)(2,1)S(1)}, u32[]{:S(2)}, u32[]{:S(2)}) %collective-permute-start.18) | collective-permute-done | bytes 2359328 | tf_op jit(solution)/shard_map/ppermute | solution.py:1110
  113.7 4.5 %collective-permute-done.19.far_other = bf16[8,2,96,768]{3,2,1,0:T(8,128)(2,1)S(1)} collective-permute-done((bf16[8,2,96,768]{3,2,1,0:T(8,128)(2,1)S(1)}, bf16[8,2,96,768]{3,2,1,0:T(8,128)(2,1)S(1)}, u32[]{:S(2)}, u32[]{:S(2)}) %collective-permute-start.19) | collective-permute-done | bytes 2359328 | tf_op jit(solution)/shard_map/ppermute | solution.py:1094
  119.7 37.5 %feed.1 = (bf16[1024,768]{1,0:T(8,128)(2,1)}, bf16[1024,3072]{1,0:T(8,128)(2,1)}, bf16[1024,3072]{1,0:T(8,128)(2,1)}, bf16[1024,768]{1,0:T(8,128)(2,1)}, bf16[10...) custom-call(s32[2]{0:T(128)} %pad_add_fusion.ids, ...), custom_call_target="tpu_custom_call" | custom-call | bytes 57600000 | tf_op jit(solution)/shard_map/feed/pallas_call | solution.py:664
  157.3 11.6 %feed_weights.2 = (bf16[8,2,96,768]{3,2,1,0:T(8,128)(2,1)}, bf16[8,2,96,768]{3,2,1,0:T(8,128)(2,1)}) custom-call(bf16[1024,3072]{1,0:T(8,128)(2,1)} %get-tuple-element.171.act, bf16[1024,3072]{1,0:T(8,128)(2,1)} %get-tuple-element.172.gup, bf16[1024,768]{1,0:T(8,128)(2,1)} %get-tuple-element.173.first, bf16[1024,768]{1,0:T(8,128)(2,1)} %get-tuple-element.195.gdown), custom_call_target="tpu_custom_call" | custom-call | bytes 14400000 | tf_op jit(solution)/shard_map/feed_weights/pallas_call | solution.py:723
  169.0 4.8 %out_weights.1 = (bf16[8,9,48,128]{3,2,1,0:T(8,128)(2,1)}, bf16[8,9,48,128]{3,2,1,0:T(8,128)(2,1)}, bf16[8,9,48,128]{3,2,1,0:T(8,128)(2,1)}, bf16[8,9,48,128]{3,2,1,0:T(8,128)(2,1)}) custom-call(s32[2]{0:T(128)} %pad_add_fusion.ids, bf16[1024,768]{1,0:T(8,128)(2,1)} %get-tuple-element.176.mixed, bf16[1024,768]{1,0:T(8,128)(2,1)} %get-tuple-element.177.gbranch), custom_call_target="tpu_custom_call" | custom-call | bytes 6400000 | tf_op jit(solution)/shard_map/out_weights/pallas_call | solution.py:752
  178.7 13.9 %attend_back.3 = (f32[1024,768]{1,0:T(8,128)}, f32[16,768]{1,0:T(8,128)}, bf16[8,9,48,128]{3,2,1,0:T(8,128)(2,1)}, bf16[8,9,48,128]{3,2,1,0:T(8,128)(2,1)}, bf16...) custom-call(s32[2]{0:T(128)} %pad_add_fusion.ids, ...), custom_call_target="tpu_custom_call", output_to_operand_aliasing={{2}: (19, {}), {3}: (20, {}), {4}: (21, {}), {5}: (22, {})} | custom-call | bytes 22400000 | tf_op jit(solution)/shard_map/attend_back/pallas_call | solution.py:992
  195.1 11.4 %feed_weights.3 = (bf16[8,2,96,768]{3,2,1,0:T(8,128)(2,1)}, bf16[8,2,96,768]{3,2,1,0:T(8,128)(2,1)}) custom-call(bf16[1024,3072]{1,0:T(8,128)(2,1)} %get-tuple-element.171.act, bf16[1024,3072]{1,0:T(8,128)(2,1)} %get-tuple-element.172.gup, bf16[1024,768]{1,0:T(8,128)(2,1)} %get-tuple-element.173.first, bf16[1024,768]{1,0:T(8,128)(2,1)} %get-tuple-element.195.gdown), custom_call_target="tpu_custom_call" | custom-call | bytes 14400000 | tf_op jit(solution)/shard_map/feed_weights/pallas_call | solution.py:723
  210.9 4.4 %unsort_rows.1 = (bf16[2,256,768]{2,1,0:T(8,128)(2,1)}, bf16[2,256,768]{2,1,0:T(8,128)(2,1)}) custom-call(s32[2]{0:T(128)} %pad_add_fusion.ids, s32[2,512]{1,0:T(2,128)} %order.9, bf16[1024,768]{1,0:T(8,128)(2,1)} %get-tuple-element.199.values), custom_call_target="tpu_custom_call" | custom-call | bytes 4800000 | tf_op jit(solution)/shard_map/unsort_rows/pallas_call | solution.py:238
  215.6 3.7 %add_convert_fusion = bf16[4,2,96,768]{3,2,1,0:T(8,128)(2,1)} fusion(bf16[4,2,96,768]{3,2,1,0:T(8,128)(2,1)S(1)} %copy-done.16, bf16[8,2,96,768]{3,2,1,0:T(8,128)(2,1)S(1)} %collective-permute-done.24, bf16[8,2,96,768]{3,2,1,0:T(8,128)(2,1)} %get-tuple-element.206), kind=kLoop, calls=%fused_computation.3 | loop fusion | flops 3538944 | bytes 4718592 | tf_op jit(solution)/shard_map/convert_element_type | solution.py:1129
  220.5 13.6 %attend_back.4 = (f32[1024,768]{1,0:T(8,128)}, f32[16,768]{1,0:T(8,128)}, bf16[8,9,48,128]{3,2,1,0:T(8,128)(2,1)}, bf16[8,9,48,128]{3,2,1,0:T(8,128)(2,1)}, bf16...) custom-call(s32[2]{0:T(128)} %pad_add_fusion.ids, ...), custom_call_target="tpu_custom_call", output_to_operand_aliasing={{2}: (19, {}), {3}: (20, {}), {4}: (21, {}), {5}: (22, {})} | custom-call | bytes 22400000 | tf_op jit(solution)/shard_map/attend_back/pallas_call | solution.py:992
  242.5 16.4 %attend_back.5 = (bf16[2,256,768]{2,1,0:T(8,128)(2,1)}, bf16[2,256,768]{2,1,0:T(8,128)(2,1)}, bf16[8,4,48,128]{3,2,1,0:T(8,128)(2,1)}, bf16[8,4,48,128]{3,2,1,0:...) custom-call(s32[2]{0:T(128)} %pad_add_fusion.ids, s32[2,8]{1,0:T(2,128)} %lengths.9, ...), custom_call_target="tpu_custom_call" | custom-call | bytes 22400000 | tf_op jit(solution)/shard_map/attend_back/pallas_call | solution.py:992
  270.0 4.0 %collective-permute-done.34 = bf16[2,96,768]{2,1,0:T(8,128)(2,1)S(1)} collective-permute-done((bf16[2,96,768]{2,1,0:T(8,128)(2,1)S(1)}, bf16[2,96,768]{2,1,0:T(8,128)(2,1)S(1)}, u32[]{:S(2)}, u32[]{:S(2)}) %collective-permute-start.34) | collective-permute-done | bytes 294944 | tf_op jit(solution)/shard_map/ppermute | solution.py:1098
  274.0 6.0 %collective-permute-done.35 = bf16[2,96,768]{2,1,0:T(8,128)(2,1)S(1)} collective-permute-done((bf16[2,96,768]{2,1,0:T(8,128)(2,1)S(1)}, bf16[2,96,768]{2,1,0:T(8,128)(2,1)S(1)}, u32[]{:S(2)}, u32[]{:S(2)}) %collective-permute-start.35) | collective-permute-done | bytes 294944 | tf_op jit(solution)/shard_map/ppermute | solution.py:1098
  284.6 8.0 %collective-permute-done.36 = bf16[4,13,48,128]{3,2,1,0:T(8,128)(2,1)S(1)} collective-permute-done((bf16[4,13,48,128]{3,2,1,0:T(8,128)(2,1)S(1)}, bf16[4,13,48,128]{3,2,1,0:T(8,128)(2,1)S(1)}, u32[]{:S(2)}, u32[]{:S(2)}) %collective-permute-start.36) | collective-permute-done | bytes 639008 | tf_op jit(solution)/shard_map/ppermute | solution.py:1301
  303.5 5.4 %collective-permute-done.38 = bf16[13,48,128]{2,1,0:T(8,128)(2,1)S(1)} collective-permute-done((bf16[13,48,128]{2,1,0:T(8,128)(2,1)S(1)}, bf16[13,48,128]{2,1,0:T(8,128)(2,1)S(1)}, u32[]{:S(2)}, u32[]{:S(2)}) %collective-permute-start.38) | collective-permute-done | bytes 159776 | tf_op jit(solution)/shard_map/ppermute | solution.py:1230
  (178 shorter events, 87.8 us)
Async XLA Ops:
  15.7 14.8 %collective-permute-start.2 = (bf16[12,48,128]{2,1,0:T(8,128)(2,1)}, bf16[12,48,128]{2,1,0:T(8,128)(2,1)S(1)}, u32[]{:S(2)}, u32[]{:S(2)}) collective-permute-start(bf16[12,48,128]{2,1,0:T(8,128)(2,1)} %get-tuple-element.140), channel_id=1, source_target_pairs={{0,24},{1,25},{2,26},{3,27},{4,28},{5,29},{6,30},{7,31},{8,16},{9,... | collective-permute-start | bytes 442376 | tf_op jit(solution)/shard_map/ppermute | solution.py:1098
  15.7 14.8 %collective-permute-start.1 = (bf16[12,48,128]{2,1,0:T(8,128)(2,1)}, bf16[12,48,128]{2,1,0:T(8,128)(2,1)S(1)}, u32[]{:S(2)}, u32[]{:S(2)}) collective-permute-start(bf16[12,48,128]{2,1,0:T(8,128)(2,1)} %get-tuple-element.140), channel_id=1, source_target_pairs={{0,16},{1,17},{2,18},{3,19},{4,20},{5,21},{6,22},{7,23},{8,24},{9,... | collective-permute-start | bytes 442376 | tf_op jit(solution)/shard_map/ppermute | solution.py:1098
  16.7 13.9 %collective-permute-start = (bf16[12,48,128]{2,1,0:T(8,128)(2,1)}, bf16[12,48,128]{2,1,0:T(8,128)(2,1)S(1)}, u32[]{:S(2)}, u32[]{:S(2)}) collective-permute-start(bf16[12,48,128]{2,1,0:T(8,128)(2,1)} %get-tuple-element.140), channel_id=1, source_target_pairs={{0,8},{1,9},{2,10},{3,11},{4,12},{5,13},{6,14},{7,15},{8,0},{9,1},... | collective-permute-start | bytes 442376 | tf_op jit(solution)/shard_map/ppermute | solution.py:1098
  30.5 14.3 %collective-permute-start.9 = (bf16[2,96,768]{2,1,0:T(8,128)(2,1)S(1)}, bf16[2,96,768]{2,1,0:T(8,128)(2,1)S(1)}, u32[]{:S(2)}, u32[]{:S(2)}) collective-permute-start(bf16[2,96,768]{2,1,0:T(8,128)(2,1)S(1)} %copy-done.11), channel_id=1, source_target_pairs={{0,16},{1,17},{2,18},{3,19},{4,20},{5,21},{6,22},{7,23},{8,24},{9,... | collective-permute-start | bytes 884744 | tf_op jit(solution)/shard_map/ppermute | solution.py:1098
  44.8 16.9 %collective-permute-start.12 = (bf16[8,12,48,128]{3,2,1,0:T(8,128)(2,1)S(1)}, bf16[8,12,48,128]{3,2,1,0:T(8,128)(2,1)S(1)}, u32[]{:S(2)}, u32[]{:S(2)}) collective-permute-start(bf16[8,12,48,128]{3,2,1,0:T(8,128)(2,1)S(1)} %constant_dynamic-update-slice_fusion.rest_0_), channel_id=1, source_target_pairs={{0,1},{1,0},{2,3},{3,2},{4,5},{5,4},{6,7},{7,6},{8,9},{9,8},{10,11... | collective-permute-start | bytes 3538952 | tf_op jit(solution)/shard_map/ppermute | solution.py:1094
  44.8 16.9 %collective-permute-start.11 = (bf16[8,12,48,128]{3,2,1,0:T(8,128)(2,1)S(1)}, bf16[8,12,48,128]{3,2,1,0:T(8,128)(2,1)S(1)}, u32[]{:S(2)}, u32[]{:S(2)}) collective-permute-start(bf16[8,12,48,128]{3,2,1,0:T(8,128)(2,1)S(1)} %constant_dynamic-update-slice_fusion.rest_0_), channel_id=1, source_target_pairs={{0,4},{1,3},{2,6},{3,1},{4,0},{5,7},{6,2},{7,5},{8,12},{9,11},{10,... | collective-permute-start | bytes 3538952 | tf_op jit(solution)/shard_map/ppermute | solution.py:1110
  46.3 15.4 %collective-permute-start.15 = (bf16[2,96,768]{2,1,0:T(8,128)(2,1)S(1)}, bf16[2,96,768]{2,1,0:T(8,128)(2,1)S(1)}, u32[]{:S(2)}, u32[]{:S(2)}) collective-permute-start(bf16[2,96,768]{2,1,0:T(8,128)(2,1)S(1)} %copy-done.12), channel_id=1, source_target_pairs={{0,24},{1,25},{2,26},{3,27},{4,28},{5,29},{6,30},{7,31},{8,16},{9,... | collective-permute-start | bytes 884744 | tf_op jit(solution)/shard_map/ppermute | solution.py:1098
  48.3 15.2 %collective-permute-start.14 = (bf16[2,96,768]{2,1,0:T(8,128)(2,1)S(1)}, bf16[2,96,768]{2,1,0:T(8,128)(2,1)}, u32[]{:S(2)}, u32[]{:S(2)}) collective-permute-start(bf16[2,96,768]{2,1,0:T(8,128)(2,1)S(1)} %copy-done.12), channel_id=1, source_target_pairs={{0,8},{1,9},{2,10},{3,11},{4,12},{5,13},{6,14},{7,15},{8,0},{9,1},... | collective-permute-start | bytes 884744 | tf_op jit(solution)/shard_map/ppermute | solution.py:1098
  48.3 13.4 %collective-permute-start.10 = (bf16[8,16,256]{2,1,0:T(8,128)(2,1)S(1)}, bf16[8,16,256]{2,1,0:T(8,128)(2,1)S(1)}, u32[]{:S(2)}, u32[]{:S(2)}) collective-permute-start(bf16[8,16,256]{2,1,0:T(8,128)(2,1)S(1)} %pad_maximum_fusion.5.near), channel_id=1, source_target_pairs={{0,4},{1,3},{2,6},{3,1},{4,0},{5,7},{6,2},{7,5},{8,12},{9,11},{10,... | collective-permute-start | bytes 196616 | tf_op jit(solution)/shard_map/ppermute | solution.py:1110
  65.7 16.5 %collective-permute-start.16 = (bf16[4,2,96,768]{3,2,1,0:T(8,128)(2,1)}, bf16[4,2,96,768]{3,2,1,0:T(8,128)(2,1)}, u32[]{:S(2)}, u32[]{:S(2)}) collective-permute-start(bf16[4,2,96,768]{3,2,1,0:T(8,128)(2,1)} %pad_maximum_fusion.1), channel_id=1, source_target_pairs={{0,2},{1,5},{2,0},{3,7},{4,6},{5,1},{6,4},{7,3},{8,10},{9,13},{10,... | collective-permute-start | bytes 3538952 | tf_op jit(solution)/shard_map/ppermute | solution.py:1106
  66.2 18.4 %collective-permute-start.13 = (bf16[8,12,48,128]{3,2,1,0:T(8,128)(2,1)S(1)}, bf16[8,12,48,128]{3,2,1,0:T(8,128)(2,1)}, u32[]{:S(2)}, u32[]{:S(2)}) collective-permute-start(bf16[8,12,48,128]{3,2,1,0:T(8,128)(2,1)S(1)} %collective-permute-done.11.rest_1_), channel_id=1, source_target_pairs={{0,1},{1,0},{2,3},{3,2},{4,5},{5,4},{6,7},{7,6},{8,9},{9,8},{10,11... | collective-permute-start | bytes 3538952 | tf_op jit(solution)/shard_map/ppermute | solution.py:1094
  84.7 29.1 %collective-permute-start.18 = (bf16[8,2,96,768]{3,2,1,0:T(8,128)(2,1)}, bf16[8,2,96,768]{3,2,1,0:T(8,128)(2,1)S(1)}, u32[]{:S(2)}, u32[]{:S(2)}) collective-permute-start(bf16[8,2,96,768]{3,2,1,0:T(8,128)(2,1)} %constant_dynamic-update-slice_fusion.5.near_own), channel_id=1, source_target_pairs={{0,4},{1,3},{2,6},{3,1},{4,0},{5,7},{6,2},{7,5},{8,12},{9,11},{10,... | collective-permute-start | bytes 7077896 | tf_op jit(solution)/shard_map/ppermute | solution.py:1110
  86.1 27.6 %collective-permute-start.17 = (bf16[8,2,96,768]{3,2,1,0:T(8,128)(2,1)}, bf16[8,2,96,768]{3,2,1,0:T(8,128)(2,1)}, u32[]{:S(2)}, u32[]{:S(2)}) collective-permute-start(bf16[8,2,96,768]{3,2,1,0:T(8,128)(2,1)} %constant_dynamic-update-slice_fusion.5.near_own), channel_id=1, source_target_pairs={{0,1},{1,0},{2,3},{3,2},{4,5},{5,4},{6,7},{7,6},{8,9},{9,8},{10,11... | collective-permute-start | bytes 7077896 | tf_op jit(solution)/shard_map/ppermute | solution.py:1094
  177.2 16.4 %collective-permute-start.21 = (bf16[4,2,96,768]{3,2,1,0:T(8,128)(2,1)}, bf16[4,2,96,768]{3,2,1,0:T(8,128)(2,1)S(1)}, u32[]{:S(2)}, u32[]{:S(2)}) collective-permute-start(bf16[4,2,96,768]{3,2,1,0:T(8,128)(2,1)} %get-tuple-element.180), channel_id=1, source_target_pairs={{0,4},{1,3},{2,6},{3,1},{4,0},{5,7},{6,2},{7,5},{8,12},{9,11},{10,... | collective-permute-start | bytes 3538952 | tf_op jit(solution)/shard_map/ppermute | solution.py:1110
  193.6 16.2 %collective-permute-start.22 = (bf16[4,2,96,768]{3,2,1,0:T(8,128)(2,1)S(1)}, bf16[4,2,96,768]{3,2,1,0:T(8,128)(2,1)S(1)}, u32[]{:S(2)}, u32[]{:S(2)}) collective-permute-start(bf16[4,2,96,768]{3,2,1,0:T(8,128)(2,1)S(1)} %get-tuple-element.194), channel_id=1, source_target_pairs={{0,4},{1,3},{2,6},{3,1},{4,0},{5,7},{6,2},{7,5},{8,12},{9,11},{10,... | collective-permute-start | bytes 3538952 | tf_op jit(solution)/shard_map/ppermute | solution.py:1110
  219.3 17.8 %collective-permute-start.25 = (bf16[4,2,96,768]{3,2,1,0:T(8,128)(2,1)}, bf16[4,2,96,768]{3,2,1,0:T(8,128)(2,1)}, u32[]{:S(2)}, u32[]{:S(2)}) collective-permute-start(bf16[4,2,96,768]{3,2,1,0:T(8,128)(2,1)} %add_convert_fusion), channel_id=1, source_target_pairs={{0,2},{1,5},{2,0},{3,7},{4,6},{5,1},{6,4},{7,3},{8,10},{9,13},{10,... | collective-permute-start | bytes 3538952 | tf_op jit(solution)/shard_map/ppermute | solution.py:1269
  234.1 24.8 %collective-permute-start.28 = (bf16[8,9,48,128]{3,2,1,0:T(8,128)(2,1)}, bf16[8,9,48,128]{3,2,1,0:T(8,128)(2,1)}, u32[]{:S(2)}, u32[]{:S(2)}) collective-permute-start(bf16[8,9,48,128]{3,2,1,0:T(8,128)(2,1)} %get-tuple-element.224), channel_id=1, source_target_pairs={{0,1},{1,0},{2,3},{3,2},{4,5},{5,4},{6,7},{7,6},{8,9},{9,8},{10,11... | collective-permute-start | bytes 2654216 | tf_op jit(solution)/shard_map/ppermute | solution.py:1094
  237.0 22.0 %collective-permute-start.29 = (bf16[8,9,48,128]{3,2,1,0:T(8,128)(2,1)}, bf16[8,9,48,128]{3,2,1,0:T(8,128)(2,1)}, u32[]{:S(2)}, u32[]{:S(2)}) collective-permute-start(bf16[8,9,48,128]{3,2,1,0:T(8,128)(2,1)} %get-tuple-element.225), channel_id=1, source_target_pairs={{0,1},{1,0},{2,3},{3,2},{4,5},{5,4},{6,7},{7,6},{8,9},{9,8},{10,11... | collective-permute-start | bytes 2654216 | tf_op jit(solution)/shard_map/ppermute | solution.py:1094
  240.5 18.4 %collective-permute-start.27 = (bf16[2,96,768]{2,1,0:T(8,128)(2,1)}, bf16[2,96,768]{2,1,0:T(8,128)(2,1)}, u32[]{:S(2)}, u32[]{:S(2)}) collective-permute-start(bf16[2,96,768]{2,1,0:T(8,128)(2,1)} %get-tuple-element.223), channel_id=1, source_target_pairs={{0,16},{1,17},{2,18},{3,19},{4,20},{5,21},{6,22},{7,23},{8,24},{9,... | collective-permute-start | bytes 884744 | tf_op jit(solution)/shard_map/ppermute | solution.py:1098
  241.9 25.6 %collective-permute-start.23 = (bf16[2,256,768]{2,1,0:T(8,128)(2,1)}, bf16[2,256,768]{2,1,0:T(8,128)(2,1)S(1)}, u32[]{:S(2)}, u32[]{:S(2)}) collective-permute-start(bf16[2,256,768]{2,1,0:T(8,128)(2,1)} %get-tuple-element.201), channel_id=1, source_target_pairs={{0,1},{1,0},{2,3},{3,2},{4,5},{5,4},{6,7},{7,6},{8,9},{9,8},{10,11... | collective-permute-start | bytes 2359304 | tf_op jit(solution)/shard_map/ppermute | solution.py:1094
  263.0 17.3 %collective-permute-start.30 = (bf16[8,9,48,128]{3,2,1,0:T(8,128)(2,1)S(1)}, bf16[8,9,48,128]{3,2,1,0:T(8,128)(2,1)S(1)}, u32[]{:S(2)}, u32[]{:S(2)}) collective-permute-start(bf16[8,9,48,128]{3,2,1,0:T(8,128)(2,1)S(1)} %add_convert_fusion.3), channel_id=1, source_target_pairs={{0,4},{1,3},{2,6},{3,1},{4,0},{5,7},{6,2},{7,5},{8,12},{9,11},{10,... | collective-permute-start | bytes 2654216 | tf_op jit(solution)/shard_map/ppermute | solution.py:1110
  265.0 15.0 %collective-permute-start.35 = (bf16[2,96,768]{2,1,0:T(8,128)(2,1)S(1)}, bf16[2,96,768]{2,1,0:T(8,128)(2,1)S(1)}, u32[]{:S(2)}, u32[]{:S(2)}) collective-permute-start(bf16[2,96,768]{2,1,0:T(8,128)(2,1)S(1)} %copy-done.23), channel_id=1, source_target_pairs={{0,24},{1,25},{2,26},{3,27},{4,28},{5,29},{6,30},{7,31},{8,16},{9,... | collective-permute-start | bytes 884744 | tf_op jit(solution)/shard_map/ppermute | solution.py:1098
  284.5 24.5 %collective-permute-start.41 = (f32[2,96,768]{2,1,0:T(8,128)S(1)}, f32[2,96,768]{2,1,0:T(8,128)S(1)}, u32[]{:S(2)}, u32[]{:S(2)}) collective-permute-start(f32[2,96,768]{2,1,0:T(8,128)S(1)} %fusion.5), channel_id=1, source_target_pairs={{0,1},{1,0},{2,3},{3,2},{4,5},{5,4},{6,7},{7,6},{8,9},{9,8},{10,11... | collective-permute-start | bytes 1769480 | tf_op jit(solution)/shard_map/ppermute | solution.py:1094
  295.9 12.9 %collective-permute-start.38 = (bf16[13,48,128]{2,1,0:T(8,128)(2,1)S(1)}, bf16[13,48,128]{2,1,0:T(8,128)(2,1)S(1)}, u32[]{:S(2)}, u32[]{:S(2)}) collective-permute-start(bf16[13,48,128]{2,1,0:T(8,128)(2,1)S(1)} %get-tuple-element.281), channel_id=1, source_target_pairs={{0,16},{1,17},{2,18},{3,19},{4,20},{5,21},{6,22},{7,23},{8,24},{9,... | collective-permute-start | bytes 479240 | tf_op jit(solution)/shard_map/ppermute | solution.py:1230
  (51 other events, 416.7 us)

commit v4 on v3

--- a/solution.py
+++ b/solution.py
@@ -26,6 +26,7 @@
 NT = (((1,), (1,)), ((), ()))
 TN = (((0,), (0,)), ((), ()))
 VMEM_SPEC = pl.BlockSpec(memory_space=pltpu.VMEM)
+ANY_SPEC = pl.BlockSpec(memory_space=pl.ANY)
 HBM_SPEC = pl.BlockSpec(memory_space=pltpu.HBM)
 SCALE = 1.6e6
 SMEM_SPEC = pl.BlockSpec(memory_space=pltpu.SMEM)
@@ -214,10 +215,10 @@
         rows = product(onehot, source(stream), TN).astype(jnp.bfloat16)
         scratch[0, stream] = rows[:block, :]
         scratch[1, stream] = rows[block:, :]
-    run_copies([
+    return [
         pltpu.make_async_copy(scratch.at[ids[HALF]], own, sems.at[0]),
         pltpu.make_async_copy(scratch.at[1 - ids[HALF]], send, sems.at[1]),
-    ])
+    ]
 
 
 def unsort_kernel(ids, order, values, own, send, held, scratch, sems):
@@ -226,9 +227,9 @@
     copy.start()
     onehot = order_onehot(ids, order)
     copy.wait()
-    put_back(
+    run_copies(put_back(
         ids, onehot, lambda s: held[s * length : (s + 1) * length, :], scratch, own, send, sems
-    )
+    ))
 
 
 def unsort_rows(ids, order, values):
@@ -680,7 +681,7 @@
             SMEM_SPEC, token, token, token,
             pl.BlockSpec((8, width), lambda i: (0, 0)),
             pl.BlockSpec((1, hidden), lambda i: (0, 0)),
-        ] + [HBM_SPEC] * (4 + len(pieces)),
+        ] + [ANY_SPEC] * 4 + [HBM_SPEC] * len(pieces),
         out_specs=(token, wide, wide, token, token, token, token, token,
                    pl.BlockSpec((8, width), lambda i: (0, 0)),
                    pl.BlockSpec((1, hidden), lambda i: (0, 0))),
@@ -693,7 +694,7 @@
         cost_estimate=cost(36),
         compiler_params=params(("arbitrary",), FULL),
         name="feed",
-    )(ids, xs, mixed, cot, rows, up_bias, *in_hbm(*feeds, *pieces))
+    )(ids, xs, mixed, cot, rows, up_bias, *feeds, *in_hbm(*pieces))
 
 
 def feed_weights_kernel(act, gup, first, gdown, own, other):
@@ -882,6 +883,16 @@
     gx[0:length, :] += product(gk_low, joined(weights, 3 * step + 1), NT) + product(
         gv_low, joined(weights, 3 * step + 2), NT
     )
+    if done:
+        sends = put_back(
+            ids, order_onehot(ids, order),
+            lambda s: gx[s * length : (s + 1) * length, :].astype(jnp.bfloat16),
+            rows_out, own, send, row_sems,
+        )
+    else:
+        sends = [pltpu.make_async_copy(gx, gx_out, in_sems.at[0])]
+    for copy in sends:
+        copy.start()
     lanes = pl.ds(pl.multiple_of(group * LANES, LANES), LANES)
     vectors[0:1, lanes] = column_sum(gq_low.astype(jnp.float32))
     vectors[1:2, lanes] = column_sum(gv_low.astype(jnp.float32))
@@ -929,30 +940,21 @@
         for copy in stores(0):
             copy.wait()
         vectors_out[...] = vectors[0:16, :]
-        run_copies([pltpu.make_async_copy(gx, gx_out, in_sems.at[0])])
+        for copy in sends:
+            copy.wait()
         return
 
-    @pl.when(step == steps - 1)
-    def _():
-        put_back(
-            ids, order_onehot(ids, order),
-            lambda s: gx[s * length : (s + 1) * length, :].astype(jnp.bfloat16),
-            rows_out, own, send, row_sems,
-        )
-        vectors[2:8, :] = sums[0:6, :]
-        vectors[8:12, :] = up_slots(ids, up_sums, rows, parts // 2)
-        vectors[13:, :] = jnp.zeros((128 - 13, width), jnp.float32)
-        tile = jnp.transpose(vectors[...]).astype(jnp.bfloat16)
-        turned[0, 0] = tile
-        turned[1, 0] = tile
-        last = block_stores(
-            ids, turned, gw_outs, vector_sems, slice(3, LAST_TILES)
-        )
-        for copy in last:
-            copy.start()
-        waits = [copy for index in range(steps) for copy in stores(index)]
-        for copy in waits + last:
-            copy.wait()
+    vectors[2:8, :] = sums[0:6, :]
+    vectors[8:12, :] = up_slots(ids, up_sums, rows, parts // 2)
+    vectors[13:, :] = jnp.zeros((128 - 13, width), jnp.float32)
+    tile = jnp.transpose(vectors[...]).astype(jnp.bfloat16)
+    turned[0, 0] = tile
+    turned[1, 0] = tile
+    last = block_stores(ids, turned, gw_outs, vector_sems, slice(3, LAST_TILES))
+    for copy in last:
+        copy.start()
+    for copy in stores(0) + last + sends:
+        copy.wait()
 
 
 def up_slots(ids, up_sums, rows, blocks):
@@ -1157,22 +1159,22 @@
 
     square_parts = high_parts(square, count)
     came = swap(theirs)
-    slots = after(slots, came)
-    slots_high = jnp.stack([slots] + high_parts(slots, count))
     xs, cs, mask = sort_rows(
         ids, lengths, (content, query_in, content_cot, query_cot), came, order
     )
+    slots = after(slots, xs)
+    slots_high = jnp.stack([slots] + high_parts(slots, count))
     feed_early = high_part(after(feed_own, came), 2, count)
-    square_parts, xs, slots_high = lax.optimization_barrier((square_parts, xs, slots_high))
+    square_parts, xs = lax.optimization_barrier((square_parts, xs))
     square_near = low_round(jnp.stack([square] + square_parts), count)
+    square_near, slots_high, feed_early = lax.optimization_barrier(
+        (square_near, slots_high, feed_early)
+    )
     slots_near = low_round(slots_high, count)
-    square_near, slots_near, feed_early = lax.optimization_barrier(
-        (square_near, slots_near, feed_early)
-    )
     square_far = last_round(square_near, count)
+    near_swapped = swap(square_near)
+    square_far = after(square_far, slots_near, near_swapped)
     slots_far = last_round(slots_near, count)
-    near_swapped = swap(square_near)
-    square_far = after(square_far, slots_far, near_swapped)
     far_swapped = swap(square_far)
     feed_later = after(feed_own, square_near)
     feed_parts = [
@@ -1239,16 +1241,17 @@
 
     gwo = out_weights(ids, after(mixed, far_own), gbranch, pieces)
     far_came, _ = lax.optimization_barrier((swap(far_other), gwo[0]))
-    far_first, far_second = (
-        low(wide(halved(far_own)[part]) + wide(halved(far_came)[part])) for part in range(2)
-    )
-    gmixed, far_first, far_second = lax.optimization_barrier((gmixed, far_first, far_second))
+    cut = near_count // 2 + max(1, near_count // 8)
+    far_first = low(wide(far_own[:cut]) + wide(far_came[:cut]))
+    gmixed, far_first = lax.optimization_barrier((gmixed, far_first))
     far_first = last_round(far_first, count)
     heads = functools.partial(
         attend_back, ids=ids, lengths=lengths, order=order, xs=xs, mask=mask, bias=bias, q=q, k=k,
         v=v, mixed=mixed, lse=lse, up_sums=up_sums, pieces=pieces, rows_each=rows,
     )
     gx, head_sums, *gws = heads(0, 1, gmixed=gmixed, sums=sums, gres=gres, grads=gwo)
+    far_own, far_came, gx = lax.optimization_barrier((far_own, far_came, gx))
+    far_second = low(wide(far_own[cut:]) + wide(far_came[cut:]))
     gdown, far_first, far_second, gx = lax.optimization_barrier(
         (gdown, far_first, far_second, gx)
     )
@@ -1260,33 +1263,35 @@
     near_came = swap(near_other)
     outs = unsort_rows(ids, order, after(out, far_second))
     near_came, near_own, _ = lax.optimization_barrier((near_came, near_own, outs[0]))
-    far_halves = (far_first, far_second)
-    near_halves = [
-        wide(halved(near_own)[part]) + wide(halved(near_came)[part]) + wide(far_halves[part])
-        for part in range(2)
-    ]
-    gx, to_send = lax.optimization_barrier((gx, low(near_halves[1])))
+    to_send = low(
+        wide(halved(near_own)[1]) + wide(halved(near_came)[1])
+        + wide(jnp.concatenate([far_first[near_count // 2 :], far_second]))
+    )
+    gx, to_send = lax.optimization_barrier((gx, to_send))
     gfeed_came = lax.ppermute(to_send, BOTH, xor_pairs(count, (1, 2)))
     gx, head_sums, *gws = result = heads(
         1, 1, gmixed=gmixed, sums=jnp.concatenate([sums, head_sums]), gres=gx, grads=gws
     )
-    gfeed_came, gx = lax.optimization_barrier((gfeed_came, gx))
-    gfeed = near_halves[0] + wide(gfeed_came)
-    gfeed_low = [low(gfeed[high]) for high in range(1, count // 4)]
-    gx, gfeed_low = lax.optimization_barrier((gx, gfeed_low))
-    early = high_part(gfeed_low[1], 2, count)
+    near_parts = [near_own, near_came, far_first, gfeed_came]
+    near_parts, gx = lax.optimization_barrier((near_parts, gx))
+    early = low(sum(wide(part[2]) for part in near_parts))
+    gx, early = lax.optimization_barrier((gx, early))
+    early = high_part(early, 2, count)
     most = by_device(result[2:])
     most_came = [swap(part) for part in most[2:]]
     grad_own, grad_send, *gws = heads(
         2, 1, gmixed=gmixed, sums=jnp.concatenate([sums, head_sums]), gres=gx, grads=()
     )
-    early, most_came, gws = lax.optimization_barrier((early, most_came, gws))
+    early, most_came, gws, near_parts = lax.optimization_barrier(
+        (early, most_came, gws, near_parts)
+    )
+    gfeed = sum(wide(part[: near_count // 2]) for part in near_parts)
     last = by_device(gws)
     most_far = last_round(low(wide(most[1]) + wide(most_came[1])), count)
     last_came = [swap(part) for part in last[2:]]
     last_far = last_round(low(wide(last[1]) + wide(last_came[1])), count)
     gfeed_parts = [
-        early if high == 2 else high_part(gfeed_low[high - 1], high, count)
+        early if high == 2 else high_part(low(gfeed[high]), high, count)
         for high in range(1, count // 4)
     ]
     outs = place_rows(half, *outs)

time: 320 us -> 317 us (level)
  waiting for transfers between devices: 86.2 us -> 77.3 us
  local copies, waits for them, and re-layouts: 14.3 us -> 17.9 us
    ppermute x3, waiting for transfers between devices: 15.6 us -> 8.18 us  [low_round(): lax.ppermute(value, BOTH, xor_pairs(count, (1, 2)))]
    ppermute x15, starting transfers between devices: 7.01 us -> 3.15 us  [swap(): return lax.ppermute(value, 'seq', [(0, 1), (1, 0)])]
    ppermute x12, waiting for transfers between devices: 17.9 us -> 21.7 us  [high_part(): return lax.ppermute(value, BOTH, xor_pairs(count, (4 * high, 4 * high)))]
    ppermute x15, waiting for transfers between devices: 8.56 us -> 5.28 us  [swap(): return lax.ppermute(value, 'seq', [(0, 1), (1, 0)])]
    unnamed x74 -> x77, local copies, waits for them, and re-layouts: 8.27 us -> 10.9 us
    convert_element_type x4 -> x5, other arithmetic: 8.65 us -> 10.3 us  [low(): return value.astype(jnp.bfloat16)]
  transfers between devices with their start and end apart: 42 -> 42, of which waited for: 20 -> 21; matrix products, arithmetic and copies ran while one was open for 7% -> 9% of each run, Pallas kernels for 30% -> 30%
where the time goes in v4:
time: 317 us; the launch traced here: 311 us
  Pallas kernels  149 us (47%)
  waiting for transfers between devices  77.3 us (24%)
  starting transfers between devices  41.5 us (13%)
  other arithmetic  24 us (8%)
  local copies, waits for them, and re-layouts  17.9 us (6%)
    pallas_call x3, Pallas kernels, attend_back(): pl.pallas_call(functools.partial(attend_back_kernel, rows_each, base, ste...  42.8 us
    pallas_call x1, Pallas kernels, feed(): pl.pallas_call(feed_kernel, grid=(tokens // BLOCK,), out_shape=(low, SDS(...  37.6 us
    pallas_call x2, Pallas kernels, feed_weights(): pl.pallas_call(feed_weights_kernel, grid=(2, 2), out_shape=(SDS(shape, jn...  22.9 us
    ppermute x7, waiting for transfers between devices, last_round(): return lax.ppermute(value, BOTH, xor_pairs(count, (2, 1)))  21.9 us
    ppermute x12, waiting for transfers between devices, high_part(): return lax.ppermute(value, BOTH, xor_pairs(count, (4 * high, 4 * high)))  21.7 us
    pallas_call x1, Pallas kernels, attend(): pl.pallas_call(attend_kernel, grid=(GROUPS,), out_shape=(SDS((tokens, wid...  20.1 us
    ppermute x12, starting transfers between devices, high_part(): return lax.ppermute(value, BOTH, xor_pairs(count, (4 * high, 4 * high)))  19.8 us
    ppermute x3, waiting for transfers between devices, high_parts_of(): lax.ppermute(low(total[high]), BOTH, xor_pairs(count, (4 * high, 4 * high)))  11.8 us
  transfers between devices with their start and end apart: 42, of which 21 were waited for; matrix products, arithmetic and copies ran while one was open for 9% of the time, Pallas kernels for 30%

profile of v4, /device:TPU:0, one launch (start us, length us, event | category | flops | bytes accessed | tf_op | source)
XLA Modules:
  0.0 311.2 jit_solution(13090895145925956791)
XLA Ops:
  2.5 4.4 %pack.1 = (bf16[4,256,768]{2,1,0:T(8,128)(2,1)}, bf16[12,48,128]{2,1,0:T(8,128)(2,1)}, bf16[2,96,768]{2,1,0:T(8,128)(2,1)}, bf16[16,256]{1,0:T(8,128)(2,1)}) custom-call(s32[2]{0:T(128)} %pad_add_fusion.ids, bf16[2,256,768]{2,1,0:T(8,128)(2,1)} %content.3, bf16[2,256,768]{2,1,0:T(8,128)(2,1)} %query.3, bf16[2,256,768]{2,1,0:T(8,128)(2,1)} %ccot.3, ...), custom_call_target="tpu_custom_call" | custom-call | bytes 6400000 | tf_op jit(solution)/shard_map/pack/pallas_call | solution.py:116
  7.4 4.7 %collective-permute-start.2 = (bf16[12,48,128]{2,1,0:T(8,128)(2,1)}, bf16[12,48,128]{2,1,0:T(8,128)(2,1)S(1)}, u32[]{:S(2)}, u32[]{:S(2)}) collective-permute-start(bf16[12,48,128]{2,1,0:T(8,128)(2,1)} %get-tuple-element.146), channel_id=1, source_target_pairs={{0,24},{1,25},{2,26},{3,27},{4,28},{5,29},{6,30},{7,31},{8,16},{9,... | collective-permute-start | bytes 442376 | tf_op jit(solution)/shard_map/ppermute | solution.py:1100
  14.9 6.3 %sort_rows.1 = (bf16[1024,768]{1,0:T(8,128)(2,1)}, bf16[1024,768]{1,0:T(8,128)(2,1)}, bf16[2,512,512]{2,1,0:T(8,128)(2,1)}) custom-call(s32[2]{0:T(128)} %pad_add_fusion.ids, s32[2,8]{1,0:T(2,128)} %lengths.9, bf16[2,256,768]{2,1,0:T(8,128)(2,1)} %content.3, bf16[2,256,768]{2,1,0:T(8,128)(2,1)} %query.3, bf16[2,256,768]{2,1,0:T(8,128)(2,1)} %ccot.3, ...), custom_call_target="tpu_custom_call" | custom-call | bytes 8000000 | tf_op jit(solution)/shard_map/sort_rows/pallas_call | solution.py:192
  21.2 3.8 %collective-permute-start.7 = (bf16[16,256]{1,0:T(8,128)(2,1)S(1)}, bf16[16,256]{1,0:T(8,128)(2,1)S(1)}, u32[]{:S(2)}, u32[]{:S(2)}) collective-permute-start(bf16[16,256]{1,0:T(8,128)(2,1)S(1)} %copy-done.32), channel_id=1, source_target_pairs={{0,24},{1,25},{2,26},{3,27},{4,28},{5,29},{6,30},{7,31},{8,16},{9,... | collective-permute-start | bytes 24584 | tf_op jit(solution)/shard_map/ppermute | solution.py:1100
  29.8 5.9 %collective-permute-done.6 = bf16[16,256]{1,0:T(8,128)(2,1)S(1)} collective-permute-done((bf16[16,256]{1,0:T(8,128)(2,1)S(1)}, bf16[16,256]{1,0:T(8,128)(2,1)S(1)}, u32[]{:S(2)}, u32[]{:S(2)}) %collective-permute-start.6) | collective-permute-done | bytes 8224 | tf_op jit(solution)/shard_map/ppermute | solution.py:1100
  50.0 7.8 %collective-permute-done.11.rest_1_ = bf16[8,12,48,128]{3,2,1,0:T(8,128)(2,1)S(1)} collective-permute-done((bf16[8,12,48,128]{3,2,1,0:T(8,128)(2,1)S(1)}, bf16[8,12,48,128]{3,2,1,0:T(8,128)(2,1)S(1)}, u32[]{:S(2)}, u32[]{:S(2)}) %collective-permute-start.11) | collective-permute-done | bytes 1179680 | tf_op jit(solution)/shard_map/ppermute | solution.py:1112
  64.1 3.4 %collective-permute-done.10.far = bf16[8,16,256]{2,1,0:T(8,128)(2,1)} collective-permute-done((bf16[8,16,256]{2,1,0:T(8,128)(2,1)S(1)}, bf16[8,16,256]{2,1,0:T(8,128)(2,1)}, u32[]{:S(2)}, u32[]{:S(2)}) %collective-permute-start.10) | collective-permute-done | bytes 65568 | tf_op jit(solution)/shard_map/ppermute | solution.py:1112
  67.6 3.7 %vectors.1 = (f32[8,768]{1,0:T(8,128)}, f32[1,3072]{1,0:T(1,128)}, bf16[12,128,640]{2,1,0:T(8,128)(2,1)}) custom-call(s32[2]{0:T(128)} %pad_add_fusion.ids, bf16[8,16,256]{2,1,0:T(8,128)(2,1)} %copy-done.29, bf16[8,16,256]{2,1,0:T(8,128)(2,1)} %collective-permute-done.10.far), custom_call_target="tpu_custom_call" | custom-call | bytes 9600000 | tf_op jit(solution)/shard_map/vectors/pallas_call | solution.py:383
  82.2 20.1 %attend.1 = (bf16[1024,768]{1,0:T(8,128)(2,1)}, bf16[512,768]{1,0:T(8,128)(2,1)}, bf16[512,768]{1,0:T(8,128)(2,1)}, bf16[1024,768]{1,0:T(8,128)(2,1)}, f32[3,1024,128]{2,1,0:T(8,128)}) custom-call(s32[2]{0:T(128)} %pad_add_fusion.ids, s32[2,8]{1,0:T(2,128)} %lengths.9, bf16[1024,768]{1,0:T(8,128)(2,1)} %get-tuple-element.149.xs.xs_far, ...), custom_call_target="tpu_custom_call" | custom-call | bytes 28800000 | tf_op jit(solution)/shard_map/attend/pallas_call | solution.py:524
  102.3 7.6 %collective-permute-done.18.far_own = bf16[8,2,96,768]{3,2,1,0:T(8,128)(2,1)S(1)} collective-permute-done((bf16[8,2,96,768]{3,2,1,0:T(8,128)(2,1)}, bf16[8,2,96,768]{3,2,1,0:T(8,128)(2,1)S(1)}, u32[]{:S(2)}, u32[]{:S(2)}) %collective-permute-start.18) | collective-permute-done | bytes 2359328 | tf_op jit(solution)/shard_map/ppermute | solution.py:1112
  109.9 4.5 %collective-permute-done.19.far_other = bf16[8,2,96,768]{3,2,1,0:T(8,128)(2,1)S(1)} collective-permute-done((bf16[8,2,96,768]{3,2,1,0:T(8,128)(2,1)S(1)}, bf16[8,2,96,768]{3,2,1,0:T(8,128)(2,1)S(1)}, u32[]{:S(2)}, u32[]{:S(2)}) %collective-permute-start.19) | collective-permute-done | bytes 2359328 | tf_op jit(solution)/shard_map/ppermute | solution.py:1096
  115.9 37.6 %feed.1 = (bf16[1024,768]{1,0:T(8,128)(2,1)}, bf16[1024,3072]{1,0:T(8,128)(2,1)}, bf16[1024,3072]{1,0:T(8,128)(2,1)}, bf16[1024,768]{1,0:T(8,128)(2,1)}, bf16[10...) custom-call(s32[2]{0:T(128)} %pad_add_fusion.ids, ...), custom_call_target="tpu_custom_call" | custom-call | bytes 57600000 | tf_op jit(solution)/shard_map/feed/pallas_call | solution.py:665
  153.5 11.6 %feed_weights.2 = (bf16[8,2,96,768]{3,2,1,0:T(8,128)(2,1)}, bf16[8,2,96,768]{3,2,1,0:T(8,128)(2,1)}) custom-call(bf16[1024,3072]{1,0:T(8,128)(2,1)} %get-tuple-element.176.act, bf16[1024,3072]{1,0:T(8,128)(2,1)} %get-tuple-element.177.gup, bf16[1024,768]{1,0:T(8,128)(2,1)} %get-tuple-element.178.first, bf16[1024,768]{1,0:T(8,128)(2,1)} %get-tuple-element.202.gdown), custom_call_target="tpu_custom_call" | custom-call | bytes 14400000 | tf_op jit(solution)/shard_map/feed_weights/pallas_call | solution.py:724
  165.1 4.9 %out_weights.1 = (bf16[8,9,48,128]{3,2,1,0:T(8,128)(2,1)}, bf16[8,9,48,128]{3,2,1,0:T(8,128)(2,1)}, bf16[8,9,48,128]{3,2,1,0:T(8,128)(2,1)}, bf16[8,9,48,128]{3,2,1,0:T(8,128)(2,1)}) custom-call(s32[2]{0:T(128)} %pad_add_fusion.ids, bf16[1024,768]{1,0:T(8,128)(2,1)} %get-tuple-element.181.mixed, bf16[1024,768]{1,0:T(8,128)(2,1)} %get-tuple-element.182.gbranch), custom_call_target="tpu_custom_call" | custom-call | bytes 6400000 | tf_op jit(solution)/shard_map/out_weights/pallas_call | solution.py:753
  174.2 13.5 %attend_back.3 = (f32[1024,768]{1,0:T(8,128)}, f32[16,768]{1,0:T(8,128)}, bf16[8,9,48,128]{3,2,1,0:T(8,128)(2,1)}, bf16[8,9,48,128]{3,2,1,0:T(8,128)(2,1)}, bf16...) custom-call(s32[2]{0:T(128)} %pad_add_fusion.ids, ...), custom_call_target="tpu_custom_call", output_to_operand_aliasing={{2}: (19, {}), {3}: (20, {}), {4}: (21, {}), {5}: (22, {})} | custom-call | bytes 22400000 | tf_op jit(solution)/shard_map/attend_back/pallas_call | solution.py:994
  193.8 11.4 %feed_weights.3 = (bf16[8,2,96,768]{3,2,1,0:T(8,128)(2,1)}, bf16[8,2,96,768]{3,2,1,0:T(8,128)(2,1)}) custom-call(bf16[1024,3072]{1,0:T(8,128)(2,1)} %get-tuple-element.176.act, bf16[1024,3072]{1,0:T(8,128)(2,1)} %get-tuple-element.177.gup, bf16[1024,768]{1,0:T(8,128)(2,1)} %get-tuple-element.178.first, bf16[1024,768]{1,0:T(8,128)(2,1)} %get-tuple-element.202.gdown), custom_call_target="tpu_custom_call" | custom-call | bytes 14400000 | tf_op jit(solution)/shard_map/feed_weights/pallas_call | solution.py:724
  206.6 4.4 %unsort_rows.1 = (bf16[2,256,768]{2,1,0:T(8,128)(2,1)}, bf16[2,256,768]{2,1,0:T(8,128)(2,1)}) custom-call(s32[2]{0:T(128)} %pad_add_fusion.ids, s32[2,512]{1,0:T(2,128)} %order.9, bf16[1024,768]{1,0:T(8,128)(2,1)} %get-tuple-element.206.values), custom_call_target="tpu_custom_call" | custom-call | bytes 4800000 | tf_op jit(solution)/shard_map/unsort_rows/pallas_call | solution.py:239
  211.4 3.6 %add_convert_fusion.1 = bf16[4,2,96,768]{3,2,1,0:T(8,128)(2,1)} fusion(bf16[3,2,96,768]{3,2,1,0:T(8,128)(2,1)S(1)} %copy-done.20, bf16[1,2,96,768]{3,2,1,0:T(8,128)(2,1)S(1)} %slice-done, bf16[8,2,96,768]{3,2,1,0:T(8,128)(2,1)S(1)} %collective-permute-done.24, bf16[8,2,96,768]{3,2,1,0:T(8,128)(2,1)} %get-tuple-element.246), kind=kLoop, calls=%fused_computation.4 | loop fusion | flops 4128768 | bytes 4718592 | tf_op jit(solution)/shard_map/convert_element_type | solution.py:1131
  216.3 13.5 %attend_back.4 = (f32[1024,768]{1,0:T(8,128)}, f32[16,768]{1,0:T(8,128)}, bf16[8,9,48,128]{3,2,1,0:T(8,128)(2,1)}, bf16[8,9,48,128]{3,2,1,0:T(8,128)(2,1)}, bf16...) custom-call(s32[2]{0:T(128)} %pad_add_fusion.ids, ...), custom_call_target="tpu_custom_call", output_to_operand_aliasing={{2}: (19, {}), {3}: (20, {}), {4}: (21, {}), {5}: (22, {})} | custom-call | bytes 22400000 | tf_op jit(solution)/shard_map/attend_back/pallas_call | solution.py:994
  237.0 15.9 %attend_back.5 = (bf16[2,256,768]{2,1,0:T(8,128)(2,1)}, bf16[2,256,768]{2,1,0:T(8,128)(2,1)}, bf16[8,4,48,128]{3,2,1,0:T(8,128)(2,1)}, bf16[8,4,48,128]{3,2,1,0:...) custom-call(s32[2]{0:T(128)} %pad_add_fusion.ids, s32[2,8]{1,0:T(2,128)} %lengths.9, ...), custom_call_target="tpu_custom_call" | custom-call | bytes 22400000 | tf_op jit(solution)/shard_map/attend_back/pallas_call | solution.py:994
  266.9 5.5 %collective-permute-done.35 = bf16[2,96,768]{2,1,0:T(8,128)(2,1)S(1)} collective-permute-done((bf16[2,96,768]{2,1,0:T(8,128)(2,1)S(1)}, bf16[2,96,768]{2,1,0:T(8,128)(2,1)S(1)}, u32[]{:S(2)}, u32[]{:S(2)}) %collective-permute-start.35) | collective-permute-done | bytes 294944 | tf_op jit(solution)/shard_map/ppermute | solution.py:1100
  272.4 4.9 %collective-permute-done.34 = bf16[2,96,768]{2,1,0:T(8,128)(2,1)S(1)} collective-permute-done((bf16[2,96,768]{2,1,0:T(8,128)(2,1)S(1)}, bf16[2,96,768]{2,1,0:T(8,128)(2,1)S(1)}, u32[]{:S(2)}, u32[]{:S(2)}) %collective-permute-start.34) | collective-permute-done | bytes 294944 | tf_op jit(solution)/shard_map/ppermute | solution.py:1100
  281.4 8.1 %collective-permute-done.36 = bf16[4,13,48,128]{3,2,1,0:T(8,128)(2,1)S(1)} collective-permute-done((bf16[4,13,48,128]{3,2,1,0:T(8,128)(2,1)S(1)}, bf16[4,13,48,128]{3,2,1,0:T(8,128)(2,1)S(1)}, u32[]{:S(2)}, u32[]{:S(2)}) %collective-permute-start.36) | collective-permute-done | bytes 639008 | tf_op jit(solution)/shard_map/ppermute | solution.py:1306
  300.4 6.0 %collective-permute-done.38 = bf16[13,48,128]{2,1,0:T(8,128)(2,1)S(1)} collective-permute-done((bf16[13,48,128]{2,1,0:T(8,128)(2,1)S(1)}, bf16[13,48,128]{2,1,0:T(8,128)(2,1)S(1)}, u32[]{:S(2)}, u32[]{:S(2)}) %collective-permute-start.38) | collective-permute-done | bytes 159776 | tf_op jit(solution)/shard_map/ppermute | solution.py:1232
  (185 shorter events, 96.9 us)
Async XLA Ops:
  7.4 17.6 %collective-permute-start.2 = (bf16[12,48,128]{2,1,0:T(8,128)(2,1)}, bf16[12,48,128]{2,1,0:T(8,128)(2,1)S(1)}, u32[]{:S(2)}, u32[]{:S(2)}) collective-permute-start(bf16[12,48,128]{2,1,0:T(8,128)(2,1)} %get-tuple-element.146), channel_id=1, source_target_pairs={{0,24},{1,25},{2,26},{3,27},{4,28},{5,29},{6,30},{7,31},{8,16},{9,... | collective-permute-start | bytes 442376 | tf_op jit(solution)/shard_map/ppermute | solution.py:1100
  12.1 13.6 %collective-permute-start.1 = (bf16[12,48,128]{2,1,0:T(8,128)(2,1)}, bf16[12,48,128]{2,1,0:T(8,128)(2,1)S(1)}, u32[]{:S(2)}, u32[]{:S(2)}) collective-permute-start(bf16[12,48,128]{2,1,0:T(8,128)(2,1)} %get-tuple-element.146), channel_id=1, source_target_pairs={{0,16},{1,17},{2,18},{3,19},{4,20},{5,21},{6,22},{7,23},{8,24},{9,... | collective-permute-start | bytes 442376 | tf_op jit(solution)/shard_map/ppermute | solution.py:1100
  12.1 15.9 %collective-permute-start = (bf16[12,48,128]{2,1,0:T(8,128)(2,1)}, bf16[12,48,128]{2,1,0:T(8,128)(2,1)S(1)}, u32[]{:S(2)}, u32[]{:S(2)}) collective-permute-start(bf16[12,48,128]{2,1,0:T(8,128)(2,1)} %get-tuple-element.146), channel_id=1, source_target_pairs={{0,8},{1,9},{2,10},{3,11},{4,12},{5,13},{6,14},{7,15},{8,0},{9,1},... | collective-permute-start | bytes 442376 | tf_op jit(solution)/shard_map/ppermute | solution.py:1100
  25.7 15.6 %collective-permute-start.8 = (bf16[2,96,768]{2,1,0:T(8,128)(2,1)S(1)}, bf16[2,96,768]{2,1,0:T(8,128)(2,1)S(1)}, u32[]{:S(2)}, u32[]{:S(2)}) collective-permute-start(bf16[2,96,768]{2,1,0:T(8,128)(2,1)S(1)} %copy-done.16), channel_id=1, source_target_pairs={{0,16},{1,17},{2,18},{3,19},{4,20},{5,21},{6,22},{7,23},{8,24},{9,... | collective-permute-start | bytes 884744 | tf_op jit(solution)/shard_map/ppermute | solution.py:1100
  41.3 16.6 %collective-permute-start.11 = (bf16[8,12,48,128]{3,2,1,0:T(8,128)(2,1)S(1)}, bf16[8,12,48,128]{3,2,1,0:T(8,128)(2,1)S(1)}, u32[]{:S(2)}, u32[]{:S(2)}) collective-permute-start(bf16[8,12,48,128]{3,2,1,0:T(8,128)(2,1)S(1)} %constant_dynamic-update-slice_fusion.rest_0_), channel_id=1, source_target_pairs={{0,4},{1,3},{2,6},{3,1},{4,0},{5,7},{6,2},{7,5},{8,12},{9,11},{10,... | collective-permute-start | bytes 3538952 | tf_op jit(solution)/shard_map/ppermute | solution.py:1112
  42.8 15.0 %collective-permute-start.15 = (bf16[2,96,768]{2,1,0:T(8,128)(2,1)S(1)}, bf16[2,96,768]{2,1,0:T(8,128)(2,1)S(1)}, u32[]{:S(2)}, u32[]{:S(2)}) collective-permute-start(bf16[2,96,768]{2,1,0:T(8,128)(2,1)S(1)} %copy-done.16), channel_id=1, source_target_pairs={{0,24},{1,25},{2,26},{3,27},{4,28},{5,29},{6,30},{7,31},{8,16},{9,... | collective-permute-start | bytes 884744 | tf_op jit(solution)/shard_map/ppermute | solution.py:1100
  45.6 14.5 %collective-permute-start.14 = (bf16[2,96,768]{2,1,0:T(8,128)(2,1)S(1)}, bf16[2,96,768]{2,1,0:T(8,128)(2,1)S(1)}, u32[]{:S(2)}, u32[]{:S(2)}) collective-permute-start(bf16[2,96,768]{2,1,0:T(8,128)(2,1)S(1)} %copy-done.16), channel_id=1, source_target_pairs={{0,8},{1,9},{2,10},{3,11},{4,12},{5,13},{6,14},{7,15},{8,0},{9,1},... | collective-permute-start | bytes 884744 | tf_op jit(solution)/shard_map/ppermute | solution.py:1100
  61.3 17.2 %collective-permute-start.16 = (bf16[4,2,96,768]{3,2,1,0:T(8,128)(2,1)}, bf16[4,2,96,768]{3,2,1,0:T(8,128)(2,1)}, u32[]{:S(2)}, u32[]{:S(2)}) collective-permute-start(bf16[4,2,96,768]{3,2,1,0:T(8,128)(2,1)} %pad_maximum_fusion.1), channel_id=1, source_target_pairs={{0,2},{1,5},{2,0},{3,7},{4,6},{5,1},{6,4},{7,3},{8,10},{9,13},{10,... | collective-permute-start | bytes 3538952 | tf_op jit(solution)/shard_map/ppermute | solution.py:1108
  61.9 19.0 %collective-permute-start.13 = (bf16[8,12,48,128]{3,2,1,0:T(8,128)(2,1)S(1)}, bf16[8,12,48,128]{3,2,1,0:T(8,128)(2,1)}, u32[]{:S(2)}, u32[]{:S(2)}) collective-permute-start(bf16[8,12,48,128]{3,2,1,0:T(8,128)(2,1)S(1)} %collective-permute-done.11.rest_1_), channel_id=1, source_target_pairs={{0,1},{1,0},{2,3},{3,2},{4,5},{5,4},{6,7},{7,6},{8,9},{9,8},{10,11... | collective-permute-start | bytes 3538952 | tf_op jit(solution)/shard_map/ppermute | solution.py:1096
  80.8 29.1 %collective-permute-start.18 = (bf16[8,2,96,768]{3,2,1,0:T(8,128)(2,1)}, bf16[8,2,96,768]{3,2,1,0:T(8,128)(2,1)S(1)}, u32[]{:S(2)}, u32[]{:S(2)}) collective-permute-start(bf16[8,2,96,768]{3,2,1,0:T(8,128)(2,1)} %constant_dynamic-update-slice_fusion.7.near_own), channel_id=1, source_target_pairs={{0,4},{1,3},{2,6},{3,1},{4,0},{5,7},{6,2},{7,5},{8,12},{9,11},{10,... | collective-permute-start | bytes 7077896 | tf_op jit(solution)/shard_map/ppermute | solution.py:1112
  82.2 27.7 %collective-permute-start.17 = (bf16[8,2,96,768]{3,2,1,0:T(8,128)(2,1)}, bf16[8,2,96,768]{3,2,1,0:T(8,128)(2,1)}, u32[]{:S(2)}, u32[]{:S(2)}) collective-permute-start(bf16[8,2,96,768]{3,2,1,0:T(8,128)(2,1)} %constant_dynamic-update-slice_fusion.7.near_own), channel_id=1, source_target_pairs={{0,1},{1,0},{2,3},{3,2},{4,5},{5,4},{6,7},{7,6},{8,9},{9,8},{10,11... | collective-permute-start | bytes 7077896 | tf_op jit(solution)/shard_map/ppermute | solution.py:1096
  172.9 19.6 %collective-permute-start.21 = (bf16[5,2,96,768]{3,2,1,0:T(8,128)(2,1)}, bf16[5,2,96,768]{3,2,1,0:T(8,128)(2,1)S(1)}, u32[]{:S(2)}, u32[]{:S(2)}) collective-permute-start(bf16[5,2,96,768]{3,2,1,0:T(8,128)(2,1)} %add_convert_fusion), channel_id=1, source_target_pairs={{0,4},{1,3},{2,6},{3,1},{4,0},{5,7},{6,2},{7,5},{8,12},{9,11},{10,... | collective-permute-start | bytes 4423688 | tf_op jit(solution)/shard_map/ppermute | solution.py:1112
  192.5 13.3 %collective-permute-start.22 = (bf16[3,2,96,768]{3,2,1,0:T(8,128)(2,1)}, bf16[3,2,96,768]{3,2,1,0:T(8,128)(2,1)S(1)}, u32[]{:S(2)}, u32[]{:S(2)}) collective-permute-start(bf16[3,2,96,768]{3,2,1,0:T(8,128)(2,1)} %add_convert_fusion.3), channel_id=1, source_target_pairs={{0,4},{1,3},{2,6},{3,1},{4,0},{5,7},{6,2},{7,5},{8,12},{9,11},{10,... | collective-permute-start | bytes 2654216 | tf_op jit(solution)/shard_map/ppermute | solution.py:1112
  215.0 16.4 %collective-permute-start.25 = (bf16[4,2,96,768]{3,2,1,0:T(8,128)(2,1)}, bf16[4,2,96,768]{3,2,1,0:T(8,128)(2,1)S(1)}, u32[]{:S(2)}, u32[]{:S(2)}) collective-permute-start(bf16[4,2,96,768]{3,2,1,0:T(8,128)(2,1)} %add_convert_fusion.1), channel_id=1, source_target_pairs={{0,2},{1,5},{2,0},{3,7},{4,6},{5,1},{6,4},{7,3},{8,10},{9,13},{10,... | collective-permute-start | bytes 3538952 | tf_op jit(solution)/shard_map/ppermute | solution.py:1271
  229.7 23.2 %collective-permute-start.28 = (bf16[8,9,48,128]{3,2,1,0:T(8,128)(2,1)}, bf16[8,9,48,128]{3,2,1,0:T(8,128)(2,1)}, u32[]{:S(2)}, u32[]{:S(2)}) collective-permute-start(bf16[8,9,48,128]{3,2,1,0:T(8,128)(2,1)} %get-tuple-element.234), channel_id=1, source_target_pairs={{0,1},{1,0},{2,3},{3,2},{4,5},{5,4},{6,7},{7,6},{8,9},{9,8},{10,11... | collective-permute-start | bytes 2654216 | tf_op jit(solution)/shard_map/ppermute | solution.py:1096
  230.4 22.5 %collective-permute-start.29 = (bf16[8,9,48,128]{3,2,1,0:T(8,128)(2,1)}, bf16[8,9,48,128]{3,2,1,0:T(8,128)(2,1)}, u32[]{:S(2)}, u32[]{:S(2)}) collective-permute-start(bf16[8,9,48,128]{3,2,1,0:T(8,128)(2,1)} %get-tuple-element.235), channel_id=1, source_target_pairs={{0,1},{1,0},{2,3},{3,2},{4,5},{5,4},{6,7},{7,6},{8,9},{9,8},{10,11... | collective-permute-start | bytes 2654216 | tf_op jit(solution)/shard_map/ppermute | solution.py:1096
  230.5 33.1 %collective-permute-start.23 = (bf16[2,256,768]{2,1,0:T(8,128)(2,1)}, bf16[2,256,768]{2,1,0:T(8,128)(2,1)}, u32[]{:S(2)}, u32[]{:S(2)}) collective-permute-start(bf16[2,256,768]{2,1,0:T(8,128)(2,1)} %get-tuple-element.208), channel_id=1, source_target_pairs={{0,1},{1,0},{2,3},{3,2},{4,5},{5,4},{6,7},{7,6},{8,9},{9,8},{10,11... | collective-permute-start | bytes 2359304 | tf_op jit(solution)/shard_map/ppermute | solution.py:1096
  233.7 19.2 %collective-permute-start.27 = (bf16[2,96,768]{2,1,0:T(8,128)(2,1)}, bf16[2,96,768]{2,1,0:T(8,128)(2,1)}, u32[]{:S(2)}, u32[]{:S(2)}) collective-permute-start(bf16[2,96,768]{2,1,0:T(8,128)(2,1)} %fusion.9), channel_id=1, source_target_pairs={{0,16},{1,17},{2,18},{3,19},{4,20},{5,21},{6,22},{7,23},{8,24},{9,... | collective-permute-start | bytes 884744 | tf_op jit(solution)/shard_map/ppermute | solution.py:1100
  253.0 24.2 %collective-permute-start.33 = (bf16[8,4,48,128]{3,2,1,0:T(8,128)(2,1)}, bf16[8,4,48,128]{3,2,1,0:T(8,128)(2,1)S(1)}, u32[]{:S(2)}, u32[]{:S(2)}) collective-permute-start(bf16[8,4,48,128]{3,2,1,0:T(8,128)(2,1)} %get-tuple-element.245), channel_id=1, source_target_pairs={{0,1},{1,0},{2,3},{3,2},{4,5},{5,4},{6,7},{7,6},{8,9},{9,8},{10,11... | collective-permute-start | bytes 1179656 | tf_op jit(solution)/shard_map/ppermute | solution.py:1096
  255.0 22.2 %collective-permute-start.30 = (bf16[8,9,48,128]{3,2,1,0:T(8,128)(2,1)S(1)}, bf16[8,9,48,128]{3,2,1,0:T(8,128)(2,1)S(1)}, u32[]{:S(2)}, u32[]{:S(2)}) collective-permute-start(bf16[8,9,48,128]{3,2,1,0:T(8,128)(2,1)S(1)} %add_convert_fusion.2), channel_id=1, source_target_pairs={{0,4},{1,3},{2,6},{3,1},{4,0},{5,7},{6,2},{7,5},{8,12},{9,11},{10,... | collective-permute-start | bytes 2654216 | tf_op jit(solution)/shard_map/ppermute | solution.py:1112
  263.3 13.9 %collective-permute-start.34 = (bf16[2,96,768]{2,1,0:T(8,128)(2,1)S(1)}, bf16[2,96,768]{2,1,0:T(8,128)(2,1)S(1)}, u32[]{:S(2)}, u32[]{:S(2)}) collective-permute-start(bf16[2,96,768]{2,1,0:T(8,128)(2,1)S(1)} %get-tuple-element.279), channel_id=1, source_target_pairs={{0,8},{1,9},{2,10},{3,11},{4,12},{5,13},{6,14},{7,15},{8,0},{9,1},... | collective-permute-start | bytes 884744 | tf_op jit(solution)/shard_map/ppermute | solution.py:1100
  263.6 13.6 %collective-permute-start.32 = (bf16[8,4,48,128]{3,2,1,0:T(8,128)(2,1)S(1)}, bf16[8,4,48,128]{3,2,1,0:T(8,128)(2,1)S(1)}, u32[]{:S(2)}, u32[]{:S(2)}) collective-permute-start(bf16[8,4,48,128]{3,2,1,0:T(8,128)(2,1)S(1)} %add_convert_fusion.4), channel_id=1, source_target_pairs={{0,4},{1,3},{2,6},{3,1},{4,0},{5,7},{6,2},{7,5},{8,12},{9,11},{10,... | collective-permute-start | bytes 1179656 | tf_op jit(solution)/shard_map/ppermute | solution.py:1112
  281.3 25.3 %collective-permute-start.41 = (f32[2,96,768]{2,1,0:T(8,128)S(1)}, f32[2,96,768]{2,1,0:T(8,128)S(1)}, u32[]{:S(2)}, u32[]{:S(2)}) collective-permute-start(f32[2,96,768]{2,1,0:T(8,128)S(1)} %fusion.5), channel_id=1, source_target_pairs={{0,1},{1,0},{2,3},{3,2},{4,5},{5,4},{6,7},{7,6},{8,9},{9,8},{10,11... | collective-permute-start | bytes 1769480 | tf_op jit(solution)/shard_map/ppermute | solution.py:1096
  291.9 14.5 %collective-permute-start.38 = (bf16[13,48,128]{2,1,0:T(8,128)(2,1)S(1)}, bf16[13,48,128]{2,1,0:T(8,128)(2,1)S(1)}, u32[]{:S(2)}, u32[]{:S(2)}) collective-permute-start(bf16[13,48,128]{2,1,0:T(8,128)(2,1)S(1)} %get-tuple-element.290), channel_id=1, source_target_pairs={{0,16},{1,17},{2,18},{3,19},{4,20},{5,21},{6,22},{7,23},{8,24},{9,... | collective-permute-start | bytes 479240 | tf_op jit(solution)/shard_map/ppermute | solution.py:1232
  (53 other events, 423.3 us)

commit v5 on v4

--- a/solution.py
+++ b/solution.py
@@ -697,43 +697,62 @@
     )(ids, xs, mixed, cot, rows, up_bias, *feeds, *in_hbm(*pieces))
 
 
-def feed_weights_kernel(act, gup, first, gdown, own, other):
-    which = pl.program_id(1)
-
-    def put(grad):
-        share = own.shape[2]
-        grad = grad.astype(jnp.bfloat16)
-
-        def store(out):
-            for block in range(out.shape[0]):
-                out[block, 0] = grad[block * share : (block + 1) * share, :]
-
-        pl.when(pl.program_id(0) == 0)(lambda: store(other))
-        pl.when(pl.program_id(0) == 1)(lambda: store(own))
-
-    pl.when(which == 0)(lambda: put(product(gup[...], first[...], TN)))
-    pl.when(which == 1)(lambda: put(product(act[...], gdown[...], TN)))
+def feed_weights_kernel(part, act, gup, first, gdown, own, other, left, right, grads, in_sems,
+                        out_sems):
+    tokens, units = left.shape[1:]
+    share = own.shape[2]
+    loads, uses = [], []
+
+    def load(source, target):
+        copy = pltpu.make_async_copy(source, target, in_sems.at[len(loads)])
+        copy.start()
+        loads.append(copy)
+
+    for side in range(2):
+        lanes = slice((2 * part + 1 - side) * units, (2 * part + 2 - side) * units)
+        for which, (source, other_side) in enumerate(((gup, first), (act, gdown))):
+            load(source.at[:, lanes], left.at[2 * side + which])
+            if side == 0:
+                load(other_side, right.at[which])
+            uses.append(len(loads))
+    stores = []
+    done = 0
+    for index in range(4):
+        for copy in loads[done : uses[index]]:
+            copy.wait()
+        done = uses[index]
+        which = index % 2
+        grad = product(left[index], right[which], TN).astype(jnp.bfloat16)
+        for block in range(own.shape[0]):
+            grads[index, block] = grad[block * share : (block + 1) * share, :]
+        out = other if index < 2 else own
+        stores.append(
+            pltpu.make_async_copy(grads.at[index], out.at[:, which], out_sems.at[index])
+        )
+        stores[-1].start()
+    for copy in stores:
+        copy.wait()
 
 
 def feed_weights(part, act, gup, first, gdown, shape):
     tokens, width = first.shape
     units = shape[0] * shape[2]
-    full = pl.BlockSpec((tokens, width), lambda s, u: (0, 0), pipeline_mode=pl.Buffered(1))
-    lanes = pl.BlockSpec((tokens, units), lambda s, u: (0, 2 * part + 1 - s))
-    block = (shape[0], 1) + shape[2:]
     return pl.pallas_call(
-        feed_weights_kernel,
-        grid=(2, 2),
+        functools.partial(feed_weights_kernel, part),
         out_shape=(SDS(shape, jnp.bfloat16),) * 2,
-        in_specs=[lanes, lanes, full, full],
-        out_specs=(
-            pl.BlockSpec(block, lambda s, u: (0, s * u, 0, 0)),
-            pl.BlockSpec(block, lambda s, u: (0, jnp.maximum(s, u), 0, 0)),
-        ),
+        in_specs=[HBM_SPEC] * 4,
+        out_specs=(HBM_SPEC,) * 2,
+        scratch_shapes=[
+            pltpu.VMEM((4, tokens, units), jnp.bfloat16),
+            pltpu.VMEM((2, tokens, width), jnp.bfloat16),
+            pltpu.VMEM((4, shape[0], shape[2], width), jnp.bfloat16),
+            pltpu.SemaphoreType.DMA((6,)),
+            pltpu.SemaphoreType.DMA((4,)),
+        ],
         cost_estimate=cost(9),
-        compiler_params=params(("arbitrary", "arbitrary"), FULL),
+        compiler_params=params(None, FULL),
         name="feed_weights",
-    )(act, gup, first, gdown)
+    )(*in_hbm(act, gup, first, gdown))
 
 
 def out_weights_kernel(ids, mixed, gbranch, *rest):
@@ -1274,9 +1293,11 @@
     )
     near_parts = [near_own, near_came, far_first, gfeed_came]
     near_parts, gx = lax.optimization_barrier((near_parts, gx))
-    early = low(sum(wide(part[2]) for part in near_parts))
-    gx, early = lax.optimization_barrier((gx, early))
-    early = high_part(early, 2, count)
+    gfeed_low = [
+        low(sum(wide(part[high]) for part in near_parts)) for high in range(1, count // 4)
+    ]
+    gx, gfeed_low = lax.optimization_barrier((gx, gfeed_low))
+    early = high_part(gfeed_low[1], 2, count)
     most = by_device(result[2:])
     most_came = [swap(part) for part in most[2:]]
     grad_own, grad_send, *gws = heads(
@@ -1285,13 +1306,12 @@
     early, most_came, gws, near_parts = lax.optimization_barrier(
         (early, most_came, gws, near_parts)
     )
-    gfeed = sum(wide(part[: near_count // 2]) for part in near_parts)
     last = by_device(gws)
     most_far = last_round(low(wide(most[1]) + wide(most_came[1])), count)
     last_came = [swap(part) for part in last[2:]]
     last_far = last_round(low(wide(last[1]) + wide(last_came[1])), count)
     gfeed_parts = [
-        early if high == 2 else high_part(low(gfeed[high]), high, count)
+        early if high == 2 else high_part(gfeed_low[high - 1], high, count)
         for high in range(1, count // 4)
     ]
     outs = place_rows(half, *outs)
@@ -1306,7 +1326,7 @@
     gw_came = lax.ppermute(low(halved(gw)[1]), BOTH, xor_pairs(count, (1, 2)))
     gw = halved(gw)[0] + wide(gw_came)
     gw_parts = high_parts_of(gw, count)
-    gfeed = own_sum(gfeed, gfeed_parts)
+    gfeed = sum(wide(part[0]) for part in near_parts) + sum(wide(part) for part in gfeed_parts)
     gfeed = in_order(half, gfeed, swap(gfeed))
     up_grad = jnp.transpose(gfeed[:, 0].reshape(hidden, width))
     down_grad = gfeed[:, 1].reshape(hidden, width)

time: 317 us -> 312 us (0.984)
  Pallas kernels: 149 us -> 155 us
  waiting for transfers between devices: 77.3 us -> 71.6 us
    pallas_call x3, Pallas kernels: 42.8 us -> 48.5 us  [attend_back(): pl.pallas_call(functools.partial(attend_back_kernel, rows_each, base, ste...]
    unnamed x77 -> x71, local copies, waits for them, and re-layouts: 10.9 us -> 10.8 us
  transfers between devices with their start and end apart: 42 -> 42, of which waited for: 21 -> 19; matrix products, arithmetic and copies ran while one was open for 9% -> 9% of each run, Pallas kernels for 30% -> 33%
where the time goes in v5:
time: 312 us; the launch traced here: 306 us
  Pallas kernels  155 us (50%)
  waiting for transfers between devices  71.6 us (23%)
  starting transfers between devices  39 us (12%)
  other arithmetic  21 us (7%)
  local copies, waits for them, and re-layouts  18 us (6%)
    pallas_call x3, Pallas kernels, attend_back(): pl.pallas_call(functools.partial(attend_back_kernel, rows_each, base, ste...  48.5 us
    pallas_call x1, Pallas kernels, feed(): pl.pallas_call(feed_kernel, grid=(tokens // BLOCK,), out_shape=(low, SDS(...  37.9 us
    pallas_call x1, Pallas kernels, attend(): pl.pallas_call(attend_kernel, grid=(GROUPS,), out_shape=(SDS((tokens, wid...  22.4 us
    ppermute x12, waiting for transfers between devices, high_part(): return lax.ppermute(value, BOTH, xor_pairs(count, (4 * high, 4 * high)))  21 us
    pallas_call x2, Pallas kernels, feed_weights(): pl.pallas_call(functools.partial(feed_weights_kernel, part), out_shape=(S...  20.5 us
    ppermute x7, waiting for transfers between devices, last_round(): return lax.ppermute(value, BOTH, xor_pairs(count, (2, 1)))  18.7 us
    ppermute x12, starting transfers between devices, high_part(): return lax.ppermute(value, BOTH, xor_pairs(count, (4 * high, 4 * high)))  18.5 us
    ppermute x3, waiting for transfers between devices, high_parts_of(): lax.ppermute(low(total[high]), BOTH, xor_pairs(count, (4 * high, 4 * high)))  11 us
  transfers between devices with their start and end apart: 42, of which 19 were waited for; matrix products, arithmetic and copies ran while one was open for 9% of the time, Pallas kernels for 33%

profile of v5, /device:TPU:0, one launch (start us, length us, event | category | flops | bytes accessed | tf_op | source)
XLA Modules:
  0.0 306.1 jit_solution(11075772669691167436)
XLA Ops:
  2.5 4.4 %pack.1 = (bf16[4,256,768]{2,1,0:T(8,128)(2,1)}, bf16[12,48,128]{2,1,0:T(8,128)(2,1)}, bf16[2,96,768]{2,1,0:T(8,128)(2,1)}, bf16[16,256]{1,0:T(8,128)(2,1)}) custom-call(s32[2]{0:T(128)} %pad_add_fusion.ids, bf16[2,256,768]{2,1,0:T(8,128)(2,1)} %content.3, bf16[2,256,768]{2,1,0:T(8,128)(2,1)} %query.3, bf16[2,256,768]{2,1,0:T(8,128)(2,1)} %ccot.3, ...), custom_call_target="tpu_custom_call" | custom-call | bytes 6400000 | tf_op jit(solution)/shard_map/pack/pallas_call | solution.py:116
  7.5 4.7 %collective-permute-start.2 = (bf16[12,48,128]{2,1,0:T(8,128)(2,1)}, bf16[12,48,128]{2,1,0:T(8,128)(2,1)S(1)}, u32[]{:S(2)}, u32[]{:S(2)}) collective-permute-start(bf16[12,48,128]{2,1,0:T(8,128)(2,1)} %get-tuple-element.148), channel_id=1, source_target_pairs={{0,24},{1,25},{2,26},{3,27},{4,28},{5,29},{6,30},{7,31},{8,16},{9,... | collective-permute-start | bytes 442376 | tf_op jit(solution)/shard_map/ppermute | solution.py:1119
  15.0 6.3 %sort_rows.1 = (bf16[1024,768]{1,0:T(8,128)(2,1)}, bf16[1024,768]{1,0:T(8,128)(2,1)}, bf16[2,512,512]{2,1,0:T(8,128)(2,1)}) custom-call(s32[2]{0:T(128)} %pad_add_fusion.ids, s32[2,8]{1,0:T(2,128)} %lengths.9, bf16[2,256,768]{2,1,0:T(8,128)(2,1)} %content.3, bf16[2,256,768]{2,1,0:T(8,128)(2,1)} %query.3, bf16[2,256,768]{2,1,0:T(8,128)(2,1)} %ccot.3, ...), custom_call_target="tpu_custom_call" | custom-call | bytes 8000000 | tf_op jit(solution)/shard_map/sort_rows/pallas_call | solution.py:192
  21.3 3.8 %collective-permute-start.7 = (bf16[16,256]{1,0:T(8,128)(2,1)S(1)}, bf16[16,256]{1,0:T(8,128)(2,1)S(1)}, u32[]{:S(2)}, u32[]{:S(2)}) collective-permute-start(bf16[16,256]{1,0:T(8,128)(2,1)S(1)} %copy-done.28), channel_id=1, source_target_pairs={{0,24},{1,25},{2,26},{3,27},{4,28},{5,29},{6,30},{7,31},{8,16},{9,... | collective-permute-start | bytes 24584 | tf_op jit(solution)/shard_map/ppermute | solution.py:1119
  29.9 5.9 %collective-permute-done.6 = bf16[16,256]{1,0:T(8,128)(2,1)S(1)} collective-permute-done((bf16[16,256]{1,0:T(8,128)(2,1)S(1)}, bf16[16,256]{1,0:T(8,128)(2,1)S(1)}, u32[]{:S(2)}, u32[]{:S(2)}) %collective-permute-start.6) | collective-permute-done | bytes 8224 | tf_op jit(solution)/shard_map/ppermute | solution.py:1119
  38.2 3.1 %collective-permute-done.8 = bf16[2,96,768]{2,1,0:T(8,128)(2,1)S(1)} collective-permute-done((bf16[2,96,768]{2,1,0:T(8,128)(2,1)S(1)}, bf16[2,96,768]{2,1,0:T(8,128)(2,1)S(1)}, u32[]{:S(2)}, u32[]{:S(2)}) %collective-permute-start.8) | collective-permute-done | bytes 294944 | tf_op jit(solution)/shard_map/ppermute | solution.py:1119
  50.1 7.8 %collective-permute-done.11.rest_1_ = bf16[8,12,48,128]{3,2,1,0:T(8,128)(2,1)S(1)} collective-permute-done((bf16[8,12,48,128]{3,2,1,0:T(8,128)(2,1)S(1)}, bf16[8,12,48,128]{3,2,1,0:T(8,128)(2,1)S(1)}, u32[]{:S(2)}, u32[]{:S(2)}) %collective-permute-start.11) | collective-permute-done | bytes 1179680 | tf_op jit(solution)/shard_map/ppermute | solution.py:1131
  64.2 3.4 %collective-permute-done.10.far = bf16[8,16,256]{2,1,0:T(8,128)(2,1)} collective-permute-done((bf16[8,16,256]{2,1,0:T(8,128)(2,1)S(1)}, bf16[8,16,256]{2,1,0:T(8,128)(2,1)}, u32[]{:S(2)}, u32[]{:S(2)}) %collective-permute-start.10) | collective-permute-done | bytes 65568 | tf_op jit(solution)/shard_map/ppermute | solution.py:1131
  67.6 3.7 %vectors.1 = (f32[8,768]{1,0:T(8,128)}, f32[1,3072]{1,0:T(1,128)}, bf16[12,128,640]{2,1,0:T(8,128)(2,1)}) custom-call(s32[2]{0:T(128)} %pad_add_fusion.ids, bf16[8,16,256]{2,1,0:T(8,128)(2,1)} %copy-done.25, bf16[8,16,256]{2,1,0:T(8,128)(2,1)} %collective-permute-done.10.far), custom_call_target="tpu_custom_call" | custom-call | bytes 9600000 | tf_op jit(solution)/shard_map/vectors/pallas_call | solution.py:383
  82.2 22.4 %attend.1 = (bf16[1024,768]{1,0:T(8,128)(2,1)}, bf16[512,768]{1,0:T(8,128)(2,1)}, bf16[512,768]{1,0:T(8,128)(2,1)}, bf16[1024,768]{1,0:T(8,128)(2,1)}, f32[3,1024,128]{2,1,0:T(8,128)}) custom-call(s32[2]{0:T(128)} %pad_add_fusion.ids, s32[2,8]{1,0:T(2,128)} %lengths.9, bf16[1024,768]{1,0:T(8,128)(2,1)} %get-tuple-element.151.xs.xs_far, ...), custom_call_target="tpu_custom_call" | custom-call | bytes 28800000 | tf_op jit(solution)/shard_map/attend/pallas_call | solution.py:524
  104.7 5.3 %collective-permute-done.18.far_own = bf16[8,2,96,768]{3,2,1,0:T(8,128)(2,1)S(1)} collective-permute-done((bf16[8,2,96,768]{3,2,1,0:T(8,128)(2,1)}, bf16[8,2,96,768]{3,2,1,0:T(8,128)(2,1)S(1)}, u32[]{:S(2)}, u32[]{:S(2)}) %collective-permute-start.18) | collective-permute-done | bytes 2359328 | tf_op jit(solution)/shard_map/ppermute | solution.py:1131
  110.0 4.5 %collective-permute-done.19.far_other = bf16[8,2,96,768]{3,2,1,0:T(8,128)(2,1)S(1)} collective-permute-done((bf16[8,2,96,768]{3,2,1,0:T(8,128)(2,1)S(1)}, bf16[8,2,96,768]{3,2,1,0:T(8,128)(2,1)S(1)}, u32[]{:S(2)}, u32[]{:S(2)}) %collective-permute-start.19) | collective-permute-done | bytes 2359328 | tf_op jit(solution)/shard_map/ppermute | solution.py:1115
  115.9 37.9 %feed.1 = (bf16[1024,768]{1,0:T(8,128)(2,1)}, bf16[1024,3072]{1,0:T(8,128)(2,1)}, bf16[1024,3072]{1,0:T(8,128)(2,1)}, bf16[1024,768]{1,0:T(8,128)(2,1)}, bf16[10...) custom-call(s32[2]{0:T(128)} %pad_add_fusion.ids, ...), custom_call_target="tpu_custom_call" | custom-call | bytes 57600000 | tf_op jit(solution)/shard_map/feed/pallas_call | solution.py:665
  153.8 10.3 %feed_weights.2 = (bf16[8,2,96,768]{3,2,1,0:T(8,128)(2,1)}, bf16[8,2,96,768]{3,2,1,0:T(8,128)(2,1)}) custom-call(bf16[1024,3072]{1,0:T(8,128)(2,1)} %get-tuple-element.178.act, bf16[1024,3072]{1,0:T(8,128)(2,1)} %get-tuple-element.179.gup, bf16[1024,768]{1,0:T(8,128)(2,1)} %get-tuple-element.180.first, bf16[1024,768]{1,0:T(8,128)(2,1)} %get-tuple-element.204.gdown), custom_call_target="tpu_custom_call" | custom-call | bytes 14400000 | tf_op jit(solution)/shard_map/feed_weights/pallas_call | solution.py:740
  164.3 4.8 %out_weights.1 = (bf16[8,9,48,128]{3,2,1,0:T(8,128)(2,1)}, bf16[8,9,48,128]{3,2,1,0:T(8,128)(2,1)}, bf16[8,9,48,128]{3,2,1,0:T(8,128)(2,1)}, bf16[8,9,48,128]{3,2,1,0:T(8,128)(2,1)}) custom-call(s32[2]{0:T(128)} %pad_add_fusion.ids, bf16[1024,768]{1,0:T(8,128)(2,1)} %get-tuple-element.183.mixed, bf16[1024,768]{1,0:T(8,128)(2,1)} %get-tuple-element.184.gbranch), custom_call_target="tpu_custom_call" | custom-call | bytes 6400000 | tf_op jit(solution)/shard_map/out_weights/pallas_call | solution.py:772
  172.3 15.2 %attend_back.3 = (f32[1024,768]{1,0:T(8,128)}, f32[16,768]{1,0:T(8,128)}, bf16[8,9,48,128]{3,2,1,0:T(8,128)(2,1)}, bf16[8,9,48,128]{3,2,1,0:T(8,128)(2,1)}, bf16...) custom-call(s32[2]{0:T(128)} %pad_add_fusion.ids, ...), custom_call_target="tpu_custom_call", output_to_operand_aliasing={{2}: (19, {}), {3}: (20, {}), {4}: (21, {}), {5}: (22, {})} | custom-call | bytes 22400000 | tf_op jit(solution)/shard_map/attend_back/pallas_call | solution.py:1013
  191.8 10.3 %feed_weights.3 = (bf16[8,2,96,768]{3,2,1,0:T(8,128)(2,1)}, bf16[8,2,96,768]{3,2,1,0:T(8,128)(2,1)}) custom-call(bf16[1024,3072]{1,0:T(8,128)(2,1)} %get-tuple-element.178.act, bf16[1024,3072]{1,0:T(8,128)(2,1)} %get-tuple-element.179.gup, bf16[1024,768]{1,0:T(8,128)(2,1)} %get-tuple-element.180.first, bf16[1024,768]{1,0:T(8,128)(2,1)} %get-tuple-element.204.gdown), custom_call_target="tpu_custom_call" | custom-call | bytes 14400000 | tf_op jit(solution)/shard_map/feed_weights/pallas_call | solution.py:740
  205.6 4.3 %unsort_rows.1 = (bf16[2,256,768]{2,1,0:T(8,128)(2,1)}, bf16[2,256,768]{2,1,0:T(8,128)(2,1)}) custom-call(s32[2]{0:T(128)} %pad_add_fusion.ids, s32[2,512]{1,0:T(2,128)} %order.9, bf16[1024,768]{1,0:T(8,128)(2,1)} %get-tuple-element.208.values), custom_call_target="tpu_custom_call" | custom-call | bytes 4800000 | tf_op jit(solution)/shard_map/unsort_rows/pallas_call | solution.py:239
  214.1 15.4 %attend_back.4 = (f32[1024,768]{1,0:T(8,128)}, f32[16,768]{1,0:T(8,128)}, bf16[8,9,48,128]{3,2,1,0:T(8,128)(2,1)}, bf16[8,9,48,128]{3,2,1,0:T(8,128)(2,1)}, bf16...) custom-call(s32[2]{0:T(128)} %pad_add_fusion.ids, ...), custom_call_target="tpu_custom_call", output_to_operand_aliasing={{2}: (19, {}), {3}: (20, {}), {4}: (21, {}), {5}: (22, {})} | custom-call | bytes 22400000 | tf_op jit(solution)/shard_map/attend_back/pallas_call | solution.py:1013
  234.7 17.8 %attend_back.5 = (bf16[2,256,768]{2,1,0:T(8,128)(2,1)}, bf16[2,256,768]{2,1,0:T(8,128)(2,1)}, bf16[8,4,48,128]{3,2,1,0:T(8,128)(2,1)}, bf16[8,4,48,128]{3,2,1,0:...) custom-call(s32[2]{0:T(128)} %pad_add_fusion.ids, s32[2,8]{1,0:T(2,128)} %lengths.9, ...), custom_call_target="tpu_custom_call" | custom-call | bytes 22400000 | tf_op jit(solution)/shard_map/attend_back/pallas_call | solution.py:1013
  264.6 8.1 %collective-permute-done.35 = bf16[2,96,768]{2,1,0:T(8,128)(2,1)S(1)} collective-permute-done((bf16[2,96,768]{2,1,0:T(8,128)(2,1)S(1)}, bf16[2,96,768]{2,1,0:T(8,128)(2,1)S(1)}, u32[]{:S(2)}, u32[]{:S(2)}) %collective-permute-start.35) | collective-permute-done | bytes 294944 | tf_op jit(solution)/shard_map/ppermute | solution.py:1119
  277.2 7.7 %collective-permute-done.36 = bf16[4,13,48,128]{3,2,1,0:T(8,128)(2,1)S(1)} collective-permute-done((bf16[4,13,48,128]{3,2,1,0:T(8,128)(2,1)S(1)}, bf16[4,13,48,128]{3,2,1,0:T(8,128)(2,1)S(1)}, u32[]{:S(2)}, u32[]{:S(2)}) %collective-permute-start.36) | collective-permute-done | bytes 639008 | tf_op jit(solution)/shard_map/ppermute | solution.py:1326
  290.1 3.6 %collective-permute-done.37 = bf16[13,48,128]{2,1,0:T(8,128)(2,1)S(1)} collective-permute-done((bf16[13,48,128]{2,1,0:T(8,128)(2,1)S(1)}, bf16[13,48,128]{2,1,0:T(8,128)(2,1)S(1)}, u32[]{:S(2)}, u32[]{:S(2)}) %collective-permute-start.37) | collective-permute-done | bytes 159776 | tf_op jit(solution)/shard_map/ppermute | solution.py:1251
  296.0 5.2 %collective-permute-done.38 = bf16[13,48,128]{2,1,0:T(8,128)(2,1)S(1)} collective-permute-done((bf16[13,48,128]{2,1,0:T(8,128)(2,1)S(1)}, bf16[13,48,128]{2,1,0:T(8,128)(2,1)S(1)}, u32[]{:S(2)}, u32[]{:S(2)}) %collective-permute-start.38) | collective-permute-done | bytes 159776 | tf_op jit(solution)/shard_map/ppermute | solution.py:1251
  (176 shorter events, 88.3 us)
Async XLA Ops:
  7.5 17.6 %collective-permute-start.2 = (bf16[12,48,128]{2,1,0:T(8,128)(2,1)}, bf16[12,48,128]{2,1,0:T(8,128)(2,1)S(1)}, u32[]{:S(2)}, u32[]{:S(2)}) collective-permute-start(bf16[12,48,128]{2,1,0:T(8,128)(2,1)} %get-tuple-element.148), channel_id=1, source_target_pairs={{0,24},{1,25},{2,26},{3,27},{4,28},{5,29},{6,30},{7,31},{8,16},{9,... | collective-permute-start | bytes 442376 | tf_op jit(solution)/shard_map/ppermute | solution.py:1119
  12.2 13.6 %collective-permute-start.1 = (bf16[12,48,128]{2,1,0:T(8,128)(2,1)}, bf16[12,48,128]{2,1,0:T(8,128)(2,1)S(1)}, u32[]{:S(2)}, u32[]{:S(2)}) collective-permute-start(bf16[12,48,128]{2,1,0:T(8,128)(2,1)} %get-tuple-element.148), channel_id=1, source_target_pairs={{0,16},{1,17},{2,18},{3,19},{4,20},{5,21},{6,22},{7,23},{8,24},{9,... | collective-permute-start | bytes 442376 | tf_op jit(solution)/shard_map/ppermute | solution.py:1119
  12.2 16.0 %collective-permute-start = (bf16[12,48,128]{2,1,0:T(8,128)(2,1)}, bf16[12,48,128]{2,1,0:T(8,128)(2,1)S(1)}, u32[]{:S(2)}, u32[]{:S(2)}) collective-permute-start(bf16[12,48,128]{2,1,0:T(8,128)(2,1)} %get-tuple-element.148), channel_id=1, source_target_pairs={{0,8},{1,9},{2,10},{3,11},{4,12},{5,13},{6,14},{7,15},{8,0},{9,1},... | collective-permute-start | bytes 442376 | tf_op jit(solution)/shard_map/ppermute | solution.py:1119
  25.8 15.6 %collective-permute-start.8 = (bf16[2,96,768]{2,1,0:T(8,128)(2,1)S(1)}, bf16[2,96,768]{2,1,0:T(8,128)(2,1)S(1)}, u32[]{:S(2)}, u32[]{:S(2)}) collective-permute-start(bf16[2,96,768]{2,1,0:T(8,128)(2,1)S(1)} %copy-done.12), channel_id=1, source_target_pairs={{0,16},{1,17},{2,18},{3,19},{4,20},{5,21},{6,22},{7,23},{8,24},{9,... | collective-permute-start | bytes 884744 | tf_op jit(solution)/shard_map/ppermute | solution.py:1119
  41.4 16.6 %collective-permute-start.11 = (bf16[8,12,48,128]{3,2,1,0:T(8,128)(2,1)S(1)}, bf16[8,12,48,128]{3,2,1,0:T(8,128)(2,1)S(1)}, u32[]{:S(2)}, u32[]{:S(2)}) collective-permute-start(bf16[8,12,48,128]{3,2,1,0:T(8,128)(2,1)S(1)} %constant_dynamic-update-slice_fusion.rest_0_), channel_id=1, source_target_pairs={{0,4},{1,3},{2,6},{3,1},{4,0},{5,7},{6,2},{7,5},{8,12},{9,11},{10,... | collective-permute-start | bytes 3538952 | tf_op jit(solution)/shard_map/ppermute | solution.py:1131
  42.9 15.0 %collective-permute-start.15 = (bf16[2,96,768]{2,1,0:T(8,128)(2,1)S(1)}, bf16[2,96,768]{2,1,0:T(8,128)(2,1)S(1)}, u32[]{:S(2)}, u32[]{:S(2)}) collective-permute-start(bf16[2,96,768]{2,1,0:T(8,128)(2,1)S(1)} %copy-done.12), channel_id=1, source_target_pairs={{0,24},{1,25},{2,26},{3,27},{4,28},{5,29},{6,30},{7,31},{8,16},{9,... | collective-permute-start | bytes 884744 | tf_op jit(solution)/shard_map/ppermute | solution.py:1119
  45.7 14.5 %collective-permute-start.14 = (bf16[2,96,768]{2,1,0:T(8,128)(2,1)S(1)}, bf16[2,96,768]{2,1,0:T(8,128)(2,1)S(1)}, u32[]{:S(2)}, u32[]{:S(2)}) collective-permute-start(bf16[2,96,768]{2,1,0:T(8,128)(2,1)S(1)} %copy-done.12), channel_id=1, source_target_pairs={{0,8},{1,9},{2,10},{3,11},{4,12},{5,13},{6,14},{7,15},{8,0},{9,1},... | collective-permute-start | bytes 884744 | tf_op jit(solution)/shard_map/ppermute | solution.py:1119
  61.4 17.2 %collective-permute-start.16 = (bf16[4,2,96,768]{3,2,1,0:T(8,128)(2,1)}, bf16[4,2,96,768]{3,2,1,0:T(8,128)(2,1)}, u32[]{:S(2)}, u32[]{:S(2)}) collective-permute-start(bf16[4,2,96,768]{3,2,1,0:T(8,128)(2,1)} %pad_maximum_fusion.1), channel_id=1, source_target_pairs={{0,2},{1,5},{2,0},{3,7},{4,6},{5,1},{6,4},{7,3},{8,10},{9,13},{10,... | collective-permute-start | bytes 3538952 | tf_op jit(solution)/shard_map/ppermute | solution.py:1127
  61.9 19.0 %collective-permute-start.13 = (bf16[8,12,48,128]{3,2,1,0:T(8,128)(2,1)S(1)}, bf16[8,12,48,128]{3,2,1,0:T(8,128)(2,1)}, u32[]{:S(2)}, u32[]{:S(2)}) collective-permute-start(bf16[8,12,48,128]{3,2,1,0:T(8,128)(2,1)S(1)} %collective-permute-done.11.rest_1_), channel_id=1, source_target_pairs={{0,1},{1,0},{2,3},{3,2},{4,5},{5,4},{6,7},{7,6},{8,9},{9,8},{10,11... | collective-permute-start | bytes 3538952 | tf_op jit(solution)/shard_map/ppermute | solution.py:1115
  80.9 29.1 %collective-permute-start.18 = (bf16[8,2,96,768]{3,2,1,0:T(8,128)(2,1)}, bf16[8,2,96,768]{3,2,1,0:T(8,128)(2,1)S(1)}, u32[]{:S(2)}, u32[]{:S(2)}) collective-permute-start(bf16[8,2,96,768]{3,2,1,0:T(8,128)(2,1)} %constant_dynamic-update-slice_fusion.7.near_own), channel_id=1, source_target_pairs={{0,4},{1,3},{2,6},{3,1},{4,0},{5,7},{6,2},{7,5},{8,12},{9,11},{10,... | collective-permute-start | bytes 7077896 | tf_op jit(solution)/shard_map/ppermute | solution.py:1131
  82.2 27.7 %collective-permute-start.17 = (bf16[8,2,96,768]{3,2,1,0:T(8,128)(2,1)}, bf16[8,2,96,768]{3,2,1,0:T(8,128)(2,1)}, u32[]{:S(2)}, u32[]{:S(2)}) collective-permute-start(bf16[8,2,96,768]{3,2,1,0:T(8,128)(2,1)} %constant_dynamic-update-slice_fusion.7.near_own), channel_id=1, source_target_pairs={{0,1},{1,0},{2,3},{3,2},{4,5},{5,4},{6,7},{7,6},{8,9},{9,8},{10,11... | collective-permute-start | bytes 7077896 | tf_op jit(solution)/shard_map/ppermute | solution.py:1115
  170.9 19.5 %collective-permute-start.21 = (bf16[5,2,96,768]{3,2,1,0:T(8,128)(2,1)S(1)}, bf16[5,2,96,768]{3,2,1,0:T(8,128)(2,1)}, u32[]{:S(2)}, u32[]{:S(2)}) collective-permute-start(bf16[5,2,96,768]{3,2,1,0:T(8,128)(2,1)S(1)} %add_convert_fusion), channel_id=1, source_target_pairs={{0,4},{1,3},{2,6},{3,1},{4,0},{5,7},{6,2},{7,5},{8,12},{9,11},{10,... | collective-permute-start | bytes 4423688 | tf_op jit(solution)/shard_map/ppermute | solution.py:1131
  190.4 13.3 %collective-permute-start.22 = (bf16[3,2,96,768]{3,2,1,0:T(8,128)(2,1)}, bf16[3,2,96,768]{3,2,1,0:T(8,128)(2,1)S(1)}, u32[]{:S(2)}, u32[]{:S(2)}) collective-permute-start(bf16[3,2,96,768]{3,2,1,0:T(8,128)(2,1)} %add_convert_fusion.3), channel_id=1, source_target_pairs={{0,4},{1,3},{2,6},{3,1},{4,0},{5,7},{6,2},{7,5},{8,12},{9,11},{10,... | collective-permute-start | bytes 2654216 | tf_op jit(solution)/shard_map/ppermute | solution.py:1131
  212.8 17.9 %collective-permute-start.25 = (bf16[4,2,96,768]{3,2,1,0:T(8,128)(2,1)S(1)}, bf16[4,2,96,768]{3,2,1,0:T(8,128)(2,1)}, u32[]{:S(2)}, u32[]{:S(2)}) collective-permute-start(bf16[4,2,96,768]{3,2,1,0:T(8,128)(2,1)S(1)} %add_convert_fusion.1), channel_id=1, source_target_pairs={{0,2},{1,5},{2,0},{3,7},{4,6},{5,1},{6,4},{7,3},{8,10},{9,13},{10,... | collective-permute-start | bytes 3538952 | tf_op jit(solution)/shard_map/ppermute | solution.py:1290
  229.6 23.0 %collective-permute-start.28 = (bf16[8,9,48,128]{3,2,1,0:T(8,128)(2,1)}, bf16[8,9,48,128]{3,2,1,0:T(8,128)(2,1)}, u32[]{:S(2)}, u32[]{:S(2)}) collective-permute-start(bf16[8,9,48,128]{3,2,1,0:T(8,128)(2,1)} %get-tuple-element.236), channel_id=1, source_target_pairs={{0,1},{1,0},{2,3},{3,2},{4,5},{5,4},{6,7},{7,6},{8,9},{9,8},{10,11... | collective-permute-start | bytes 2654216 | tf_op jit(solution)/shard_map/ppermute | solution.py:1115
  230.6 22.0 %collective-permute-start.29 = (bf16[8,9,48,128]{3,2,1,0:T(8,128)(2,1)}, bf16[8,9,48,128]{3,2,1,0:T(8,128)(2,1)}, u32[]{:S(2)}, u32[]{:S(2)}) collective-permute-start(bf16[8,9,48,128]{3,2,1,0:T(8,128)(2,1)} %get-tuple-element.237), channel_id=1, source_target_pairs={{0,1},{1,0},{2,3},{3,2},{4,5},{5,4},{6,7},{7,6},{8,9},{9,8},{10,11... | collective-permute-start | bytes 2654216 | tf_op jit(solution)/shard_map/ppermute | solution.py:1115
  233.6 18.9 %collective-permute-start.27 = (bf16[2,96,768]{2,1,0:T(8,128)(2,1)}, bf16[2,96,768]{2,1,0:T(8,128)(2,1)}, u32[]{:S(2)}, u32[]{:S(2)}) collective-permute-start(bf16[2,96,768]{2,1,0:T(8,128)(2,1)} %get-tuple-element.235), channel_id=1, source_target_pairs={{0,16},{1,17},{2,18},{3,19},{4,20},{5,21},{6,22},{7,23},{8,24},{9,... | collective-permute-start | bytes 884744 | tf_op jit(solution)/shard_map/ppermute | solution.py:1119
  233.6 25.9 %collective-permute-start.23 = (bf16[2,256,768]{2,1,0:T(8,128)(2,1)}, bf16[2,256,768]{2,1,0:T(8,128)(2,1)}, u32[]{:S(2)}, u32[]{:S(2)}) collective-permute-start(bf16[2,256,768]{2,1,0:T(8,128)(2,1)} %get-tuple-element.210), channel_id=1, source_target_pairs={{0,1},{1,0},{2,3},{3,2},{4,5},{5,4},{6,7},{7,6},{8,9},{9,8},{10,11... | collective-permute-start | bytes 2359304 | tf_op jit(solution)/shard_map/ppermute | solution.py:1115
  254.3 18.5 %collective-permute-start.30 = (bf16[8,9,48,128]{3,2,1,0:T(8,128)(2,1)S(1)}, bf16[8,9,48,128]{3,2,1,0:T(8,128)(2,1)S(1)}, u32[]{:S(2)}, u32[]{:S(2)}) collective-permute-start(bf16[8,9,48,128]{3,2,1,0:T(8,128)(2,1)S(1)} %add_convert_fusion.2), channel_id=1, source_target_pairs={{0,4},{1,3},{2,6},{3,1},{4,0},{5,7},{6,2},{7,5},{8,12},{9,11},{10,... | collective-permute-start | bytes 2654216 | tf_op jit(solution)/shard_map/ppermute | solution.py:1131
  256.9 15.8 %collective-permute-start.35 = (bf16[2,96,768]{2,1,0:T(8,128)(2,1)S(1)}, bf16[2,96,768]{2,1,0:T(8,128)(2,1)S(1)}, u32[]{:S(2)}, u32[]{:S(2)}) collective-permute-start(bf16[2,96,768]{2,1,0:T(8,128)(2,1)S(1)} %get-tuple-element.250), channel_id=1, source_target_pairs={{0,24},{1,25},{2,26},{3,27},{4,28},{5,29},{6,30},{7,31},{8,16},{9,... | collective-permute-start | bytes 884744 | tf_op jit(solution)/shard_map/ppermute | solution.py:1119
  259.4 13.3 %collective-permute-start.33 = (bf16[8,4,48,128]{3,2,1,0:T(8,128)(2,1)S(1)}, bf16[8,4,48,128]{3,2,1,0:T(8,128)(2,1)S(1)}, u32[]{:S(2)}, u32[]{:S(2)}) collective-permute-start(bf16[8,4,48,128]{3,2,1,0:T(8,128)(2,1)S(1)} %copy-done.30), channel_id=1, source_target_pairs={{0,1},{1,0},{2,3},{3,2},{4,5},{5,4},{6,7},{7,6},{8,9},{9,8},{10,11... | collective-permute-start | bytes 1179656 | tf_op jit(solution)/shard_map/ppermute | solution.py:1115
  259.5 13.2 %collective-permute-start.32 = (bf16[8,4,48,128]{3,2,1,0:T(8,128)(2,1)S(1)}, bf16[8,4,48,128]{3,2,1,0:T(8,128)(2,1)S(1)}, u32[]{:S(2)}, u32[]{:S(2)}) collective-permute-start(bf16[8,4,48,128]{3,2,1,0:T(8,128)(2,1)S(1)} %add_convert_fusion.4), channel_id=1, source_target_pairs={{0,4},{1,3},{2,6},{3,1},{4,0},{5,7},{6,2},{7,5},{8,12},{9,11},{10,... | collective-permute-start | bytes 1179656 | tf_op jit(solution)/shard_map/ppermute | solution.py:1131
  277.2 24.2 %collective-permute-start.41 = (f32[2,96,768]{2,1,0:T(8,128)S(1)}, f32[2,96,768]{2,1,0:T(8,128)S(1)}, u32[]{:S(2)}, u32[]{:S(2)}) collective-permute-start(f32[2,96,768]{2,1,0:T(8,128)S(1)} %bitcast_add_fusion), channel_id=1, source_target_pairs={{0,1},{1,0},{2,3},{3,2},{4,5},{5,4},{6,7},{7,6},{8,9},{9,8},{10,11... | collective-permute-start | bytes 1769480 | tf_op jit(solution)/shard_map/ppermute | solution.py:1115
  287.9 13.3 %collective-permute-start.38 = (bf16[13,48,128]{2,1,0:T(8,128)(2,1)S(1)}, bf16[13,48,128]{2,1,0:T(8,128)(2,1)S(1)}, u32[]{:S(2)}, u32[]{:S(2)}) collective-permute-start(bf16[13,48,128]{2,1,0:T(8,128)(2,1)S(1)} %get-tuple-element.293), channel_id=1, source_target_pairs={{0,16},{1,17},{2,18},{3,19},{4,20},{5,21},{6,22},{7,23},{8,24},{9,... | collective-permute-start | bytes 479240 | tf_op jit(solution)/shard_map/ppermute | solution.py:1251
  (49 other events, 378.4 us)

commit v6 on v5

--- a/solution.py
+++ b/solution.py
@@ -578,22 +578,23 @@
 BLOCK = 256
 
 
-def feed_kernel(ids, xs, mixed, cot, rows, up_bias, near_own, near_other, far_own, far_other,
-                *rest):
+def feed_kernel(ids, xs, mixed, cot, rows, up_bias, *rest):
+    feeds, rest = rest[:8], rest[8:]
     pieces, rest = rest[:-14], rest[-14:]
     (out, act_out, gup_out, first_out, gdown_out, gres_out, gbranch_out, gmixed_out,
      sums, up_sums, up_all, down_all, wo_all, sems) = rest
     step = pl.program_id(0)
     units = up_all.shape[0] // 4
-    parts = (near_own, near_other, far_own, far_other)
+    parts = [feeds[index : index + 2] for index in range(0, 8, 2)]
     held = sum(piece.shape[0] for piece in pieces)
 
     def weight_copies():
         copies = []
-        share = near_own.shape[2]
-        for index, part in enumerate(parts):
-            for block in range(part.shape[0]):
-                here = slice(index * units + block * share, index * units + (block + 1) * share)
+        share = feeds[0].shape[2]
+        for index, pair in enumerate(parts):
+            blocks = [(part, block) for part in pair for block in range(part.shape[0])]
+            for at, (part, block) in enumerate(blocks):
+                here = slice(index * units + at * share, index * units + (at + 1) * share)
                 for which, target in ((0, up_all), (1, down_all)):
                     copies.append(
                         pltpu.make_async_copy(
@@ -681,7 +682,7 @@
             SMEM_SPEC, token, token, token,
             pl.BlockSpec((8, width), lambda i: (0, 0)),
             pl.BlockSpec((1, hidden), lambda i: (0, 0)),
-        ] + [ANY_SPEC] * 4 + [HBM_SPEC] * len(pieces),
+        ] + [ANY_SPEC] * len(feeds) + [HBM_SPEC] * len(pieces),
         out_specs=(token, wide, wide, token, token, token, token, token,
                    pl.BlockSpec((8, width), lambda i: (0, 0)),
                    pl.BlockSpec((1, hidden), lambda i: (0, 0))),
@@ -1201,9 +1202,13 @@
         for high in range(1, count // 4)
     ]
     feed_parts = lax.optimization_barrier((feed_parts, square_far))[0]
-    feed_near = low_round(jnp.stack([feed_own] + feed_parts), count)
+    feed_high = jnp.stack([feed_own] + feed_parts)
+    feed_near = lax.ppermute(feed_high, BOTH, xor_pairs(count, (1, 2)))
     vector_rows, up_biases, bias = vectors_to_all(ids, slots_near, slots_far, width, sizes)
-    feed_near = after(feed_near, far_swapped, bias)
+    feed_near, feed_high = lax.optimization_barrier(
+        (feed_near, feed_high, far_swapped, bias)
+    )[:2]
+    feed_near = (feed_high, feed_near)
     pieces = (square_near, square_far, near_swapped, far_swapped)
 
     flips = offsets(count, half)
@@ -1220,10 +1225,13 @@
         pieces = tuple(ordered)
 
     q, k, v, mixed, lse = attend(ids, lengths, xs, mask, bias, vector_rows, pieces)
-    feed_far = last_round(feed_near, count)
-    feed_far = after(feed_far, mixed)
-
-    feeds = (feed_near, swap(feed_near), feed_far, swap(feed_far))
+    feed_far = [last_round(part, count) for part in feed_near]
+    feed_far = lax.optimization_barrier((feed_far, mixed))[0]
+
+    feeds = [
+        part for pair in (feed_near, map(swap, feed_near), feed_far, map(swap, feed_far))
+        for part in pair
+    ]
     out, act, gup, first, gdown, gres, gbranch, gmixed, sums, up_sums = feed(
         ids, xs, mixed, cs, vector_rows, up_biases, feeds, pieces
     )

time: 312 us -> 309 us (level)
  local copies, waits for them, and re-layouts: 18 us -> 10.3 us
  starting transfers between devices: 39 us -> 42.2 us
    ppermute x0 -> x1, waiting for transfers between devices: none -> 6.6 us  [shards(): feed_near = lax.ppermute(feed_high, BOTH, xor_pairs(count, (1, 2)))]
    unnamed x71 -> x65, local copies, waits for them, and re-layouts: 10.8 us -> 5.58 us
    ppermute x3 -> x2, waiting for transfers between devices: 8.17 us -> 5.18 us  [low_round(): lax.ppermute(value, BOTH, xor_pairs(count, (1, 2)))]
    ppermute x7 -> x8, starting transfers between devices: 9.09 us -> 9.93 us  [last_round(): return lax.ppermute(value, BOTH, xor_pairs(count, (2, 1)))]
    ppermute x7 -> x8, waiting for transfers between devices: 18.7 us -> 18.2 us  [last_round(): return lax.ppermute(value, BOTH, xor_pairs(count, (2, 1)))]
  transfers between devices with their start and end apart: 42 -> 45, of which waited for: 19 -> 20; matrix products, arithmetic and copies ran while one was open for 9% -> 6% of each run, Pallas kernels for 33% -> 33%
where the time goes in v6:
time: 309 us; the launch traced here: 304 us
  Pallas kernels  155 us (50%)
  waiting for transfers between devices  73.6 us (24%)
  starting transfers between devices  42.2 us (14%)
  other arithmetic  20.9 us (7%)
  local copies, waits for them, and re-layouts  10.3 us (3%)
    pallas_call x3, Pallas kernels, attend_back(): pl.pallas_call(functools.partial(attend_back_kernel, rows_each, base, ste...  48.4 us
    pallas_call x1, Pallas kernels, feed(): pl.pallas_call(feed_kernel, grid=(tokens // BLOCK,), out_shape=(low, SDS(...  37.9 us
    pallas_call x1, Pallas kernels, attend(): pl.pallas_call(attend_kernel, grid=(GROUPS,), out_shape=(SDS((tokens, wid...  22.5 us
    pallas_call x2, Pallas kernels, feed_weights(): pl.pallas_call(functools.partial(feed_weights_kernel, part), out_shape=(S...  20.6 us
    ppermute x12, waiting for transfers between devices, high_part(): return lax.ppermute(value, BOTH, xor_pairs(count, (4 * high, 4 * high)))  20.3 us
    ppermute x12, starting transfers between devices, high_part(): return lax.ppermute(value, BOTH, xor_pairs(count, (4 * high, 4 * high)))  19 us
    ppermute x8, waiting for transfers between devices, last_round(): return lax.ppermute(value, BOTH, xor_pairs(count, (2, 1)))  18.2 us
    ppermute x3, waiting for transfers between devices, high_parts_of(): lax.ppermute(low(total[high]), BOTH, xor_pairs(count, (4 * high, 4 * high)))  11.1 us
  transfers between devices with their start and end apart: 45, of which 20 were waited for; matrix products, arithmetic and copies ran while one was open for 6% of the time, Pallas kernels for 33%

profile of v6, /device:TPU:0, one launch (start us, length us, event | category | flops | bytes accessed | tf_op | source)
XLA Modules:
  0.0 303.7 jit_solution(3589352356491550344)
XLA Ops:
  2.5 4.4 %pack.1 = (bf16[4,256,768]{2,1,0:T(8,128)(2,1)}, bf16[12,48,128]{2,1,0:T(8,128)(2,1)}, bf16[2,96,768]{2,1,0:T(8,128)(2,1)}, bf16[16,256]{1,0:T(8,128)(2,1)}) custom-call(s32[2]{0:T(128)} %pad_add_fusion.ids, bf16[2,256,768]{2,1,0:T(8,128)(2,1)} %content.3, bf16[2,256,768]{2,1,0:T(8,128)(2,1)} %query.3, bf16[2,256,768]{2,1,0:T(8,128)(2,1)} %ccot.3, ...), custom_call_target="tpu_custom_call" | custom-call | bytes 6400000 | tf_op jit(solution)/shard_map/pack/pallas_call | solution.py:116
  7.5 4.7 %collective-permute-start.2 = (bf16[12,48,128]{2,1,0:T(8,128)(2,1)}, bf16[12,48,128]{2,1,0:T(8,128)(2,1)S(1)}, u32[]{:S(2)}, u32[]{:S(2)}) collective-permute-start(bf16[12,48,128]{2,1,0:T(8,128)(2,1)} %get-tuple-element.150), channel_id=1, source_target_pairs={{0,24},{1,25},{2,26},{3,27},{4,28},{5,29},{6,30},{7,31},{8,16},{9,... | collective-permute-start | bytes 442376 | tf_op jit(solution)/shard_map/ppermute | solution.py:1120
  15.0 6.4 %sort_rows.1 = (bf16[1024,768]{1,0:T(8,128)(2,1)}, bf16[1024,768]{1,0:T(8,128)(2,1)}, bf16[2,512,512]{2,1,0:T(8,128)(2,1)}) custom-call(s32[2]{0:T(128)} %pad_add_fusion.ids, s32[2,8]{1,0:T(2,128)} %lengths.9, bf16[2,256,768]{2,1,0:T(8,128)(2,1)} %content.3, bf16[2,256,768]{2,1,0:T(8,128)(2,1)} %query.3, bf16[2,256,768]{2,1,0:T(8,128)(2,1)} %ccot.3, ...), custom_call_target="tpu_custom_call" | custom-call | bytes 8000000 | tf_op jit(solution)/shard_map/sort_rows/pallas_call | solution.py:192
  21.3 3.8 %collective-permute-start.7 = (bf16[16,256]{1,0:T(8,128)(2,1)S(1)}, bf16[16,256]{1,0:T(8,128)(2,1)S(1)}, u32[]{:S(2)}, u32[]{:S(2)}) collective-permute-start(bf16[16,256]{1,0:T(8,128)(2,1)S(1)} %copy-done.27), channel_id=1, source_target_pairs={{0,24},{1,25},{2,26},{3,27},{4,28},{5,29},{6,30},{7,31},{8,16},{9,... | collective-permute-start | bytes 24584 | tf_op jit(solution)/shard_map/ppermute | solution.py:1120
  29.9 5.9 %collective-permute-done.6 = bf16[16,256]{1,0:T(8,128)(2,1)S(1)} collective-permute-done((bf16[16,256]{1,0:T(8,128)(2,1)S(1)}, bf16[16,256]{1,0:T(8,128)(2,1)S(1)}, u32[]{:S(2)}, u32[]{:S(2)}) %collective-permute-start.6) | collective-permute-done | bytes 8224 | tf_op jit(solution)/shard_map/ppermute | solution.py:1120
  50.1 7.8 %collective-permute-done.11.rest_1_.rest_9_ = bf16[8,12,48,128]{3,2,1,0:T(8,128)(2,1)S(1)} collective-permute-done((bf16[8,12,48,128]{3,2,1,0:T(8,128)(2,1)S(1)}, bf16[8,12,48,128]{3,2,1,0:T(8,128)(2,1)S(1)}, u32[]{:S(2)}, u32[]{:S(2)}) %collective-permute-start.11) | collective-permute-done | bytes 1179680 | tf_op jit(solution)/shard_map/ppermute | solution.py:1132
  63.4 4.1 %collective-permute-done.10.far = bf16[8,16,256]{2,1,0:T(8,128)(2,1)S(1)} collective-permute-done((bf16[8,16,256]{2,1,0:T(8,128)(2,1)S(1)}, bf16[8,16,256]{2,1,0:T(8,128)(2,1)S(1)}, u32[]{:S(2)}, u32[]{:S(2)}) %collective-permute-start.10) | collective-permute-done | bytes 65568 | tf_op jit(solution)/shard_map/ppermute | solution.py:1132
  68.1 3.8 %vectors.1 = (f32[8,768]{1,0:T(8,128)}, f32[1,3072]{1,0:T(1,128)}, bf16[12,128,640]{2,1,0:T(8,128)(2,1)}) custom-call(s32[2]{0:T(128)} %pad_add_fusion.ids, bf16[8,16,256]{2,1,0:T(8,128)(2,1)} %copy-done.23, bf16[8,16,256]{2,1,0:T(8,128)(2,1)} %copy-done.24), custom_call_target="tpu_custom_call" | custom-call | bytes 9600000 | tf_op jit(solution)/shard_map/vectors/pallas_call | solution.py:383
  71.9 6.6 %collective-permute-done.16.rest_1_ = bf16[4,2,96,768]{3,2,1,0:T(8,128)(2,1)} collective-permute-done((bf16[4,2,96,768]{3,2,1,0:T(8,128)(2,1)}, bf16[4,2,96,768]{3,2,1,0:T(8,128)(2,1)}, u32[]{:S(2)}, u32[]{:S(2)}) %collective-permute-start.16) | collective-permute-done | bytes 1179680 | tf_op jit(solution)/shard_map/ppermute | solution.py:1206
  81.1 22.5 %attend.1 = (bf16[1024,768]{1,0:T(8,128)(2,1)}, bf16[512,768]{1,0:T(8,128)(2,1)}, bf16[512,768]{1,0:T(8,128)(2,1)}, bf16[1024,768]{1,0:T(8,128)(2,1)}, f32[3,1024,128]{2,1,0:T(8,128)}) custom-call(s32[2]{0:T(128)} %pad_add_fusion.ids, s32[2,8]{1,0:T(2,128)} %lengths.9, bf16[1024,768]{1,0:T(8,128)(2,1)} %get-tuple-element.153.xs.xs_far, ...), custom_call_target="tpu_custom_call" | custom-call | bytes 28800000 | tf_op jit(solution)/shard_map/attend/pallas_call | solution.py:524
  103.5 4.1 %collective-permute-done.20.rest_5_ = bf16[4,2,96,768]{3,2,1,0:T(8,128)(2,1)} collective-permute-done((bf16[4,2,96,768]{3,2,1,0:T(8,128)(2,1)}, bf16[4,2,96,768]{3,2,1,0:T(8,128)(2,1)}, u32[]{:S(2)}, u32[]{:S(2)}) %collective-permute-start.20) | collective-permute-done | bytes 1179680 | tf_op jit(solution)/shard_map/ppermute | solution.py:1132
  113.4 37.9 %feed.1 = (bf16[1024,768]{1,0:T(8,128)(2,1)}, bf16[1024,3072]{1,0:T(8,128)(2,1)}, bf16[1024,3072]{1,0:T(8,128)(2,1)}, bf16[1024,768]{1,0:T(8,128)(2,1)}, bf16[10...) custom-call(s32[2]{0:T(128)} %pad_add_fusion.ids, ...), custom_call_target="tpu_custom_call" | custom-call | bytes 57600000 | tf_op jit(solution)/shard_map/feed/pallas_call | solution.py:666
  151.4 10.3 %feed_weights.2 = (bf16[8,2,96,768]{3,2,1,0:T(8,128)(2,1)}, bf16[8,2,96,768]{3,2,1,0:T(8,128)(2,1)}) custom-call(bf16[1024,3072]{1,0:T(8,128)(2,1)} %get-tuple-element.182.act, bf16[1024,3072]{1,0:T(8,128)(2,1)} %get-tuple-element.183.gup, bf16[1024,768]{1,0:T(8,128)(2,1)} %get-tuple-element.184.first, bf16[1024,768]{1,0:T(8,128)(2,1)} %get-tuple-element.208.gdown), custom_call_target="tpu_custom_call" | custom-call | bytes 14400000 | tf_op jit(solution)/shard_map/feed_weights/pallas_call | solution.py:741
  161.9 4.8 %out_weights.1 = (bf16[8,9,48,128]{3,2,1,0:T(8,128)(2,1)}, bf16[8,9,48,128]{3,2,1,0:T(8,128)(2,1)}, bf16[8,9,48,128]{3,2,1,0:T(8,128)(2,1)}, bf16[8,9,48,128]{3,2,1,0:T(8,128)(2,1)}) custom-call(s32[2]{0:T(128)} %pad_add_fusion.ids, bf16[1024,768]{1,0:T(8,128)(2,1)} %get-tuple-element.187.mixed, bf16[1024,768]{1,0:T(8,128)(2,1)} %get-tuple-element.188.gbranch), custom_call_target="tpu_custom_call" | custom-call | bytes 6400000 | tf_op jit(solution)/shard_map/out_weights/pallas_call | solution.py:773
  169.8 15.2 %attend_back.3 = (f32[1024,768]{1,0:T(8,128)}, f32[16,768]{1,0:T(8,128)}, bf16[8,9,48,128]{3,2,1,0:T(8,128)(2,1)}, bf16[8,9,48,128]{3,2,1,0:T(8,128)(2,1)}, bf16...) custom-call(s32[2]{0:T(128)} %pad_add_fusion.ids, ...), custom_call_target="tpu_custom_call", output_to_operand_aliasing={{2}: (19, {}), {3}: (20, {}), {4}: (21, {}), {5}: (22, {})} | custom-call | bytes 22400000 | tf_op jit(solution)/shard_map/attend_back/pallas_call | solution.py:1014
  189.3 10.3 %feed_weights.3 = (bf16[8,2,96,768]{3,2,1,0:T(8,128)(2,1)}, bf16[8,2,96,768]{3,2,1,0:T(8,128)(2,1)}) custom-call(bf16[1024,3072]{1,0:T(8,128)(2,1)} %get-tuple-element.182.act, bf16[1024,3072]{1,0:T(8,128)(2,1)} %get-tuple-element.183.gup, bf16[1024,768]{1,0:T(8,128)(2,1)} %get-tuple-element.184.first, bf16[1024,768]{1,0:T(8,128)(2,1)} %get-tuple-element.208.gdown), custom_call_target="tpu_custom_call" | custom-call | bytes 14400000 | tf_op jit(solution)/shard_map/feed_weights/pallas_call | solution.py:741
  203.1 4.3 %unsort_rows.1 = (bf16[2,256,768]{2,1,0:T(8,128)(2,1)}, bf16[2,256,768]{2,1,0:T(8,128)(2,1)}) custom-call(s32[2]{0:T(128)} %pad_add_fusion.ids, s32[2,512]{1,0:T(2,128)} %order.9, bf16[1024,768]{1,0:T(8,128)(2,1)} %get-tuple-element.212.values), custom_call_target="tpu_custom_call" | custom-call | bytes 4800000 | tf_op jit(solution)/shard_map/unsort_rows/pallas_call | solution.py:239
  211.6 15.4 %attend_back.4 = (f32[1024,768]{1,0:T(8,128)}, f32[16,768]{1,0:T(8,128)}, bf16[8,9,48,128]{3,2,1,0:T(8,128)(2,1)}, bf16[8,9,48,128]{3,2,1,0:T(8,128)(2,1)}, bf16...) custom-call(s32[2]{0:T(128)} %pad_add_fusion.ids, ...), custom_call_target="tpu_custom_call", output_to_operand_aliasing={{2}: (19, {}), {3}: (20, {}), {4}: (21, {}), {5}: (22, {})} | custom-call | bytes 22400000 | tf_op jit(solution)/shard_map/attend_back/pallas_call | solution.py:1014
  232.3 17.8 %attend_back.5 = (bf16[2,256,768]{2,1,0:T(8,128)(2,1)}, bf16[2,256,768]{2,1,0:T(8,128)(2,1)}, bf16[8,4,48,128]{3,2,1,0:T(8,128)(2,1)}, bf16[8,4,48,128]{3,2,1,0:...) custom-call(s32[2]{0:T(128)} %pad_add_fusion.ids, s32[2,8]{1,0:T(2,128)} %lengths.9, ...), custom_call_target="tpu_custom_call" | custom-call | bytes 22400000 | tf_op jit(solution)/shard_map/attend_back/pallas_call | solution.py:1014
  262.3 7.9 %collective-permute-done.38 = bf16[2,96,768]{2,1,0:T(8,128)(2,1)S(1)} collective-permute-done((bf16[2,96,768]{2,1,0:T(8,128)(2,1)S(1)}, bf16[2,96,768]{2,1,0:T(8,128)(2,1)S(1)}, u32[]{:S(2)}, u32[]{:S(2)}) %collective-permute-start.38) | collective-permute-done | bytes 294944 | tf_op jit(solution)/shard_map/ppermute | solution.py:1120
  275.0 7.5 %collective-permute-done.39 = bf16[4,13,48,128]{3,2,1,0:T(8,128)(2,1)S(1)} collective-permute-done((bf16[4,13,48,128]{3,2,1,0:T(8,128)(2,1)S(1)}, bf16[4,13,48,128]{3,2,1,0:T(8,128)(2,1)S(1)}, u32[]{:S(2)}, u32[]{:S(2)}) %collective-permute-start.39) | collective-permute-done | bytes 639008 | tf_op jit(solution)/shard_map/ppermute | solution.py:1334
  282.8 3.2 %collective-permute-start.42 = (bf16[13,48,128]{2,1,0:T(8,128)(2,1)S(1)}, bf16[13,48,128]{2,1,0:T(8,128)(2,1)S(1)}, u32[]{:S(2)}, u32[]{:S(2)}) collective-permute-start(bf16[13,48,128]{2,1,0:T(8,128)(2,1)S(1)} %get-tuple-element.296), channel_id=1, source_target_pairs={{0,24},{1,25},{2,26},{3,27},{4,28},{5,29},{6,30},{7,31},{8,16},{9,... | collective-permute-start | bytes 479240 | tf_op jit(solution)/shard_map/ppermute | solution.py:1259
  290.4 3.1 %collective-permute-done.42 = bf16[13,48,128]{2,1,0:T(8,128)(2,1)S(1)} collective-permute-done((bf16[13,48,128]{2,1,0:T(8,128)(2,1)S(1)}, bf16[13,48,128]{2,1,0:T(8,128)(2,1)S(1)}, u32[]{:S(2)}, u32[]{:S(2)}) %collective-permute-start.42) | collective-permute-done | bytes 159776 | tf_op jit(solution)/shard_map/ppermute | solution.py:1259
  293.5 5.2 %collective-permute-done.41 = bf16[13,48,128]{2,1,0:T(8,128)(2,1)S(1)} collective-permute-done((bf16[13,48,128]{2,1,0:T(8,128)(2,1)S(1)}, bf16[13,48,128]{2,1,0:T(8,128)(2,1)S(1)}, u32[]{:S(2)}, u32[]{:S(2)}) %collective-permute-start.41) | collective-permute-done | bytes 159776 | tf_op jit(solution)/shard_map/ppermute | solution.py:1259
  (175 shorter events, 85.1 us)
Async XLA Ops:
  7.5 17.7 %collective-permute-start.2 = (bf16[12,48,128]{2,1,0:T(8,128)(2,1)}, bf16[12,48,128]{2,1,0:T(8,128)(2,1)S(1)}, u32[]{:S(2)}, u32[]{:S(2)}) collective-permute-start(bf16[12,48,128]{2,1,0:T(8,128)(2,1)} %get-tuple-element.150), channel_id=1, source_target_pairs={{0,24},{1,25},{2,26},{3,27},{4,28},{5,29},{6,30},{7,31},{8,16},{9,... | collective-permute-start | bytes 442376 | tf_op jit(solution)/shard_map/ppermute | solution.py:1120
  12.1 13.7 %collective-permute-start.1 = (bf16[12,48,128]{2,1,0:T(8,128)(2,1)}, bf16[12,48,128]{2,1,0:T(8,128)(2,1)S(1)}, u32[]{:S(2)}, u32[]{:S(2)}) collective-permute-start(bf16[12,48,128]{2,1,0:T(8,128)(2,1)} %get-tuple-element.150), channel_id=1, source_target_pairs={{0,16},{1,17},{2,18},{3,19},{4,20},{5,21},{6,22},{7,23},{8,24},{9,... | collective-permute-start | bytes 442376 | tf_op jit(solution)/shard_map/ppermute | solution.py:1120
  12.1 16.0 %collective-permute-start = (bf16[12,48,128]{2,1,0:T(8,128)(2,1)}, bf16[12,48,128]{2,1,0:T(8,128)(2,1)S(1)}, u32[]{:S(2)}, u32[]{:S(2)}) collective-permute-start(bf16[12,48,128]{2,1,0:T(8,128)(2,1)} %get-tuple-element.150), channel_id=1, source_target_pairs={{0,8},{1,9},{2,10},{3,11},{4,12},{5,13},{6,14},{7,15},{8,0},{9,1},... | collective-permute-start | bytes 442376 | tf_op jit(solution)/shard_map/ppermute | solution.py:1120
  25.8 15.5 %collective-permute-start.8 = (bf16[2,96,768]{2,1,0:T(8,128)(2,1)S(1)}, bf16[2,96,768]{2,1,0:T(8,128)(2,1)S(1)}, u32[]{:S(2)}, u32[]{:S(2)}) collective-permute-start(bf16[2,96,768]{2,1,0:T(8,128)(2,1)S(1)} %copy-done.19), channel_id=1, source_target_pairs={{0,16},{1,17},{2,18},{3,19},{4,20},{5,21},{6,22},{7,23},{8,24},{9,... | collective-permute-start | bytes 884744 | tf_op jit(solution)/shard_map/ppermute | solution.py:1120
  41.3 16.6 %collective-permute-start.11 = (bf16[8,12,48,128]{3,2,1,0:T(8,128)(2,1)S(1)}, bf16[8,12,48,128]{3,2,1,0:T(8,128)(2,1)S(1)}, u32[]{:S(2)}, u32[]{:S(2)}) collective-permute-start(bf16[8,12,48,128]{3,2,1,0:T(8,128)(2,1)S(1)} %constant_dynamic-update-slice_fusion.rest_0_.rest_8_), channel_id=1, source_target_pairs={{0,4},{1,3},{2,6},{3,1},{4,0},{5,7},{6,2},{7,5},{8,12},{9,11},{10,... | collective-permute-start | bytes 3538952 | tf_op jit(solution)/shard_map/ppermute | solution.py:1132
  42.8 15.0 %collective-permute-start.15 = (bf16[2,96,768]{2,1,0:T(8,128)(2,1)S(1)}, bf16[2,96,768]{2,1,0:T(8,128)(2,1)S(1)}, u32[]{:S(2)}, u32[]{:S(2)}) collective-permute-start(bf16[2,96,768]{2,1,0:T(8,128)(2,1)S(1)} %copy-done.19), channel_id=1, source_target_pairs={{0,24},{1,25},{2,26},{3,27},{4,28},{5,29},{6,30},{7,31},{8,16},{9,... | collective-permute-start | bytes 884744 | tf_op jit(solution)/shard_map/ppermute | solution.py:1120
  45.8 14.4 %collective-permute-start.14 = (bf16[2,96,768]{2,1,0:T(8,128)(2,1)S(1)}, bf16[2,96,768]{2,1,0:T(8,128)(2,1)S(1)}, u32[]{:S(2)}, u32[]{:S(2)}) collective-permute-start(bf16[2,96,768]{2,1,0:T(8,128)(2,1)S(1)} %copy-done.19), channel_id=1, source_target_pairs={{0,8},{1,9},{2,10},{3,11},{4,12},{5,13},{6,14},{7,15},{8,0},{9,1},... | collective-permute-start | bytes 884744 | tf_op jit(solution)/shard_map/ppermute | solution.py:1120
  61.4 17.2 %collective-permute-start.16 = (bf16[4,2,96,768]{3,2,1,0:T(8,128)(2,1)}, bf16[4,2,96,768]{3,2,1,0:T(8,128)(2,1)}, u32[]{:S(2)}, u32[]{:S(2)}) collective-permute-start(bf16[4,2,96,768]{3,2,1,0:T(8,128)(2,1)} %pad_maximum_fusion.1.rest_0_), channel_id=1, source_target_pairs={{0,2},{1,5},{2,0},{3,7},{4,6},{5,1},{6,4},{7,3},{8,10},{9,13},{10,... | collective-permute-start | bytes 3538952 | tf_op jit(solution)/shard_map/ppermute | solution.py:1206
  61.9 16.6 %collective-permute-start.13 = (bf16[8,12,48,128]{3,2,1,0:T(8,128)(2,1)S(1)}, bf16[8,12,48,128]{3,2,1,0:T(8,128)(2,1)}, u32[]{:S(2)}, u32[]{:S(2)}) collective-permute-start(bf16[8,12,48,128]{3,2,1,0:T(8,128)(2,1)S(1)} %collective-permute-done.11.rest_1_.rest_9_), channel_id=1, source_target_pairs={{0,1},{1,0},{2,3},{3,2},{4,5},{5,4},{6,7},{7,6},{8,9},{9,8},{10,11... | collective-permute-start | bytes 3538952 | tf_op jit(solution)/shard_map/ppermute | solution.py:1116
  78.5 25.0 %collective-permute-start.19 = (bf16[4,2,96,768]{3,2,1,0:T(8,128)(2,1)}, bf16[4,2,96,768]{3,2,1,0:T(8,128)(2,1)}, u32[]{:S(2)}, u32[]{:S(2)}) collective-permute-start(bf16[4,2,96,768]{3,2,1,0:T(8,128)(2,1)} %pad_maximum_fusion.1.rest_0_), channel_id=1, source_target_pairs={{0,4},{1,3},{2,6},{3,1},{4,0},{5,7},{6,2},{7,5},{8,12},{9,11},{10,... | collective-permute-start | bytes 3538952 | tf_op jit(solution)/shard_map/ppermute | solution.py:1132
  79.9 27.8 %collective-permute-start.20 = (bf16[4,2,96,768]{3,2,1,0:T(8,128)(2,1)}, bf16[4,2,96,768]{3,2,1,0:T(8,128)(2,1)}, u32[]{:S(2)}, u32[]{:S(2)}) collective-permute-start(bf16[4,2,96,768]{3,2,1,0:T(8,128)(2,1)} %collective-permute-done.16.rest_1_), channel_id=1, source_target_pairs={{0,4},{1,3},{2,6},{3,1},{4,0},{5,7},{6,2},{7,5},{8,12},{9,11},{10,... | collective-permute-start | bytes 3538952 | tf_op jit(solution)/shard_map/ppermute | solution.py:1132
  80.5 27.6 %collective-permute-start.17 = (bf16[4,2,96,768]{3,2,1,0:T(8,128)(2,1)}, bf16[4,2,96,768]{3,2,1,0:T(8,128)(2,1)}, u32[]{:S(2)}, u32[]{:S(2)}) collective-permute-start(bf16[4,2,96,768]{3,2,1,0:T(8,128)(2,1)} %pad_maximum_fusion.1.rest_0_), channel_id=1, source_target_pairs={{0,1},{1,0},{2,3},{3,2},{4,5},{5,4},{6,7},{7,6},{8,9},{9,8},{10,11... | collective-permute-start | bytes 3538952 | tf_op jit(solution)/shard_map/ppermute | solution.py:1116
  80.5 27.6 %collective-permute-start.18 = (bf16[4,2,96,768]{3,2,1,0:T(8,128)(2,1)}, bf16[4,2,96,768]{3,2,1,0:T(8,128)(2,1)}, u32[]{:S(2)}, u32[]{:S(2)}) collective-permute-start(bf16[4,2,96,768]{3,2,1,0:T(8,128)(2,1)} %collective-permute-done.16.rest_1_), channel_id=1, source_target_pairs={{0,1},{1,0},{2,3},{3,2},{4,5},{5,4},{6,7},{7,6},{8,9},{9,8},{10,11... | collective-permute-start | bytes 3538952 | tf_op jit(solution)/shard_map/ppermute | solution.py:1116
  168.4 19.5 %collective-permute-start.24 = (bf16[5,2,96,768]{3,2,1,0:T(8,128)(2,1)S(1)}, bf16[5,2,96,768]{3,2,1,0:T(8,128)(2,1)}, u32[]{:S(2)}, u32[]{:S(2)}) collective-permute-start(bf16[5,2,96,768]{3,2,1,0:T(8,128)(2,1)S(1)} %add_convert_fusion), channel_id=1, source_target_pairs={{0,4},{1,3},{2,6},{3,1},{4,0},{5,7},{6,2},{7,5},{8,12},{9,11},{10,... | collective-permute-start | bytes 4423688 | tf_op jit(solution)/shard_map/ppermute | solution.py:1132
  188.0 13.3 %collective-permute-start.25 = (bf16[3,2,96,768]{3,2,1,0:T(8,128)(2,1)}, bf16[3,2,96,768]{3,2,1,0:T(8,128)(2,1)S(1)}, u32[]{:S(2)}, u32[]{:S(2)}) collective-permute-start(bf16[3,2,96,768]{3,2,1,0:T(8,128)(2,1)} %add_convert_fusion.3), channel_id=1, source_target_pairs={{0,4},{1,3},{2,6},{3,1},{4,0},{5,7},{6,2},{7,5},{8,12},{9,11},{10,... | collective-permute-start | bytes 2654216 | tf_op jit(solution)/shard_map/ppermute | solution.py:1132
  210.3 17.9 %collective-permute-start.28 = (bf16[4,2,96,768]{3,2,1,0:T(8,128)(2,1)S(1)}, bf16[4,2,96,768]{3,2,1,0:T(8,128)(2,1)}, u32[]{:S(2)}, u32[]{:S(2)}) collective-permute-start(bf16[4,2,96,768]{3,2,1,0:T(8,128)(2,1)S(1)} %add_convert_fusion.1), channel_id=1, source_target_pairs={{0,2},{1,5},{2,0},{3,7},{4,6},{5,1},{6,4},{7,3},{8,10},{9,13},{10,... | collective-permute-start | bytes 3538952 | tf_op jit(solution)/shard_map/ppermute | solution.py:1298
  227.1 23.0 %collective-permute-start.31 = (bf16[8,9,48,128]{3,2,1,0:T(8,128)(2,1)}, bf16[8,9,48,128]{3,2,1,0:T(8,128)(2,1)}, u32[]{:S(2)}, u32[]{:S(2)}) collective-permute-start(bf16[8,9,48,128]{3,2,1,0:T(8,128)(2,1)} %get-tuple-element.240), channel_id=1, source_target_pairs={{0,1},{1,0},{2,3},{3,2},{4,5},{5,4},{6,7},{7,6},{8,9},{9,8},{10,11... | collective-permute-start | bytes 2654216 | tf_op jit(solution)/shard_map/ppermute | solution.py:1116
  228.1 22.0 %collective-permute-start.32 = (bf16[8,9,48,128]{3,2,1,0:T(8,128)(2,1)}, bf16[8,9,48,128]{3,2,1,0:T(8,128)(2,1)}, u32[]{:S(2)}, u32[]{:S(2)}) collective-permute-start(bf16[8,9,48,128]{3,2,1,0:T(8,128)(2,1)} %get-tuple-element.241), channel_id=1, source_target_pairs={{0,1},{1,0},{2,3},{3,2},{4,5},{5,4},{6,7},{7,6},{8,9},{9,8},{10,11... | collective-permute-start | bytes 2654216 | tf_op jit(solution)/shard_map/ppermute | solution.py:1116
  231.2 19.0 %collective-permute-start.30 = (bf16[2,96,768]{2,1,0:T(8,128)(2,1)}, bf16[2,96,768]{2,1,0:T(8,128)(2,1)}, u32[]{:S(2)}, u32[]{:S(2)}) collective-permute-start(bf16[2,96,768]{2,1,0:T(8,128)(2,1)} %get-tuple-element.239), channel_id=1, source_target_pairs={{0,16},{1,17},{2,18},{3,19},{4,20},{5,21},{6,22},{7,23},{8,24},{9,... | collective-permute-start | bytes 884744 | tf_op jit(solution)/shard_map/ppermute | solution.py:1120
  231.5 25.7 %collective-permute-start.26 = (bf16[2,256,768]{2,1,0:T(8,128)(2,1)}, bf16[2,256,768]{2,1,0:T(8,128)(2,1)}, u32[]{:S(2)}, u32[]{:S(2)}) collective-permute-start(bf16[2,256,768]{2,1,0:T(8,128)(2,1)} %get-tuple-element.214), channel_id=1, source_target_pairs={{0,1},{1,0},{2,3},{3,2},{4,5},{5,4},{6,7},{7,6},{8,9},{9,8},{10,11... | collective-permute-start | bytes 2359304 | tf_op jit(solution)/shard_map/ppermute | solution.py:1116
  252.1 18.1 %collective-permute-start.33 = (bf16[8,9,48,128]{3,2,1,0:T(8,128)(2,1)S(1)}, bf16[8,9,48,128]{3,2,1,0:T(8,128)(2,1)S(1)}, u32[]{:S(2)}, u32[]{:S(2)}) collective-permute-start(bf16[8,9,48,128]{3,2,1,0:T(8,128)(2,1)S(1)} %add_convert_fusion.2), channel_id=1, source_target_pairs={{0,4},{1,3},{2,6},{3,1},{4,0},{5,7},{6,2},{7,5},{8,12},{9,11},{10,... | collective-permute-start | bytes 2654216 | tf_op jit(solution)/shard_map/ppermute | solution.py:1132
  254.9 15.3 %collective-permute-start.38 = (bf16[2,96,768]{2,1,0:T(8,128)(2,1)S(1)}, bf16[2,96,768]{2,1,0:T(8,128)(2,1)S(1)}, u32[]{:S(2)}, u32[]{:S(2)}) collective-permute-start(bf16[2,96,768]{2,1,0:T(8,128)(2,1)S(1)} %get-tuple-element.254), channel_id=1, source_target_pairs={{0,24},{1,25},{2,26},{3,27},{4,28},{5,29},{6,30},{7,31},{8,16},{9,... | collective-permute-start | bytes 884744 | tf_op jit(solution)/shard_map/ppermute | solution.py:1120
  257.0 13.2 %collective-permute-start.36 = (bf16[8,4,48,128]{3,2,1,0:T(8,128)(2,1)S(1)}, bf16[8,4,48,128]{3,2,1,0:T(8,128)(2,1)S(1)}, u32[]{:S(2)}, u32[]{:S(2)}) collective-permute-start(bf16[8,4,48,128]{3,2,1,0:T(8,128)(2,1)S(1)} %copy-done.29), channel_id=1, source_target_pairs={{0,1},{1,0},{2,3},{3,2},{4,5},{5,4},{6,7},{7,6},{8,9},{9,8},{10,11... | collective-permute-start | bytes 1179656 | tf_op jit(solution)/shard_map/ppermute | solution.py:1116
  274.9 24.0 %collective-permute-start.44 = (f32[2,96,768]{2,1,0:T(8,128)S(1)}, f32[2,96,768]{2,1,0:T(8,128)S(1)}, u32[]{:S(2)}, u32[]{:S(2)}) collective-permute-start(f32[2,96,768]{2,1,0:T(8,128)S(1)} %bitcast_add_fusion), channel_id=1, source_target_pairs={{0,1},{1,0},{2,3},{3,2},{4,5},{5,4},{6,7},{7,6},{8,9},{9,8},{10,11... | collective-permute-start | bytes 1769480 | tf_op jit(solution)/shard_map/ppermute | solution.py:1116
  (51 other events, 421.1 us)
